TPU v7x, 128 devices: a whole 4x4x4 slice. The times are simulated.
128 devices in a mesh: tm: 4 (over x), space: 32 (over z, y, core).
Axes of the slice: x: 4, y: 4, z: 4, core: 2. Of those that a mesh axis runs over, the one named last changes fastest.
Arguments:
- source: float32 [32, 2048, 1024], P('tm', 'space'), may hold values from -6 to 6
- guess: float32 [32, 2048, 1024], P('tm', 'space'), may hold values from -6 to 6
- start_state: float32 [2048, 1024], P('space'), may hold values from -6 to 6
- conduct: float32 [2048, 1024], P('space'), may hold values from 0.5 to 4
Outputs:
- solution_field: float32 [32, 2048, 1024], P('tm', 'space')
- residual: float32 [32, 2048, 1024], P('tm', 'space')
All inputs are finite; a program needn't handle non-finite values.
Results may differ from a plain program's by a relative error of at most 0.00002.
Values sent between devices are 32-bit elements; how exact they have to be, the bound alone decides.
No kernel may reach another device: no remote copies, remote signals or barrier semaphores. Data moves between devices by JAX's collectives and lax.ppermute only.
A program may use at most 64 MiB of HBM per device.

v0:
```python
import jax
import jax.numpy as jnp
from jax import lax
from jax.sharding import PartitionSpec as P

damping = 0.8


def extended(cells, sides, width):
    for axis, dim in sides:
        count = lax.axis_size(axis)
        ends = count - 1
        head = lax.slice_in_dim(cells, 0, width, axis=dim)
        tail = lax.slice_in_dim(cells, cells.shape[dim] - width, cells.shape[dim], axis=dim)
        cells = jnp.concatenate(
            [
                lax.ppermute(tail, axis, [(i, (i + 1) % count) for i in range(ends)]),
                cells,
                lax.ppermute(head, axis, [((i + 1) % count, i) for i in range(ends)]),
            ],
            axis=dim,
        )
    return cells


def passed_along(block, axis, distance):
    devices = range(lax.axis_size(axis))
    route = [(i - distance, i) for i in devices if i - distance in devices]
    return lax.ppermute(block, axis, route)


def apply_operator(field, conduct):
    rimmed = extended(field, (("space", 1),), 1)
    padded = jnp.pad(rimmed, ((0, 0), (0, 0), (1, 1)))
    beside = padded[:, 2:, 1:-1] + padded[:, :-2, 1:-1] + padded[:, 1:-1, 2:] + padded[:, 1:-1, :-2]
    return field + conduct * (4.0 * field - beside)


def approx_inverse(resid, conduct):
    diagonal = 1.0 + 4.0 * conduct
    first_sweep = resid / diagonal
    return first_sweep + (resid - apply_operator(first_sweep, conduct)) / diagonal


def fine_residual(field, before, source, conduct):
    earlier = jnp.concatenate([before[None], field[:-1]], axis=0)
    return source + earlier - apply_operator(field, conduct)


def coarse_before(coarse):
    boundary = passed_along(coarse[-1], "tm", 1)
    return jnp.concatenate([boundary[None], coarse[:-1]], axis=0)


def apply_inner(widened, cond_wide):
    padded = jnp.pad(widened, ((0, 0), (0, 0), (1, 1)))
    centre = widened[:, 1:-1]
    beside = widened[:, 2:] + widened[:, :-2] + padded[:, 1:-1, 2:] + padded[:, 1:-1, :-2]
    return centre + cond_wide[1:-1] * (4.0 * centre - beside)


def widened_smooth(field, earlier, rhs, cond_wide, inside_mask):
    stacked = jnp.stack([field, earlier, rhs], axis=0)
    widened = extended(stacked, (("space", 2),), 2)
    resid_wide = widened[2][:, 1:-1] + widened[1][:, 1:-1] - apply_inner(widened[0], cond_wide)
    resid_wide = resid_wide * inside_mask
    cond_mid = cond_wide[1:-1]
    diagonal = 1.0 + 4.0 * cond_mid
    first_sweep = resid_wide / diagonal
    image = apply_inner(first_sweep, cond_mid)
    return first_sweep[:, 1:-1] + (resid_wide[:, 1:-1] - image) / diagonal[1:-1]


def shards(source, guess, start_state, conduct):
    is_first = lax.axis_index("tm") == 0

    def fine_before(field):
        boundary = passed_along(field[-1], "tm", 1)
        return jnp.where(is_first, start_state, boundary)

    half_steps = source.shape[0] // 2
    coarse_cond = 2.0 * conduct
    before0 = fine_before(guess)
    local_rows = conduct.shape[0]
    cond_wide = extended(conduct, (("space", 0),), 2)
    coarse_wide = 2.0 * cond_wide
    row_index = jnp.arange(local_rows + 2) + lax.axis_index("space") * local_rows - 1
    inside = (row_index >= 0) & (row_index < local_rows * lax.axis_size("space"))
    inside_mask = inside.astype(jnp.float32)[:, None]
    earlier0 = jnp.concatenate([before0[None], guess[:-1]], axis=0)
    smooth1 = guess + damping * widened_smooth(guess, earlier0, source, cond_wide, inside_mask)
    before1 = fine_before(smooth1)
    resid1 = fine_residual(smooth1, before1, source, conduct)
    pairs = resid1.reshape(half_steps, 2, source.shape[1], source.shape[2])
    restricted = pairs[:, 0] + pairs[:, 1]
    correction = damping * approx_inverse(restricted, coarse_cond)
    for sweep in range(2):
        earlier_coarse = coarse_before(correction)
        correction = correction + damping * widened_smooth(
            correction, earlier_coarse, restricted, coarse_wide, inside_mask
        )
    shifted_final = coarse_before(correction)
    even_steps = 0.5 * (shifted_final + correction)
    fine_corr = jnp.stack([even_steps, correction], axis=1).reshape(source.shape)
    smooth2 = smooth1 + fine_corr
    before2 = before1 + shifted_final[0]
    earlier2 = jnp.concatenate([before2[None], smooth2[:-1]], axis=0)
    smooth3 = smooth2 + damping * widened_smooth(smooth2, earlier2, source, cond_wide, inside_mask)
    before3 = fine_before(smooth3)
    resid3 = fine_residual(smooth3, before3, source, conduct)
    return (smooth3, resid3)


def solution(mesh):
    return jax.shard_map(
        shards,
        mesh=mesh,
        in_specs=(
            P("tm", "space", None),
            P("tm", "space", None),
            P("space", None),
            P("space", None),
        ),
        out_specs=(P("tm", "space", None), P("tm", "space", None)),
        check_vma=False,
    )
```

profile of v0, /device:TPU:30, one launch (start us, length us, event | category | flops | bytes accessed | tf_op | source)
XLA Modules:
  0.0 162.2 jit_solution(4502473798915692248)
XLA Ops:
  0.6 0.8 fusion.105
  1.4 1.9 %collective-permute-start.3 = (f32[2,1024]{1,0:T(2,128)S(1)}, f32[2,1024]{1,0:T(2,128)S(1)}, u32[]{:S(2)}, u32[]{:S(2)}) collective-permute-start(f32[2,1024]{1,0:T(2,128)S(1)} %get-tuple-element.44), channel_id=1, source_target_pairs={{0,1},{1,2},{2,3},{3,4},{4,5},{5,6},{6,7},{7,8},{8,9},{9,10},{10,1... | collective-permute-start | bytes 24584 | tf_op jit(solution)/shard_map/ppermute | solution.py:17
  3.3 3.6 %collective-permute-start.4 = (f32[2,1024]{1,0:T(2,128)S(1)}, f32[2,1024]{1,0:T(2,128)S(1)}, u32[]{:S(2)}, u32[]{:S(2)}) collective-permute-start(f32[2,1024]{1,0:T(2,128)S(1)} %get-tuple-element.45), channel_id=1, source_target_pairs={{1,0},{2,1},{3,2},{4,3},{5,4},{6,5},{7,6},{8,7},{9,8},{10,9},{11,1... | collective-permute-start | bytes 24584 | tf_op jit(solution)/shard_map/ppermute | solution.py:19
  7.0 1.0 slice_bitcast_fusion.17
  8.0 1.4 collective-permute-start
  9.4 1.0 broadcast_multiply_fusion.1
  10.5 7.6 %collective-permute-done = f32[64,1024]{1,0:T(8,128)S(1)} collective-permute-done((f32[64,1024]{1,0:T(8,128)S(1)}, f32[64,1024]{1,0:T(8,128)S(1)}, u32[]{:S(2)}, u32[]{:S(2)}) %collective-permute-start) | collective-permute-done | bytes 262176 | tf_op jit(solution)/shard_map/ppermute | solution.py:29
  18.5 1.3 copy-done
  19.8 0.6 copy-done.2
  20.4 1.1 pad_maximum_fusion.3
  21.7 1.9 %collective-permute-start.1 = (f32[3,8,2,1024]{3,2,1,0:T(2,128)S(1)}, f32[3,8,2,1024]{3,2,1,0:T(2,128)S(1)}, u32[]{:S(2)}, u32[]{:S(2)}) collective-permute-start(f32[3,8,2,1024]{3,2,1,0:T(2,128)S(1)} %get-tuple-element.18), channel_id=1, source_target_pairs={{0,1},{1,2},{2,3},{3,4},{4,5},{5,6},{6,7},{7,8},{8,9},{9,10},{10,1... | collective-permute-start | bytes 589832 | tf_op jit(solution)/shard_map/ppermute | solution.py:17
  23.7 3.6 %collective-permute-start.2 = (f32[3,8,2,1024]{3,2,1,0:T(2,128)S(1)}, f32[3,8,2,1024]{3,2,1,0:T(2,128)S(1)}, u32[]{:S(2)}, u32[]{:S(2)}) collective-permute-start(f32[3,8,2,1024]{3,2,1,0:T(2,128)S(1)} %get-tuple-element.19), channel_id=1, source_target_pairs={{1,0},{2,1},{3,2},{4,3},{5,4},{6,5},{7,6},{8,7},{9,8},{10,9},{11,1... | collective-permute-start | bytes 589832 | tf_op jit(solution)/shard_map/ppermute | solution.py:19
  27.4 1.3 collective-permute-done.1
  28.7 1.8 %collective-permute-done.2 = f32[3,8,2,1024]{3,2,1,0:T(2,128)S(1)} collective-permute-done((f32[3,8,2,1024]{3,2,1,0:T(2,128)S(1)}, f32[3,8,2,1024]{3,2,1,0:T(2,128)S(1)}, u32[]{:S(2)}, u32[]{:S(2)}) %collective-permute-start.2) | collective-permute-done | bytes 196640 | tf_op jit(solution)/shard_map/ppermute | solution.py:19
  30.5 1.7 %fusion.1 = f32[3,8,68,1024]{3,2,1,0:T(8,128)S(1)} fusion(f32[1,8,64,1024]{3,2,1,0:T(8,128)S(1)} %bitcast.74, f32[3,8,2,1024]{3,2,1,0:T(2,128)S(1)} %collective-permute-done.2, f32[1,8,64,1024]{3,2,1,0:T(8,128)S(1)} %maximum_bitcast_fusion, f32[1,8,64,1024]{3,2,1,0:T(8,128)S(1)} %bitcast.83, f32[3,8,2,1024]{3,2,1,0:T(2,128)S(1)} %collective-permute-done.1), kind=kLoop, calls=%fused_computation.5 | loop fusion | flops 6684672 | bytes 13369344 | tf_op jit(solution)/shard_map/concatenate | solution.py:15
  32.2 1.3 slice_bitcast_fusion.5
  33.5 2.5 %broadcast_divide_fusion.1 = (f32[8,66,1024]{2,1,0:T(8,128)S(1)}, f32[8,66,1024]{2,1,0:T(8,128)S(1)}) fusion(f32[66,1024]{1,0:T(8,128)S(1)} %get-tuple-element.39, f32[66]{0:T(128)S(1)} %and_convert_fusion, f32[8,68,1024]{2,1,0:T(8,128)S(1)} %get-tuple-element.14, f32[66,1024]{1,0:T(8,128)S(1)} %get-tuple-element.38, ...), kind=kLoop, calls=%fused_computation.137 | loop fusion | flops 5947392 | bytes 19071488 | tf_op jit(solution)/shard_map/div | solution.py:69
  36.0 2.2 %multiply_add_fusion.1 = f32[8,64,1024]{2,1,0:T(8,128)S(1)} fusion(f32[8,64,1024]{2,1,0:T(8,128)S(1)} %copy-done.2, f32[8,66,1024]{2,1,0:T(8,128)S(1)} %get-tuple-element.8, f32[8,66,1024]{2,1,0:T(8,128)S(1)} %get-tuple-element.9, f32[64,1024]{1,0:T(8,128)S(1)} %slice.492, f32[64,1024]{1,0:T(8,128)S(1)} %copy-done.3), kind=kLoop, calls=%fused_computation.98 | loop fusion | flops 6291456 | bytes 15466496 | tf_op jit(solution)/shard_map/add | solution.py:91
  38.3 6.2 %collective-permute-start.7 = (f32[8,1,1024]{2,1,0:T(1,128)S(1)}, f32[8,1,1024]{2,1,0:T(1,128)S(1)}, u32[]{:S(2)}, u32[]{:S(2)}) collective-permute-start(f32[8,1,1024]{2,1,0:T(1,128)S(1)} %get-tuple-element.32), channel_id=1, source_target_pairs={{0,1},{1,2},{2,3},{3,4},{4,5},{5,6},{6,7},{7,8},{8,9},{9,10},{10,1... | collective-permute-start | bytes 98312 | tf_op jit(solution)/shard_map/ppermute | solution.py:17
  44.4 1.9 %collective-permute-start.6 = (f32[8,1,1024]{2,1,0:T(1,128)S(1)}, f32[8,1,1024]{2,1,0:T(1,128)S(1)}, u32[]{:S(2)}, u32[]{:S(2)}) collective-permute-start(f32[8,1,1024]{2,1,0:T(1,128)S(1)} %get-tuple-element.33), channel_id=1, source_target_pairs={{1,0},{2,1},{3,2},{4,3},{5,4},{6,5},{7,6},{8,7},{9,8},{10,9},{11,1... | collective-permute-start | bytes 98312 | tf_op jit(solution)/shard_map/ppermute | solution.py:19
  46.5 1.3 collective-permute-start.5
  48.0 1.0 select_maximum_fusion.2
  49.0 8.2 %collective-permute-done.5 = f32[64,1024]{1,0:T(8,128)S(1)} collective-permute-done((f32[64,1024]{1,0:T(8,128)S(1)}, f32[64,1024]{1,0:T(8,128)S(1)}, u32[]{:S(2)}, u32[]{:S(2)}) %collective-permute-start.5) | collective-permute-done | bytes 262176 | tf_op jit(solution)/shard_map/ppermute | solution.py:29
  57.2 1.8 %fusion.47 = f32[8,64,1024]{2,1,0:T(8,128)S(1)} fusion(f32[8,64,1024]{2,1,0:T(8,128)S(1)} %multiply_add_fusion.1, f32[8,66,1026]{2,1,0:T(8,128)S(1)} %select_maximum_fusion.2, f32[8,1,1024]{2,1,0:T(1,128)S(1)} %collective-permute-done.7, f32[8,1,1024]{2,1,0:T(1,128)S(1)} %collective-permute-done.6, f32[8,64,1024]{2,1,0:T(8,128)S(1)} %copy-done, ...), kind=kLoop, calls=%fused_computation.85 | loop fusion | flops 6291456 | bytes 12910592 | tf_op jit(solution)/shard_map/sub | solution.py:47
  59.2 1.9 %collective-permute-start.9 = (f32[4,1,1024]{2,1,0:T(1,128)S(1)}, f32[4,1,1024]{2,1,0:T(1,128)S(1)}, u32[]{:S(2)}, u32[]{:S(2)}) collective-permute-start(f32[4,1,1024]{2,1,0:T(1,128)S(1)} %get-tuple-element.34), channel_id=1, source_target_pairs={{0,1},{1,2},{2,3},{3,4},{4,5},{5,6},{6,7},{7,8},{8,9},{9,10},{10,1... | collective-permute-start | bytes 49160 | tf_op jit(solution)/shard_map/ppermute | solution.py:17
  61.2 3.6 %collective-permute-start.8 = (f32[4,1,1024]{2,1,0:T(1,128)S(1)}, f32[4,1,1024]{2,1,0:T(1,128)S(1)}, u32[]{:S(2)}, u32[]{:S(2)}) collective-permute-start(f32[4,1,1024]{2,1,0:T(1,128)S(1)} %get-tuple-element.35), channel_id=1, source_target_pairs={{1,0},{2,1},{3,2},{4,3},{5,4},{6,5},{7,6},{8,7},{9,8},{10,9},{11,1... | collective-permute-start | bytes 49160 | tf_op jit(solution)/shard_map/ppermute | solution.py:19
  64.8 1.4 collective-permute-done.8
  66.3 0.5 select_maximum_fusion.4
  66.8 0.9 fusion.89
  67.7 1.3 collective-permute-start.10
  69.2 6.9 %collective-permute-done.10 = f32[64,1024]{1,0:T(8,128)S(1)} collective-permute-done((f32[64,1024]{1,0:T(8,128)S(1)}, f32[64,1024]{1,0:T(8,128)S(1)}, u32[]{:S(2)}, u32[]{:S(2)}) %collective-permute-start.10) | collective-permute-done | bytes 262176 | tf_op jit(solution)/shard_map/ppermute | solution.py:29
  76.2 0.3 pad_maximum_fusion.7
  76.7 4.4 %collective-permute-start.11 = (f32[3,4,2,1024]{3,2,1,0:T(2,128)S(1)}, f32[3,4,2,1024]{3,2,1,0:T(2,128)S(1)}, u32[]{:S(2)}, u32[]{:S(2)}) collective-permute-start(f32[3,4,2,1024]{3,2,1,0:T(2,128)S(1)} %get-tuple-element.28), channel_id=1, source_target_pairs={{0,1},{1,2},{2,3},{3,4},{4,5},{5,6},{6,7},{7,8},{8,9},{9,10},{10,1... | collective-permute-start | bytes 294920 | tf_op jit(solution)/shard_map/ppermute | solution.py:17
  81.0 2.1 %collective-permute-start.12 = (f32[3,4,2,1024]{3,2,1,0:T(2,128)S(1)}, f32[3,4,2,1024]{3,2,1,0:T(2,128)S(1)}, u32[]{:S(2)}, u32[]{:S(2)}) collective-permute-start(f32[3,4,2,1024]{3,2,1,0:T(2,128)S(1)} %get-tuple-element.29), channel_id=1, source_target_pairs={{1,0},{2,1},{3,2},{4,3},{5,4},{6,5},{7,6},{8,7},{9,8},{10,9},{11,1... | collective-permute-start | bytes 294920 | tf_op jit(solution)/shard_map/ppermute | solution.py:19
  83.3 1.9 %collective-permute-done.12 = f32[3,4,2,1024]{3,2,1,0:T(2,128)S(1)} collective-permute-done((f32[3,4,2,1024]{3,2,1,0:T(2,128)S(1)}, f32[3,4,2,1024]{3,2,1,0:T(2,128)S(1)}, u32[]{:S(2)}, u32[]{:S(2)}) %collective-permute-start.12) | collective-permute-done | bytes 98336 | tf_op jit(solution)/shard_map/ppermute | solution.py:19
  85.2 0.5 fusion.5
  85.7 0.4 slice_bitcast_fusion.11
  86.0 1.3 broadcast_divide_fusion.3
  87.3 1.0 multiply_add_fusion.3
  88.4 1.3 collective-permute-start.13
  89.7 6.9 %collective-permute-done.13 = f32[64,1024]{1,0:T(8,128)S(1)} collective-permute-done((f32[64,1024]{1,0:T(8,128)S(1)}, f32[64,1024]{1,0:T(8,128)S(1)}, u32[]{:S(2)}, u32[]{:S(2)}) %collective-permute-start.13) | collective-permute-done | bytes 262176 | tf_op jit(solution)/shard_map/ppermute | solution.py:29
  97.1 5.7 %collective-permute-start.14 = (f32[3,4,2,1024]{3,2,1,0:T(2,128)S(1)}, f32[3,4,2,1024]{3,2,1,0:T(2,128)S(1)}, u32[]{:S(2)}, u32[]{:S(2)}) collective-permute-start(f32[3,4,2,1024]{3,2,1,0:T(2,128)S(1)} %get-tuple-element.26), channel_id=1, source_target_pairs={{0,1},{1,2},{2,3},{3,4},{4,5},{5,6},{6,7},{7,8},{8,9},{9,10},{10,1... | collective-permute-start | bytes 294920 | tf_op jit(solution)/shard_map/ppermute | solution.py:17
  102.8 1.9 %collective-permute-start.15 = (f32[3,4,2,1024]{3,2,1,0:T(2,128)S(1)}, f32[3,4,2,1024]{3,2,1,0:T(2,128)S(1)}, u32[]{:S(2)}, u32[]{:S(2)}) collective-permute-start(f32[3,4,2,1024]{3,2,1,0:T(2,128)S(1)} %get-tuple-element.27), channel_id=1, source_target_pairs={{1,0},{2,1},{3,2},{4,3},{5,4},{6,5},{7,6},{8,7},{9,8},{10,9},{11,1... | collective-permute-start | bytes 294920 | tf_op jit(solution)/shard_map/ppermute | solution.py:19
  104.8 2.2 %collective-permute-done.15 = f32[3,4,2,1024]{3,2,1,0:T(2,128)S(1)} collective-permute-done((f32[3,4,2,1024]{3,2,1,0:T(2,128)S(1)}, f32[3,4,2,1024]{3,2,1,0:T(2,128)S(1)}, u32[]{:S(2)}, u32[]{:S(2)}) %collective-permute-start.15) | collective-permute-done | bytes 98336 | tf_op jit(solution)/shard_map/ppermute | solution.py:19
  107.0 0.5 fusion.7
  107.8 1.3 broadcast_divide_fusion.2
  109.0 1.1 multiply_add_fusion.2
  110.1 1.3 collective-permute-start.16
  111.5 6.9 %collective-permute-done.16 = f32[64,1024]{1,0:T(8,128)S(1)} collective-permute-done((f32[64,1024]{1,0:T(8,128)S(1)}, f32[64,1024]{1,0:T(8,128)S(1)}, u32[]{:S(2)}, u32[]{:S(2)}) %collective-permute-start.16) | collective-permute-done | bytes 262176 | tf_op jit(solution)/shard_map/ppermute | solution.py:29
  119.0 0.5 bitcast_add_fusion
  119.8 1.1 pad_maximum_fusion.2
  121.1 5.8 %collective-permute-start.17 = (f32[3,8,2,1024]{3,2,1,0:T(2,128)S(1)}, f32[3,8,2,1024]{3,2,1,0:T(2,128)S(1)}, u32[]{:S(2)}, u32[]{:S(2)}) collective-permute-start(f32[3,8,2,1024]{3,2,1,0:T(2,128)S(1)} %get-tuple-element.16), channel_id=1, source_target_pairs={{0,1},{1,2},{2,3},{3,4},{4,5},{5,6},{6,7},{7,8},{8,9},{9,10},{10,1... | collective-permute-start | bytes 589832 | tf_op jit(solution)/shard_map/ppermute | solution.py:17
  126.8 2.1 %collective-permute-start.18 = (f32[3,8,2,1024]{3,2,1,0:T(2,128)S(1)}, f32[3,8,2,1024]{3,2,1,0:T(2,128)S(1)}, u32[]{:S(2)}, u32[]{:S(2)}) collective-permute-start(f32[3,8,2,1024]{3,2,1,0:T(2,128)S(1)} %get-tuple-element.17), channel_id=1, source_target_pairs={{1,0},{2,1},{3,2},{4,3},{5,4},{6,5},{7,6},{8,7},{9,8},{10,9},{11,1... | collective-permute-start | bytes 589832 | tf_op jit(solution)/shard_map/ppermute | solution.py:19
  129.0 2.9 %collective-permute-done.18 = f32[3,8,2,1024]{3,2,1,0:T(2,128)S(1)} collective-permute-done((f32[3,8,2,1024]{3,2,1,0:T(2,128)S(1)}, f32[3,8,2,1024]{3,2,1,0:T(2,128)S(1)}, u32[]{:S(2)}, u32[]{:S(2)}) %collective-permute-start.18) | collective-permute-done | bytes 196640 | tf_op jit(solution)/shard_map/ppermute | solution.py:19
  131.9 1.7 %fusion.3 = f32[3,8,68,1024]{3,2,1,0:T(8,128)S(1)} fusion(f32[1,8,64,1024]{3,2,1,0:T(8,128)S(1)} %bitcast.76, f32[3,8,2,1024]{3,2,1,0:T(2,128)S(1)} %collective-permute-done.18, f32[1,8,64,1024]{3,2,1,0:T(8,128)S(1)} %maximum_bitcast_fusion.1, f32[1,8,64,1024]{3,2,1,0:T(8,128)S(1)} %bitcast.78, f32[3,8,2,1024]{3,2,1,0:T(2,128)S(1)} %collective-permute-done.17), kind=kLoop, calls=%fused_computation.7 | loop fusion | flops 6684672 | bytes 13369344 | tf_op jit(solution)/shard_map/concatenate | solution.py:15
  133.6 1.3 slice_bitcast_fusion.2
  135.0 2.5 %broadcast_divide_fusion = (f32[8,66,1024]{2,1,0:T(8,128)S(1)}, f32[8,66,1024]{2,1,0:T(8,128)S(1)}) fusion(f32[66,1024]{1,0:T(8,128)S(1)} %get-tuple-element.39, f32[66]{0:T(128)S(1)} %and_convert_fusion, f32[8,68,1024]{2,1,0:T(8,128)S(1)} %get-tuple-element.11, f32[66,1024]{1,0:T(8,128)S(1)} %get-tuple-element.38, ...), kind=kLoop, calls=%fused_computation.136 | loop fusion | flops 5947392 | bytes 19071488 | tf_op jit(solution)/shard_map/div | solution.py:69
  137.5 2.2 %multiply_add_fusion = f32[8,64,1024]{2,1,0:T(8,128)S(1)} fusion(f32[8,64,1024]{2,1,0:T(8,128)S(1)} %bitcast_add_fusion, f32[8,66,1024]{2,1,0:T(8,128)S(1)} %get-tuple-element.2, f32[8,66,1024]{2,1,0:T(8,128)S(1)} %get-tuple-element.3, f32[64,1024]{1,0:T(8,128)S(1)} %slice.492, f32[64,1024]{1,0:T(8,128)S(1)} %copy-done.3), kind=kLoop, calls=%fused_computation.97 | loop fusion | flops 6291456 | bytes 15466496 | tf_op jit(solution)/shard_map/add | solution.py:108
  139.7 7.0 %collective-permute-start.21 = (f32[8,1,1024]{2,1,0:T(1,128)S(1)}, f32[8,1,1024]{2,1,0:T(1,128)S(1)}, u32[]{:S(2)}, u32[]{:S(2)}) collective-permute-start(f32[8,1,1024]{2,1,0:T(1,128)S(1)} %get-tuple-element.30), channel_id=1, source_target_pairs={{0,1},{1,2},{2,3},{3,4},{4,5},{5,6},{6,7},{7,8},{8,9},{9,10},{10,1... | collective-permute-start | bytes 98312 | tf_op jit(solution)/shard_map/ppermute | solution.py:17
  146.7 1.9 %collective-permute-start.20 = (f32[8,1,1024]{2,1,0:T(1,128)S(1)}, f32[8,1,1024]{2,1,0:T(1,128)S(1)}, u32[]{:S(2)}, u32[]{:S(2)}) collective-permute-start(f32[8,1,1024]{2,1,0:T(1,128)S(1)} %get-tuple-element.31), channel_id=1, source_target_pairs={{1,0},{2,1},{3,2},{4,3},{5,4},{6,5},{7,6},{8,7},{9,8},{10,9},{11,1... | collective-permute-start | bytes 98312 | tf_op jit(solution)/shard_map/ppermute | solution.py:19
  148.8 1.3 collective-permute-start.19
  150.2 1.0 select_maximum_fusion
  151.2 8.2 %collective-permute-done.19 = f32[64,1024]{1,0:T(8,128)S(1)} collective-permute-done((f32[64,1024]{1,0:T(8,128)S(1)}, f32[64,1024]{1,0:T(8,128)S(1)}, u32[]{:S(2)}, u32[]{:S(2)}) %collective-permute-start.19) | collective-permute-done | bytes 262176 | tf_op jit(solution)/shard_map/ppermute | solution.py:29
  159.4 2.7 %fusion.42 = f32[8,64,1024]{2,1,0:T(8,128)} fusion(f32[8,64,1024]{2,1,0:T(8,128)S(1)} %multiply_add_fusion, f32[8,66,1026]{2,1,0:T(8,128)S(1)} %select_maximum_fusion, f32[8,1,1024]{2,1,0:T(1,128)S(1)} %collective-permute-done.21, f32[8,1,1024]{2,1,0:T(1,128)S(1)} %collective-permute-done.20, f32[8,64,1024]{2,1,0:T(8,128)S(1)} %copy-done, ...), kind=kLoop, calls=%fused_computation.75 | loop fusion | flops 6291456 | bytes 12910592 | tf_op jit(solution)/shard_map/sub | solution.py:47
  (60 shorter events, 4.0 us)
Async XLA Ops:
  1.4 9.0 %collective-permute-start.3 = (f32[2,1024]{1,0:T(2,128)S(1)}, f32[2,1024]{1,0:T(2,128)S(1)}, u32[]{:S(2)}, u32[]{:S(2)}) collective-permute-start(f32[2,1024]{1,0:T(2,128)S(1)} %get-tuple-element.44), channel_id=1, source_target_pairs={{0,1},{1,2},{2,3},{3,4},{4,5},{5,6},{6,7},{7,8},{8,9},{9,10},{10,1... | collective-permute-start | bytes 24584 | tf_op jit(solution)/shard_map/ppermute | solution.py:17
  3.3 7.1 %collective-permute-start.4 = (f32[2,1024]{1,0:T(2,128)S(1)}, f32[2,1024]{1,0:T(2,128)S(1)}, u32[]{:S(2)}, u32[]{:S(2)}) collective-permute-start(f32[2,1024]{1,0:T(2,128)S(1)} %get-tuple-element.45), channel_id=1, source_target_pairs={{1,0},{2,1},{3,2},{4,3},{5,4},{6,5},{7,6},{8,7},{9,8},{10,9},{11,1... | collective-permute-start | bytes 24584 | tf_op jit(solution)/shard_map/ppermute | solution.py:19
  8.0 2.5 %copy-start.3 = (f32[64,1024]{1,0:T(8,128)S(1)}, f32[64,1024]{1,0:T(8,128)}, u32[]{:S(2)}) copy-start(f32[64,1024]{1,0:T(8,128)} %param.7) | copy-start | bytes 786436
  8.0 10.2 %collective-permute-start = (f32[64,1024]{1,0:T(8,128)S(1)}, f32[64,1024]{1,0:T(8,128)S(1)}, u32[]{:S(2)}, u32[]{:S(2)}) collective-permute-start(f32[64,1024]{1,0:T(8,128)S(1)} %slice_bitcast_fusion.17), channel_id=1, source_target_pairs={{0,32},{32,64},{64,96},{1,33},{33,65},{65,97},{2,34},{34,66},{66,9... | collective-permute-start | bytes 786440 | tf_op jit(solution)/shard_map/ppermute | solution.py:29
  10.4 7.7 %copy-start.4 = (f32[64,1024]{1,0:T(8,128)S(1)}, f32[64,1024]{1,0:T(8,128)}, u32[]{:S(2)}) copy-start(f32[64,1024]{1,0:T(8,128)} %param.6) | copy-start | bytes 786436
  10.4 7.8 %slice-start = ((f32[8,64,1024]{2,1,0:T(8,128)}), f32[7,64,1024]{2,1,0:T(8,128)S(1)}, s32[]{:S(2)}) async-start(f32[8,64,1024]{2,1,0:T(8,128)} %param.5), calls=%async_computation | async-start | bytes 3670016 | tf_op jit(solution)/shard_map/slice | solution.py:90
  18.2 1.6 copy-start
  18.2 2.2 %copy-start.2 = (f32[8,64,1024]{2,1,0:T(8,128)S(1)}, f32[8,64,1024]{2,1,0:T(8,128)}, u32[]{:S(2)}) copy-start(f32[8,64,1024]{2,1,0:T(8,128)} %param.5) | copy-start | bytes 6291460
  21.7 7.0 %collective-permute-start.1 = (f32[3,8,2,1024]{3,2,1,0:T(2,128)S(1)}, f32[3,8,2,1024]{3,2,1,0:T(2,128)S(1)}, u32[]{:S(2)}, u32[]{:S(2)}) collective-permute-start(f32[3,8,2,1024]{3,2,1,0:T(2,128)S(1)} %get-tuple-element.18), channel_id=1, source_target_pairs={{0,1},{1,2},{2,3},{3,4},{4,5},{5,6},{6,7},{7,8},{8,9},{9,10},{10,1... | collective-permute-start | bytes 589832 | tf_op jit(solution)/shard_map/ppermute | solution.py:17
  23.7 6.8 %collective-permute-start.2 = (f32[3,8,2,1024]{3,2,1,0:T(2,128)S(1)}, f32[3,8,2,1024]{3,2,1,0:T(2,128)S(1)}, u32[]{:S(2)}, u32[]{:S(2)}) collective-permute-start(f32[3,8,2,1024]{3,2,1,0:T(2,128)S(1)} %get-tuple-element.19), channel_id=1, source_target_pairs={{1,0},{2,1},{3,2},{4,3},{5,4},{6,5},{7,6},{8,7},{9,8},{10,9},{11,1... | collective-permute-start | bytes 589832 | tf_op jit(solution)/shard_map/ppermute | solution.py:19
  38.3 9.6 %collective-permute-start.7 = (f32[8,1,1024]{2,1,0:T(1,128)S(1)}, f32[8,1,1024]{2,1,0:T(1,128)S(1)}, u32[]{:S(2)}, u32[]{:S(2)}) collective-permute-start(f32[8,1,1024]{2,1,0:T(1,128)S(1)} %get-tuple-element.32), channel_id=1, source_target_pairs={{0,1},{1,2},{2,3},{3,4},{4,5},{5,6},{6,7},{7,8},{8,9},{9,10},{10,1... | collective-permute-start | bytes 98312 | tf_op jit(solution)/shard_map/ppermute | solution.py:17
  44.4 3.5 %collective-permute-start.6 = (f32[8,1,1024]{2,1,0:T(1,128)S(1)}, f32[8,1,1024]{2,1,0:T(1,128)S(1)}, u32[]{:S(2)}, u32[]{:S(2)}) collective-permute-start(f32[8,1,1024]{2,1,0:T(1,128)S(1)} %get-tuple-element.33), channel_id=1, source_target_pairs={{1,0},{2,1},{3,2},{4,3},{5,4},{6,5},{7,6},{8,7},{9,8},{10,9},{11,1... | collective-permute-start | bytes 98312 | tf_op jit(solution)/shard_map/ppermute | solution.py:19
  46.5 10.6 %collective-permute-start.5 = (f32[64,1024]{1,0:T(8,128)S(1)}, f32[64,1024]{1,0:T(8,128)S(1)}, u32[]{:S(2)}, u32[]{:S(2)}) collective-permute-start(f32[64,1024]{1,0:T(8,128)S(1)} %slice_bitcast_fusion.16), channel_id=1, source_target_pairs={{0,32},{32,64},{64,96},{1,33},{33,65},{65,97},{2,34},{34,66},{66,9... | collective-permute-start | bytes 786440 | tf_op jit(solution)/shard_map/ppermute | solution.py:29
  59.2 5.6 %collective-permute-start.9 = (f32[4,1,1024]{2,1,0:T(1,128)S(1)}, f32[4,1,1024]{2,1,0:T(1,128)S(1)}, u32[]{:S(2)}, u32[]{:S(2)}) collective-permute-start(f32[4,1,1024]{2,1,0:T(1,128)S(1)} %get-tuple-element.34), channel_id=1, source_target_pairs={{0,1},{1,2},{2,3},{3,4},{4,5},{5,6},{6,7},{7,8},{8,9},{9,10},{10,1... | collective-permute-start | bytes 49160 | tf_op jit(solution)/shard_map/ppermute | solution.py:17
  61.2 5.1 %collective-permute-start.8 = (f32[4,1,1024]{2,1,0:T(1,128)S(1)}, f32[4,1,1024]{2,1,0:T(1,128)S(1)}, u32[]{:S(2)}, u32[]{:S(2)}) collective-permute-start(f32[4,1,1024]{2,1,0:T(1,128)S(1)} %get-tuple-element.35), channel_id=1, source_target_pairs={{1,0},{2,1},{3,2},{4,3},{5,4},{6,5},{7,6},{8,7},{9,8},{10,9},{11,1... | collective-permute-start | bytes 49160 | tf_op jit(solution)/shard_map/ppermute | solution.py:19
  67.7 8.4 %collective-permute-start.10 = (f32[64,1024]{1,0:T(8,128)S(1)}, f32[64,1024]{1,0:T(8,128)S(1)}, u32[]{:S(2)}, u32[]{:S(2)}) collective-permute-start(f32[64,1024]{1,0:T(8,128)S(1)} %slice_bitcast_fusion.15), channel_id=1, source_target_pairs={{0,32},{32,64},{64,96},{1,33},{33,65},{65,97},{2,34},{34,66},{66,9... | collective-permute-start | bytes 786440 | tf_op jit(solution)/shard_map/ppermute | solution.py:29
  76.7 6.6 %collective-permute-start.11 = (f32[3,4,2,1024]{3,2,1,0:T(2,128)S(1)}, f32[3,4,2,1024]{3,2,1,0:T(2,128)S(1)}, u32[]{:S(2)}, u32[]{:S(2)}) collective-permute-start(f32[3,4,2,1024]{3,2,1,0:T(2,128)S(1)} %get-tuple-element.28), channel_id=1, source_target_pairs={{0,1},{1,2},{2,3},{3,4},{4,5},{5,6},{6,7},{7,8},{8,9},{9,10},{10,1... | collective-permute-start | bytes 294920 | tf_op jit(solution)/shard_map/ppermute | solution.py:17
  81.0 4.1 %collective-permute-start.12 = (f32[3,4,2,1024]{3,2,1,0:T(2,128)S(1)}, f32[3,4,2,1024]{3,2,1,0:T(2,128)S(1)}, u32[]{:S(2)}, u32[]{:S(2)}) collective-permute-start(f32[3,4,2,1024]{3,2,1,0:T(2,128)S(1)} %get-tuple-element.29), channel_id=1, source_target_pairs={{1,0},{2,1},{3,2},{4,3},{5,4},{6,5},{7,6},{8,7},{9,8},{10,9},{11,1... | collective-permute-start | bytes 294920 | tf_op jit(solution)/shard_map/ppermute | solution.py:19
  88.4 8.3 %collective-permute-start.13 = (f32[64,1024]{1,0:T(8,128)S(1)}, f32[64,1024]{1,0:T(8,128)S(1)}, u32[]{:S(2)}, u32[]{:S(2)}) collective-permute-start(f32[64,1024]{1,0:T(8,128)S(1)} %slice_bitcast_fusion.14), channel_id=1, source_target_pairs={{0,32},{32,64},{64,96},{1,33},{33,65},{65,97},{2,34},{34,66},{66,9... | collective-permute-start | bytes 786440 | tf_op jit(solution)/shard_map/ppermute | solution.py:29
  97.1 7.6 %collective-permute-start.14 = (f32[3,4,2,1024]{3,2,1,0:T(2,128)S(1)}, f32[3,4,2,1024]{3,2,1,0:T(2,128)S(1)}, u32[]{:S(2)}, u32[]{:S(2)}) collective-permute-start(f32[3,4,2,1024]{3,2,1,0:T(2,128)S(1)} %get-tuple-element.26), channel_id=1, source_target_pairs={{0,1},{1,2},{2,3},{3,4},{4,5},{5,6},{6,7},{7,8},{8,9},{9,10},{10,1... | collective-permute-start | bytes 294920 | tf_op jit(solution)/shard_map/ppermute | solution.py:17
  102.8 4.1 %collective-permute-start.15 = (f32[3,4,2,1024]{3,2,1,0:T(2,128)S(1)}, f32[3,4,2,1024]{3,2,1,0:T(2,128)S(1)}, u32[]{:S(2)}, u32[]{:S(2)}) collective-permute-start(f32[3,4,2,1024]{3,2,1,0:T(2,128)S(1)} %get-tuple-element.27), channel_id=1, source_target_pairs={{1,0},{2,1},{3,2},{4,3},{5,4},{6,5},{7,6},{8,7},{9,8},{10,9},{11,1... | collective-permute-start | bytes 294920 | tf_op jit(solution)/shard_map/ppermute | solution.py:19
  110.1 8.3 %collective-permute-start.16 = (f32[64,1024]{1,0:T(8,128)S(1)}, f32[64,1024]{1,0:T(8,128)S(1)}, u32[]{:S(2)}, u32[]{:S(2)}) collective-permute-start(f32[64,1024]{1,0:T(8,128)S(1)} %slice_bitcast_fusion.13), channel_id=1, source_target_pairs={{0,32},{32,64},{64,96},{1,33},{33,65},{65,97},{2,34},{34,66},{66,9... | collective-permute-start | bytes 786440 | tf_op jit(solution)/shard_map/ppermute | solution.py:29
  121.1 7.9 %collective-permute-start.17 = (f32[3,8,2,1024]{3,2,1,0:T(2,128)S(1)}, f32[3,8,2,1024]{3,2,1,0:T(2,128)S(1)}, u32[]{:S(2)}, u32[]{:S(2)}) collective-permute-start(f32[3,8,2,1024]{3,2,1,0:T(2,128)S(1)} %get-tuple-element.16), channel_id=1, source_target_pairs={{0,1},{1,2},{2,3},{3,4},{4,5},{5,6},{6,7},{7,8},{8,9},{9,10},{10,1... | collective-permute-start | bytes 589832 | tf_op jit(solution)/shard_map/ppermute | solution.py:17
  126.8 5.1 %collective-permute-start.18 = (f32[3,8,2,1024]{3,2,1,0:T(2,128)S(1)}, f32[3,8,2,1024]{3,2,1,0:T(2,128)S(1)}, u32[]{:S(2)}, u32[]{:S(2)}) collective-permute-start(f32[3,8,2,1024]{3,2,1,0:T(2,128)S(1)} %get-tuple-element.17), channel_id=1, source_target_pairs={{1,0},{2,1},{3,2},{4,3},{5,4},{6,5},{7,6},{8,7},{9,8},{10,9},{11,1... | collective-permute-start | bytes 589832 | tf_op jit(solution)/shard_map/ppermute | solution.py:19
  139.7 19.8 %copy-start.1 = (f32[8,64,1024]{2,1,0:T(8,128)}, f32[8,64,1024]{2,1,0:T(8,128)S(1)}, u32[]{:S(2)}) copy-start(f32[8,64,1024]{2,1,0:T(8,128)S(1)} %multiply_add_fusion) | copy-start | bytes 6291460
  139.7 10.4 %collective-permute-start.21 = (f32[8,1,1024]{2,1,0:T(1,128)S(1)}, f32[8,1,1024]{2,1,0:T(1,128)S(1)}, u32[]{:S(2)}, u32[]{:S(2)}) collective-permute-start(f32[8,1,1024]{2,1,0:T(1,128)S(1)} %get-tuple-element.30), channel_id=1, source_target_pairs={{0,1},{1,2},{2,3},{3,4},{4,5},{5,6},{6,7},{7,8},{8,9},{9,10},{10,1... | collective-permute-start | bytes 98312 | tf_op jit(solution)/shard_map/ppermute | solution.py:17
  146.7 3.5 %collective-permute-start.20 = (f32[8,1,1024]{2,1,0:T(1,128)S(1)}, f32[8,1,1024]{2,1,0:T(1,128)S(1)}, u32[]{:S(2)}, u32[]{:S(2)}) collective-permute-start(f32[8,1,1024]{2,1,0:T(1,128)S(1)} %get-tuple-element.31), channel_id=1, source_target_pairs={{1,0},{2,1},{3,2},{4,3},{5,4},{6,5},{7,6},{8,7},{9,8},{10,9},{11,1... | collective-permute-start | bytes 98312 | tf_op jit(solution)/shard_map/ppermute | solution.py:19
  148.8 10.6 %collective-permute-start.19 = (f32[64,1024]{1,0:T(8,128)S(1)}, f32[64,1024]{1,0:T(8,128)S(1)}, u32[]{:S(2)}, u32[]{:S(2)}) collective-permute-start(f32[64,1024]{1,0:T(8,128)S(1)} %slice_bitcast_fusion.12), channel_id=1, source_target_pairs={{0,32},{32,64},{64,96},{1,33},{33,65},{65,97},{2,34},{34,66},{66,9... | collective-permute-start | bytes 786440 | tf_op jit(solution)/shard_map/ppermute | solution.py:29
where the time goes:
time: 163 us; the launch traced here: 162 us
  starting transfers between devices  63.5 us (39%)
  waiting for transfers between devices  56.4 us (35%)
  other arithmetic  32.4 us (20%)
  local copies, waits for them, and re-layouts  8.51 us (5%)
    ppermute x6, waiting for transfers between devices, passed_along(): return lax.ppermute(block, axis, route)  44.7 us
    ppermute x8, starting transfers between devices, extended(): lax.ppermute(tail, axis, [(i, (i + 1) % count) for i in range(ends)])  34.7 us
    ppermute x8, starting transfers between devices, extended(): lax.ppermute(head, axis, [((i + 1) % count, i) for i in range(ends)])  20.9 us
    ppermute x8, waiting for transfers between devices, extended(): lax.ppermute(head, axis, [((i + 1) % count, i) for i in range(ends)])  10.4 us
    ppermute x6, starting transfers between devices, passed_along(): return lax.ppermute(block, axis, route)  7.88 us
    div x4, other arithmetic, widened_smooth(): first_sweep = resid_wide / diagonal  7.53 us
    concatenate x7, other arithmetic, extended(): jnp.concatenate([lax.ppermute(tail, axis, [(i, (i + 1) % count) for i in...  6.93 us
    sub x2, other arithmetic, fine_residual(): return source + earlier - apply_operator(field, conduct)  4.54 us
  transfers between devices with their start and end apart: 22, of which 14 were waited for; matrix products, arithmetic and copies ran while one was open for 3% of the time, Pallas kernels for 0%

commit v1 on v0

v1 whole, which is shorter than its diff:
```python
import jax
import jax.numpy as jnp
from jax import lax
from jax.experimental import pallas as pl
from jax.experimental.pallas import tpu as pltpu
from jax.sharding import PartitionSpec as P


F32 = jnp.float32
ROWS = 64
HALO = 11
EXT = ROWS + 2 * HALO
DAMP = 0.8
C, D, INV, Q, K, KD, KINV, KQ, ST = range(9)
FULL = pl.BlockSpec(memory_space=pltpu.VMEM)
SMEM = pl.BlockSpec(memory_space=pltpu.SMEM)
ANY = pl.BlockSpec(memory_space=pl.ANY)


def ext(steps):
    return jax.ShapeDtypeStruct((steps, EXT, 8, 128), F32)


def rows_of(count):
    return jax.ShapeDtypeStruct((count, 8, 128), F32)


def view(x):
    steps = x.shape[0]
    return x.reshape(steps, ROWS // 8, 8, 8, 128).transpose(0, 1, 3, 2, 4).reshape(steps * ROWS * 8, 128)


def unview(y, steps):
    return y.reshape(steps, ROWS // 8, 8, 8, 128).transpose(0, 1, 3, 2, 4).reshape(steps, ROWS, 1024)


def at(ref, step, row):
    return ref[pl.ds(step * ROWS * 8 + (row // 8) * 64 + row % 8, 8, 8), :]


def tile_at(step, tile, row):
    return pl.ds(step * ROWS * 8 + tile * 64 + row, 8, 8)


def beside_maker():
    lane = lax.broadcasted_iota(jnp.int32, (8, 128), 1)
    sub = lax.broadcasted_iota(jnp.int32, (8, 128), 0)
    first, last = lane == 0, lane == 127
    top, bottom = sub == 0, sub == 7

    def beside(x):
        before = jnp.where(top, 0.0, pltpu.roll(x, 1, 0))
        after = jnp.where(bottom, 0.0, pltpu.roll(x, 7, 0))
        return pltpu.roll(jnp.where(last, before, x), 1, 1) + pltpu.roll(jnp.where(first, after, x), 127, 1)

    return beside


def around(beside, ref, step, r):
    return ref[step, r - 1] + ref[step, r + 1] + beside(ref[step, r])


def sweep(low, high, unroll, body):
    low, high = low + HALO, high + HALO
    count = high - low
    unroll = min(unroll, count)
    blocks = -(-count // unroll)
    if blocks == 1:
        for j in range(unroll):
            body(low + j)
        return

    def step(i, carry):
        start = jnp.minimum(low + i * unroll, high - unroll)
        for j in range(unroll):
            body(start + j)
        return carry

    lax.fori_loop(0, blocks, step, 0)


def coefficients(co, r, c):
    diag = 1.0 + 4.0 * c
    coarse = 1.0 + 8.0 * c
    recip = 1.0 / diag
    coarse_recip = 1.0 / coarse
    co[C, r] = c
    co[D, r] = diag
    co[INV, r] = DAMP * recip
    co[Q, r] = c * recip
    co[K, r] = 2.0 * c
    co[KD, r] = coarse
    co[KINV, r] = DAMP * coarse_recip
    co[KQ, r] = 2.0 * c * coarse_recip


class Stages:
    def __init__(self, beside, co):
        self.beside, self.co = beside, co

    def fine_defect(self, out, field, earlier, source, steps):
        def body(r):
            c, d, inv = self.co[C, r], self.co[D, r], self.co[INV, r]
            for t in steps:
                out[t, r] = (source[t, r] + earlier(t, r) - d * field[t, r] + c * around(self.beside, field, t, r)) * inv

        return body

    def coarse_defect(self, out, field, earlier, rhs, steps):
        def body(r):
            k, kd, kinv = self.co[K, r], self.co[KD, r], self.co[KINV, r]
            for m in steps:
                out[m, r] = (rhs[m, r] + earlier(m, r) - kd * field[m, r] + k * around(self.beside, field, m, r)) * kinv

        return body

    def smoothed(self, out, field, defect, steps, plane):
        def body(r):
            q = self.co[plane, r]
            for t in steps:
                base = defect[t, r] if field is None else field[t, r] + defect[t, r]
                out[t, r] = base + q * around(self.beside, defect, t, r)

        return body

    def restricted(self, out, scaled, field, earlier, source, pairs):
        def body(r):
            c, d, kinv = self.co[C, r], self.co[D, r], self.co[KINV, r]
            for m in pairs:
                parts = [
                    source[t, r] + earlier(t, r) - d * field[t, r] + c * around(self.beside, field, t, r)
                    for t in (2 * m, 2 * m + 1)
                ]
                both = parts[0] + parts[1]
                out[m, r] = both
                scaled[m, r] = both * kinv

        return body


def edge_pack(is_first, guess, source, start, conduct, top, bottom):
    for out, low in ((top, 0), (bottom, ROWS - HALO)):
        for j in range(HALO):
            for t in range(8):
                out[t, j] = at(guess, t, low + j)
                out[8 + t, j] = at(source, t, low + j)
            out[16, j] = at(conduct, 0, low + j)
            out[17, j] = at(start, 0, low + j) * is_first[0]


def last_step_pack(guess, source, conduct, out, g, e):
    beside = beside_maker()

    def fill(i, carry):
        for j in range(8):
            r = 8 * i + j
            for t in (6, 7):
                g[t - 6, r] = guess[tile_at(t, i, j), :]
            out[r] = g[1, r]
        return carry

    lax.fori_loop(0, ROWS // 8, fill, 0)

    def cond_at(r):
        return conduct[pl.ds((r // 8) * 64 + r % 8, 8, 8), :]

    def defect(i, carry):
        start = jnp.minimum(1 + i * 16, 63 - 16)
        for j in range(16):
            r = start + j
            c = cond_at(r)
            d = 1.0 + 4.0 * c
            right = source[pl.ds(7 * 512 + (r // 8) * 64 + r % 8, 8, 8), :]
            e[r] = (right + g[0, r] - d * g[1, r] + c * around(beside, g, 1, r)) * (DAMP / d)
        return carry

    lax.fori_loop(0, 4, defect, 0)

    def smooth(i, carry):
        start = jnp.minimum(2 + i * 16, 62 - 16)
        for j in range(16):
            r = start + j
            c = cond_at(r)
            q = c / (1.0 + 4.0 * c)
            out[ROWS - 2 + r] = g[1, r] + e[r] + q * (e[r - 1] + e[r + 1] + beside(e[r]))
        return carry

    lax.fori_loop(0, 4, smooth, 0)


def interior(is_first, guess, source, start, conduct, g, s, co, u, rs, e0, e1, e2, tmp):
    beside = beside_maker()

    def fill(i, carry):
        for j in range(8):
            r = HALO + 8 * i + j
            for t in range(8):
                g[t, r] = guess[tile_at(t, i, j), :]
                s[t, r] = source[tile_at(t, i, j), :]
            coefficients(co, r, conduct[tile_at(0, i, j), :])
            co[ST, r] = start[tile_at(0, i, j), :] * is_first[0]
        return carry

    lax.fori_loop(0, ROWS // 8, fill, 0)
    st = Stages(beside, co)
    sweep(1, 63, 8, st.fine_defect(tmp, g, lambda t, r: g[t - 1, r], s, range(1, 8)))
    sweep(2, 62, 8, st.smoothed(u, g, tmp, range(1, 8), Q))
    sweep(3, 61, 8, st.restricted(rs, tmp, u, lambda t, r: u[t - 1, r], s, range(1, 4)))
    sweep(4, 60, 16, st.smoothed(e0, None, tmp, range(1, 4), KQ))
    sweep(5, 59, 16, st.coarse_defect(tmp, e0, lambda m, r: e0[m - 1, r], rs, (2, 3)))
    sweep(6, 58, 16, st.smoothed(e1, e0, tmp, (2, 3), KQ))
    sweep(7, 57, 16, st.coarse_defect(tmp, e1, lambda m, r: e1[m - 1, r], rs, (3,)))
    sweep(8, 56, 16, st.smoothed(e2, e1, tmp, (3,), KQ))


def edge_first(above, below, g_in, s_in, co_in, u_in, g, s, co, u, out, tmp):
    del g_in, s_in, co_in, u_in
    beside = beside_maker()
    for source, low in ((above, 0), (below, HALO + ROWS)):

        def fill(j, carry):
            for t in range(8):
                g[t, low + j] = source[t, j]
                s[t, low + j] = source[8 + t, j]
            coefficients(co, low + j, source[16, j])
            co[ST, low + j] = source[17, j]
            return carry

        lax.fori_loop(0, HALO, fill, 0)
    st = Stages(beside, co)
    for low, high in ((-10, 3), (61, 74)):
        sweep(low, high, 16, st.fine_defect(tmp, g, lambda t, r: g[t - 1, r], s, (7,)))
    for low, high in ((-9, 2), (62, 73)):
        sweep(low, high, 16, st.smoothed(u, g, tmp, (7,), Q))
    for j in range(10):
        out[j] = g[7, HALO - 10 + j]
        out[10 + j] = g[7, HALO + ROWS + j]
        out[20 + j] = u[7, HALO - 8 + j]
        out[30 + j] = u[7, HALO + 62 + j]


def edges(g, s, co, u_in, rs_in, e0_in, e1_in, e2_in, u, rs, e0, e1, e2, out, tmp):
    del u_in, rs_in, e0_in, e1_in, e2_in
    beside = beside_maker()
    st = Stages(beside, co)

    def both(inner, depth, unroll, body):
        sweep(-depth, inner, unroll, body)
        sweep(ROWS - inner, ROWS + depth, unroll, body)

    both(3, 10, 13, st.fine_defect(tmp, g, lambda t, r: g[t - 1, r], s, range(1, 7)))
    both(2, 9, 11, st.smoothed(u, g, tmp, range(1, 7), Q))
    both(3, 8, 11, st.restricted(rs, tmp, u, lambda t, r: u[t - 1, r], s, range(1, 4)))

    def scale(r):
        for m in range(1, 4):
            tmp[m, r] = rs[m, r] * co[KINV, r]

    sweep(3, 5, 2, scale)
    sweep(59, 61, 2, scale)
    both(4, 7, 11, st.smoothed(e0, None, tmp, range(1, 4), KQ))
    both(7, 6, 13, st.coarse_defect(tmp, e0, lambda m, r: e0[m - 1, r], rs, (2, 3)))
    both(6, 5, 11, st.smoothed(e1, e0, tmp, (2, 3), KQ))
    both(9, 4, 13, st.coarse_defect(tmp, e1, lambda m, r: e1[m - 1, r], rs, (3,)))
    both(8, 3, 11, st.smoothed(e2, e1, tmp, (3,), KQ))

    def copy(i, carry):
        for j in range(19):
            r = jnp.minimum(i * 19 + j, 75)
            out[r] = e0[3, HALO - 6 + r]
            q = jnp.minimum(r, 71)
            out[76 + q] = e1[3, HALO - 4 + q]
            p = jnp.minimum(r, 69)
            out[148 + p] = e2[3, HALO - 3 + p]
        return carry

    lax.fori_loop(0, 4, copy, 0)


def middle(t0, t1, g, s, co, u_in, rs_in, e0_in, e1_in, e2_in, u, rs, e0, e1, e2, before, sol7, send, gb, tmp, u2):
    del u_in, rs_in, e0_in, e1_in, e2_in
    beside = beside_maker()
    st = Stages(beside, co)

    def fill(i, carry):
        for j in range(8):
            r = i * 8 + j
            gb[HALO + r] = t0[r] + co[ST, HALO + r]
            q = jnp.minimum(r, 59)
            before[HALO + 2 + q] = t0[ROWS + q] + co[ST, HALO + 2 + q]
        return carry

    lax.fori_loop(0, ROWS // 8, fill, 0)
    for j in range(10):
        gb[HALO - 10 + j] = t1[j] + co[ST, HALO - 10 + j]
        gb[HALO + ROWS + j] = t1[10 + j] + co[ST, HALO + ROWS + j]
        before[HALO - 8 + j] = t1[20 + j] + co[ST, HALO - 8 + j]
        before[HALO + 62 + j] = t1[30 + j] + co[ST, HALO + 62 + j]
    sweep(-10, 74, 21, st.fine_defect(tmp, g, lambda t, r: gb[r], s, (0,)))
    sweep(-9, 73, 21, st.smoothed(u, g, tmp, (0,), Q))
    sweep(-8, 72, 16, st.restricted(rs, tmp, u, lambda t, r: u[0, r] if t else before[r], s, (0,)))
    sweep(-7, 71, 20, st.smoothed(e0, None, tmp, (0,), KQ))
    sweep(-6, 70, 19, st.coarse_defect(tmp, e0, lambda m, r: e0[0, r], rs, (1,)))
    sweep(-5, 69, 19, st.smoothed(e1, e0, tmp, (1,), KQ))
    sweep(-4, 68, 18, st.coarse_defect(tmp, e1, lambda m, r: e1[1, r], rs, (2,)))

    def corrected(r):
        q = co[KQ, r]
        late = e1[2, r] + tmp[2, r] + q * around(beside, tmp, 2, r)
        e2[2, r] = late
        u2[0, r] = u[6, r] + 0.5 * (late + e2[3, r])
        u2[1, r] = u[7, r] + e2[3, r]

    sweep(-3, 67, 18, corrected)

    def defect(r):
        tmp[0, r] = (
            s[7, r] + u2[0, r] - co[D, r] * u2[1, r] + co[C, r] * around(beside, u2, 1, r)
        ) * co[INV, r]

    sweep(-2, 66, 17, defect)

    def final(r):
        sol7[0, r] = u2[1, r] + tmp[0, r] + co[Q, r] * around(beside, tmp, 0, r)

    sweep(-1, 65, 17, final)

    def copy(i, carry):
        for j in range(8):
            send[tile_at(0, i, j), :] = sol7[0, HALO + 8 * i + j]
        return carry

    lax.fori_loop(0, ROWS // 8, copy, 0)


def last(t2, s, co, u, rs, e0, e1_in, e2_in, before, sol7, sol_out, res_out, base, e1, u2, tmp, sol, sol_nat, res_nat, sems):
    beside = beside_maker()
    st = Stages(beside, co)

    def first_defect(r):
        tmp[0, r] = (
            rs[0, r] + t2[r - (HALO - 6)] - co[KD, r] * e0[0, r] + co[K, r] * around(beside, e0, 0, r)
        ) * co[KINV, r]

    sweep(-6, 70, 19, first_defect)
    sweep(-5, 69, 19, st.smoothed(e1, e0, tmp, (0,), KQ))

    def carry_over(r):
        e1[1, r] = e1_in[1, r]

    sweep(-5, 69, 19, carry_over)

    def second_defect(r):
        k, kd, kinv = co[K, r], co[KD, r], co[KINV, r]
        earlier = (t2[76 + r - (HALO - 4)], e1[0, r])
        for m in (0, 1):
            tmp[m, r] = (rs[m, r] + earlier[m] - kd * e1[m, r] + k * around(beside, e1, m, r)) * kinv

    sweep(-4, 68, 18, second_defect)

    def corrected(r):
        q = co[KQ, r]
        boundary = t2[148 + r - (HALO - 3)]
        e20 = e1[0, r] + tmp[0, r] + q * around(beside, tmp, 0, r)
        e21 = e1[1, r] + tmp[1, r] + q * around(beside, tmp, 1, r)
        e22, e23 = e2_in[2, r], e2_in[3, r]
        u2[7, r] = before[r] + boundary
        u2[0, r] = u[0, r] + 0.5 * (boundary + e20)
        u2[1, r] = u[1, r] + e20
        u2[2, r] = u[2, r] + 0.5 * (e20 + e21)
        u2[3, r] = u[3, r] + e21
        u2[4, r] = u[4, r] + 0.5 * (e21 + e22)
        u2[5, r] = u[5, r] + e22
        u2[6, r] = u[6, r] + 0.5 * (e22 + e23)

    sweep(-3, 67, 10, corrected)
    sweep(-2, 66, 8, st.fine_defect(tmp, u2, lambda t, r: u2[(t - 1) % 8, r], s, range(7)))
    final = st.smoothed(sol, u2, tmp, range(7), Q)

    def final_all(r):
        final(r)
        sol[7, r] = sol7[0, r]

    sweep(-1, 0, 1, final_all)
    sweep(64, 65, 1, final_all)

    def solve(i, carry):
        for j in range(8):
            r = HALO + 8 * i + j
            final_all(r)
            for t in range(8):
                sol_nat[tile_at(t, i, j), :] = sol[t, r]
        return carry

    lax.fori_loop(0, ROWS // 8, solve, 0)
    copy_sol = pltpu.make_async_copy(sol_nat, sol_out, sems.at[0])
    copy_sol.start()

    def resid(i, carry):
        for j in range(8):
            r = HALO + 8 * i + j
            c, d = co[C, r], co[D, r]
            for t in range(8):
                earlier = sol[t - 1, r] if t else co[ST, r]
                value = s[t, r] + earlier - d * sol[t, r] + c * around(beside, sol, t, r)
                if t:
                    res_nat[tile_at(t - 1, i, j), :] = value
                else:
                    base[tile_at(0, i, j), :] = value
        return carry

    lax.fori_loop(0, ROWS // 8, resid, 0)
    copy_res = pltpu.make_async_copy(res_nat, res_out.at[pl.ds(ROWS * 8, 7 * ROWS * 8)], sems.at[1])
    copy_res.start()
    copy_sol.wait()
    copy_res.wait()


def finish(res_in, base, t3, res_out, total, sem):
    del res_in
    total[...] = base[...] + t3[...]
    copy = pltpu.make_async_copy(total, res_out.at[pl.ds(0, ROWS * 8)], sem)
    copy.start()
    copy.wait()


def call(kernel, ins, outs, scratch=(), aliases=None, specs=None, out_specs=None, limit=24):
    return pl.pallas_call(
        kernel,
        out_shape=outs,
        in_specs=specs or [FULL] * len(ins),
        out_specs=out_specs or [FULL] * len(outs),
        scratch_shapes=list(scratch),
        input_output_aliases=aliases or {},
        compiler_params=pltpu.CompilerParams(vmem_limit_bytes=limit * 2**20),
    )(*ins)


def along(block, axis, distance):
    count = lax.axis_size(axis)
    return lax.ppermute(block, axis, [(i, i + distance) for i in range(count) if 0 <= i + distance < count])


def cycle(source, guess, start_state, conduct):
    is_first = (lax.axis_index("tm") == 0).astype(F32).reshape(1)
    guess_v, source_v = view(guess), view(source)
    start_v, conduct_v = view(start_state[None]), view(conduct[None])
    halo = jax.ShapeDtypeStruct((18, HALO, 8, 128), F32)
    vmem = lambda steps: pltpu.VMEM((steps, EXT, 8, 128), F32)

    top, bottom = call(
        edge_pack, (is_first, guess_v, source_v, start_v, conduct_v), [halo, halo], specs=[SMEM] + [FULL] * 4, limit=4
    )
    above = along(bottom, "space", 1)
    below = along(top, "space", -1)
    (send0,) = call(
        last_step_pack,
        (guess_v, source_v, conduct_v),
        [rows_of(124)],
        [pltpu.VMEM((2, ROWS, 8, 128), F32), pltpu.VMEM((ROWS, 8, 128), F32)],
        limit=4,
    )
    t0 = along(send0, "tm", 1)
    g, s, co, u, rs, e0, e1, e2 = call(
        interior,
        (is_first, guess_v, source_v, start_v, conduct_v),
        [ext(8), ext(8), ext(9), ext(8), ext(4), ext(4), ext(4), ext(4)],
        [vmem(8)],
        specs=[SMEM] + [FULL] * 4,
        limit=6,
    )
    g, s, co, u, send1 = call(
        edge_first,
        (above, below, g, s, co, u),
        [ext(8), ext(8), ext(9), ext(8), rows_of(40)],
        [vmem(8)],
        aliases={2: 0, 3: 1, 4: 2, 5: 3},
        limit=6,
    )
    t1 = along(send1, "tm", 1)
    u, rs, e0, e1, e2, send2 = call(
        edges,
        (g, s, co, u, rs, e0, e1, e2),
        [ext(8), ext(4), ext(4), ext(4), ext(4), rows_of(218)],
        [vmem(8)],
        aliases={3: 0, 4: 1, 5: 2, 6: 3, 7: 4},
        limit=6,
    )
    t2 = along(send2, "tm", 1)
    u, rs, e0, e1, e2, before, sol7, send3 = call(
        middle,
        (t0, t1, g, s, co, u, rs, e0, e1, e2),
        [
            ext(8), ext(4), ext(4), ext(4), ext(4), rows_of(EXT), ext(1),
            jax.ShapeDtypeStruct((ROWS * 8, 128), F32),
        ],
        [pltpu.VMEM((EXT, 8, 128), F32), vmem(4), vmem(2)],
        aliases={5: 0, 6: 1, 7: 2, 8: 3, 9: 4},
        limit=6,
    )
    t3 = along(send3, "tm", 1)
    nat = jax.ShapeDtypeStruct((8 * ROWS * 8, 128), F32)
    one = jax.ShapeDtypeStruct((ROWS * 8, 128), F32)
    sol, res, base = call(
        last,
        (t2, s, co, u, rs, e0, e1, e2, before, sol7),
        [nat, nat, one],
        [
            vmem(2), vmem(8), vmem(8), vmem(8),
            pltpu.VMEM(nat.shape, F32), pltpu.VMEM((7 * ROWS * 8, 128), F32), pltpu.SemaphoreType.DMA((2,)),
        ],
        out_specs=[ANY, ANY, FULL],
        limit=16,
    )
    (res,) = call(
        finish,
        (res, base, t3),
        [nat],
        [pltpu.VMEM((ROWS * 8, 128), F32), pltpu.SemaphoreType.DMA],
        aliases={0: 0},
        specs=[ANY, FULL, FULL],
        out_specs=[ANY],
        limit=4,
    )
    return unview(sol, 8), unview(res, 8)


def solution(mesh):
    return jax.shard_map(
        cycle,
        mesh=mesh,
        in_specs=(P("tm", "space", None), P("tm", "space", None), P("space", None), P("space", None)),
        out_specs=(P("tm", "space", None), P("tm", "space", None)),
        check_vma=False,
    )
```

time: 163 us -> 82.5 us (0.51)
  the two profiles are of different devices: /device:TPU:30 before, /device:TPU:32 now
where the time goes in v1:
time: 82.5 us; the launch traced here: 82.2 us
  waiting for transfers between devices  27.3 us (33%)
  Pallas kernels  26.9 us (33%)
  starting transfers between devices  22.1 us (27%)
  local copies, waits for them, and re-layouts  5.09 us (6%)
    ppermute x6, waiting for transfers between devices, along(): lax.ppermute(block, axis, [(i, i + distance) for i in range(count) if 0 <...  27.3 us
    pallas_call x8, Pallas kernels, call(): pl.pallas_call(kernel, out_shape=outs, in_specs=specs or [FULL] * len(ins...  26.9 us
    ppermute x6, starting transfers between devices, along(): lax.ppermute(block, axis, [(i, i + distance) for i in range(count) if 0 <...  22.1 us
    unnamed x14, local copies, waits for them, and re-layouts  5.09 us
  transfers between devices with their start and end apart: 6, of which 3 were waited for; matrix products, arithmetic and copies ran while one was open for 0% of the time, Pallas kernels for 28%

profile of v1, /device:TPU:32, one launch (start us, length us, event | category | flops | bytes accessed | tf_op | source)
XLA Modules:
  0.0 82.2 jit_solution(8391053022144233915)
XLA Ops:
  0.6 0.0 copy-start
  0.6 1.6 %copy-done = f32[8,64,1024]{2,1,0:T(8,128)S(1)} copy-done((f32[8,64,1024]{2,1,0:T(8,128)S(1)}, f32[8,64,1024]{2,1,0:T(8,128)}, u32[]{:S(2)}) %copy-start) | copy-done | bytes 2097176
  2.2 0.0 copy-start.2
  2.2 1.6 %copy-done.2 = f32[8,64,1024]{2,1,0:T(8,128)S(1)} copy-done((f32[8,64,1024]{2,1,0:T(8,128)S(1)}, f32[8,64,1024]{2,1,0:T(8,128)}, u32[]{:S(2)}) %copy-start.2) | copy-done | bytes 2097176
  3.8 0.0 copy-start.4
  3.8 0.9 %copy-done.4 = f32[64,1024]{1,0:T(8,128)S(1)} copy-done((f32[64,1024]{1,0:T(8,128)S(1)}, f32[64,1024]{1,0:T(8,128)}, u32[]{:S(2)}) %copy-start.4) | copy-done | bytes 262168
  4.8 0.0 copy-start.6
  4.8 0.9 %copy-done.6 = f32[64,1024]{1,0:T(8,128)S(1)} copy-done((f32[64,1024]{1,0:T(8,128)S(1)}, f32[64,1024]{1,0:T(8,128)}, u32[]{:S(2)}) %copy-start.6) | copy-done | bytes 262168
  5.7 0.0 copy-start.1
  5.7 0.3 shard_map.59
  6.0 2.1 %collective-permute-start = (f32[18,11,8,128]{3,2,1,0:T(8,128)S(1)}, f32[18,11,8,128]{3,2,1,0:T(8,128)S(1)}, u32[]{:S(2)}, u32[]{:S(2)}) collective-permute-start(f32[18,11,8,128]{3,2,1,0:T(8,128)S(1)} %get-tuple-element.34), channel_id=1, source_target_pairs={{0,1},{1,2},{2,3},{3,4},{4,5},{5,6},{6,7},{7,8},{8,9},{9,10},{10,1... | collective-permute-start | bytes 2433032 | tf_op jit(solution)/shard_map/ppermute | solution.py:441
  8.1 5.8 %collective-permute-start.1 = (f32[18,11,8,128]{3,2,1,0:T(8,128)S(1)}, f32[18,11,8,128]{3,2,1,0:T(8,128)S(1)}, u32[]{:S(2)}, u32[]{:S(2)}) collective-permute-start(f32[18,11,8,128]{3,2,1,0:T(8,128)S(1)} %get-tuple-element.35), channel_id=1, source_target_pairs={{1,0},{2,1},{3,2},{4,3},{5,4},{6,5},{7,6},{8,7},{9,8},{10,9},{11,1... | collective-permute-start | bytes 2433032 | tf_op jit(solution)/shard_map/ppermute | solution.py:441
  13.8 0.0 copy-done.1
  13.8 8.2 %shard_map.60 = (f32[8,86,8,128]{3,2,1,0:T(8,128)S(1)}, f32[8,86,8,128]{3,2,1,0:T(8,128)S(1)}, f32[9,86,8,128]{3,2,1,0:T(8,128)S(1)}, f32[8,86,8,128]{3,2,1,0:T(...) custom-call(f32[1]{0:T(128)} %bitcast.is_first, ...), custom_call_target="tpu_custom_call" | custom-call | tf_op jit(solution)/shard_map/pallas_call | solution.py:428
  22.0 0.0 collective-permute-done.above
  22.0 1.5 %collective-permute-done.1.below = f32[18,11,8,128]{3,2,1,0:T(8,128)S(1)} collective-permute-done((f32[18,11,8,128]{3,2,1,0:T(8,128)S(1)}, f32[18,11,8,128]{3,2,1,0:T(8,128)S(1)}, u32[]{:S(2)}, u32[]{:S(2)}) %collective-permute-start.1) | collective-permute-done | bytes 811040 | tf_op jit(solution)/shard_map/ppermute | solution.py:441
  23.6 0.5 shard_map.61
  24.1 0.0 copy-start.3
  24.1 0.0 copy-start.5
  24.1 2.0 %shard_map.62 = (f32[8,86,8,128]{3,2,1,0:T(8,128)S(1)}, f32[4,86,8,128]{3,2,1,0:T(8,128)S(1)}, f32[4,86,8,128]{3,2,1,0:T(8,128)S(1)}, f32[4,86,8,128]{3,2,1,0:T(...) custom-call(f32[8,86,8,128]{3,2,1,0:T(8,128)S(1)} %get-tuple-element, ...), custom_call_target="tpu_custom_call", output_to_operand_aliasing={{0}: (3, {}), {1}: (4, {}), {2}: (5, {}), {3}: (6, {}), {4}... | custom-call | tf_op jit(solution)/shard_map/pallas_call | solution.py:428
  26.2 3.5 %collective-permute-start.2 = (f32[218,8,128]{2,1,0:T(8,128)S(1)}, f32[218,8,128]{2,1,0:T(8,128)S(1)}, u32[]{:S(2)}, u32[]{:S(2)}) collective-permute-start(f32[218,8,128]{2,1,0:T(8,128)S(1)} %get-tuple-element.48), channel_id=1, source_target_pairs={{0,32},{32,64},{64,96},{1,33},{33,65},{65,97},{2,34},{34,66},{66,9... | collective-permute-start | bytes 2678792 | tf_op jit(solution)/shard_map/ppermute | solution.py:441
  29.6 0.0 copy-done.3
  29.6 0.0 copy-done.5
  29.6 1.1 %shard_map.63 = f32[124,8,128]{2,1,0:T(8,128)S(1)} custom-call(f32[4096,128]{1,0:T(8,128)S(1)} %bitcast.33, f32[4096,128]{1,0:T(8,128)S(1)} %bitcast.36, f32[512,128]{1,0:T(8,128)S(1)} %bitcast.39), custom_call_target="tpu_custom_call" | custom-call | tf_op jit(solution)/shard_map/pallas_call | solution.py:428
  30.7 3.4 %collective-permute-start.3 = (f32[124,8,128]{2,1,0:T(8,128)S(1)}, f32[124,8,128]{2,1,0:T(8,128)S(1)}, u32[]{:S(2)}, u32[]{:S(2)}) collective-permute-start(f32[124,8,128]{2,1,0:T(8,128)S(1)} %shard_map.63), channel_id=1, source_target_pairs={{0,32},{32,64},{64,96},{1,33},{33,65},{65,97},{2,34},{34,66},{66,9... | collective-permute-start | bytes 1523720 | tf_op jit(solution)/shard_map/ppermute | solution.py:441
  34.1 3.1 %collective-permute-start.4 = (f32[40,8,128]{2,1,0:T(8,128)S(1)}, f32[40,8,128]{2,1,0:T(8,128)S(1)}, u32[]{:S(2)}, u32[]{:S(2)}) collective-permute-start(f32[40,8,128]{2,1,0:T(8,128)S(1)} %get-tuple-element.49), channel_id=1, source_target_pairs={{0,32},{32,64},{64,96},{1,33},{33,65},{65,97},{2,34},{34,66},{66,9... | collective-permute-start | bytes 491528 | tf_op jit(solution)/shard_map/ppermute | solution.py:441
  37.2 23.5 %collective-permute-done.3.t0 = f32[124,8,128]{2,1,0:T(8,128)S(1)} collective-permute-done((f32[124,8,128]{2,1,0:T(8,128)S(1)}, f32[124,8,128]{2,1,0:T(8,128)S(1)}, u32[]{:S(2)}, u32[]{:S(2)}) %collective-permute-start.3) | collective-permute-done | bytes 507936 | tf_op jit(solution)/shard_map/ppermute | solution.py:441
  60.6 2.3 %collective-permute-done.4.t1 = f32[40,8,128]{2,1,0:T(8,128)S(1)} collective-permute-done((f32[40,8,128]{2,1,0:T(8,128)S(1)}, f32[40,8,128]{2,1,0:T(8,128)S(1)}, u32[]{:S(2)}, u32[]{:S(2)}) %collective-permute-start.4) | collective-permute-done | bytes 163872 | tf_op jit(solution)/shard_map/ppermute | solution.py:441
  62.9 5.2 %shard_map.64 = (f32[8,86,8,128]{3,2,1,0:T(8,128)S(1)}, f32[4,86,8,128]{3,2,1,0:T(8,128)S(1)}, f32[4,86,8,128]{3,2,1,0:T(8,128)S(1)}, f32[4,86,8,128]{3,2,1,0:T(...) custom-call(f32[124,8,128]{2,1,0:T(8,128)S(1)} %collective-permute-d, ...), custom_call_target="tpu_custom_call", output_to_operand_aliasing={{0}: (5, {}), {1}: (6, {}), {2}: (7, {}), {3}: (8, {}), {4}... | custom-call | tf_op jit(solution)/shard_map/pallas_call | solution.py:428
  68.1 4.4 %collective-permute-start.5 = (f32[512,128]{1,0:T(8,128)S(1)}, f32[512,128]{1,0:T(8,128)S(1)}, u32[]{:S(2)}, u32[]{:S(2)}) collective-permute-start(f32[512,128]{1,0:T(8,128)S(1)} %get-tuple-element.65), channel_id=1, source_target_pairs={{0,32},{32,64},{64,96},{1,33},{33,65},{65,97},{2,34},{34,66},{66,9... | collective-permute-start | bytes 786440 | tf_op jit(solution)/shard_map/ppermute | solution.py:441
  72.5 0.0 collective-permute-done.2.t2
  72.5 8.9 %shard_map.65 = (f32[4096,128]{1,0:T(8,128)}, f32[4096,128]{1,0:T(8,128)}, f32[512,128]{1,0:T(8,128)S(1)}) custom-call(f32[218,8,128]{2,1,0:T(8,128)S(1)} %collective-permute-done.2.t2, f32[8,86,8,128]{3,2,1,0:T(8,128)S(1)} %get-tuple-element.41.s, f32[9,86,8,128]{3,2,1,0:T(8,128)S(1)} %get-tuple-element.42.co, f32[8,86,8,128]{3,2,1,0:T(8,128)S(1)} %get-tuple-element.55.u, ...), custom_call_target="tpu_custom_call" | custom-call | tf_op jit(solution)/shard_map/pallas_call | solution.py:428
  81.4 0.0 collective-permute-done.5.t3
  81.4 0.7 shard_map.66
Async XLA Ops:
  0.6 1.6 %copy-start = (f32[8,64,1024]{2,1,0:T(8,128)S(1)}, f32[8,64,1024]{2,1,0:T(8,128)}, u32[]{:S(2)}) copy-start(f32[8,64,1024]{2,1,0:T(8,128)} %param.5) | copy-start | bytes 6291460
  2.2 1.6 %copy-start.2 = (f32[8,64,1024]{2,1,0:T(8,128)S(1)}, f32[8,64,1024]{2,1,0:T(8,128)}, u32[]{:S(2)}) copy-start(f32[8,64,1024]{2,1,0:T(8,128)} %param.4) | copy-start | bytes 6291460
  3.8 0.9 %copy-start.4 = (f32[64,1024]{1,0:T(8,128)S(1)}, f32[64,1024]{1,0:T(8,128)}, u32[]{:S(2)}) copy-start(f32[64,1024]{1,0:T(8,128)} %param.7) | copy-start | bytes 786436
  4.8 0.9 %copy-start.6 = (f32[64,1024]{1,0:T(8,128)S(1)}, f32[64,1024]{1,0:T(8,128)}, u32[]{:S(2)}) copy-start(f32[64,1024]{1,0:T(8,128)} %param.6) | copy-start | bytes 786436
  5.7 8.1 %copy-start.1 = (f32[8,64,1024]{2,1,0:T(8,128)S(1)}, f32[8,64,1024]{2,1,0:T(8,128)}, u32[]{:S(2)}) copy-start(f32[8,64,1024]{2,1,0:T(8,128)} %param.5) | copy-start | bytes 6291460
  6.0 16.0 %collective-permute-start = (f32[18,11,8,128]{3,2,1,0:T(8,128)S(1)}, f32[18,11,8,128]{3,2,1,0:T(8,128)S(1)}, u32[]{:S(2)}, u32[]{:S(2)}) collective-permute-start(f32[18,11,8,128]{3,2,1,0:T(8,128)S(1)} %get-tuple-element.34), channel_id=1, source_target_pairs={{0,1},{1,2},{2,3},{3,4},{4,5},{5,6},{6,7},{7,8},{8,9},{9,10},{10,1... | collective-permute-start | bytes 2433032 | tf_op jit(solution)/shard_map/ppermute | solution.py:441
  8.1 15.5 %collective-permute-start.1 = (f32[18,11,8,128]{3,2,1,0:T(8,128)S(1)}, f32[18,11,8,128]{3,2,1,0:T(8,128)S(1)}, u32[]{:S(2)}, u32[]{:S(2)}) collective-permute-start(f32[18,11,8,128]{3,2,1,0:T(8,128)S(1)} %get-tuple-element.35), channel_id=1, source_target_pairs={{1,0},{2,1},{3,2},{4,3},{5,4},{6,5},{7,6},{8,7},{9,8},{10,9},{11,1... | collective-permute-start | bytes 2433032 | tf_op jit(solution)/shard_map/ppermute | solution.py:441
  24.1 5.5 %copy-start.3 = (f32[8,64,1024]{2,1,0:T(8,128)S(1)}, f32[8,64,1024]{2,1,0:T(8,128)}, u32[]{:S(2)}) copy-start(f32[8,64,1024]{2,1,0:T(8,128)} %param.4) | copy-start | bytes 6291460
  24.1 5.5 %copy-start.5 = (f32[64,1024]{1,0:T(8,128)S(1)}, f32[64,1024]{1,0:T(8,128)}, u32[]{:S(2)}) copy-start(f32[64,1024]{1,0:T(8,128)} %param.7) | copy-start | bytes 786436
  26.2 46.4 %collective-permute-start.2 = (f32[218,8,128]{2,1,0:T(8,128)S(1)}, f32[218,8,128]{2,1,0:T(8,128)S(1)}, u32[]{:S(2)}, u32[]{:S(2)}) collective-permute-start(f32[218,8,128]{2,1,0:T(8,128)S(1)} %get-tuple-element.48), channel_id=1, source_target_pairs={{0,32},{32,64},{64,96},{1,33},{33,65},{65,97},{2,34},{34,66},{66,9... | collective-permute-start | bytes 2678792 | tf_op jit(solution)/shard_map/ppermute | solution.py:441
  30.7 29.9 %collective-permute-start.3 = (f32[124,8,128]{2,1,0:T(8,128)S(1)}, f32[124,8,128]{2,1,0:T(8,128)S(1)}, u32[]{:S(2)}, u32[]{:S(2)}) collective-permute-start(f32[124,8,128]{2,1,0:T(8,128)S(1)} %shard_map.63), channel_id=1, source_target_pairs={{0,32},{32,64},{64,96},{1,33},{33,65},{65,97},{2,34},{34,66},{66,9... | collective-permute-start | bytes 1523720 | tf_op jit(solution)/shard_map/ppermute | solution.py:441
  34.1 28.8 %collective-permute-start.4 = (f32[40,8,128]{2,1,0:T(8,128)S(1)}, f32[40,8,128]{2,1,0:T(8,128)S(1)}, u32[]{:S(2)}, u32[]{:S(2)}) collective-permute-start(f32[40,8,128]{2,1,0:T(8,128)S(1)} %get-tuple-element.49), channel_id=1, source_target_pairs={{0,32},{32,64},{64,96},{1,33},{33,65},{65,97},{2,34},{34,66},{66,9... | collective-permute-start | bytes 491528 | tf_op jit(solution)/shard_map/ppermute | solution.py:441
  68.1 13.3 %collective-permute-start.5 = (f32[512,128]{1,0:T(8,128)S(1)}, f32[512,128]{1,0:T(8,128)S(1)}, u32[]{:S(2)}, u32[]{:S(2)}) collective-permute-start(f32[512,128]{1,0:T(8,128)S(1)} %get-tuple-element.65), channel_id=1, source_target_pairs={{0,32},{32,64},{64,96},{1,33},{33,65},{65,97},{2,34},{34,66},{66,9... | collective-permute-start | bytes 786440 | tf_op jit(solution)/shard_map/ppermute | solution.py:441

commit v2 on v1

v2 whole, which is shorter than its diff:
```python
import jax
import jax.numpy as jnp
from jax import lax
from jax.experimental import pallas as pl
from jax.experimental.pallas import tpu as pltpu
from jax.sharding import PartitionSpec as P


F32 = jnp.float32
ROWS = 64
HALO = 11
EXT = ROWS + 2 * HALO
DAMP = 0.8
C, D, INV, Q, K, KD, KINV, KQ, ST = range(9)
FULL = pl.BlockSpec(memory_space=pltpu.VMEM)
SMEM = pl.BlockSpec(memory_space=pltpu.SMEM)
ANY = pl.BlockSpec(memory_space=pltpu.HBM)


def ext(steps):
    return jax.ShapeDtypeStruct((steps, EXT, 8, 128), F32)


def rows_of(count):
    return jax.ShapeDtypeStruct((count, 8, 128), F32)


def view(x):
    steps = x.shape[0]
    return x.reshape(steps, ROWS // 8, 8, 8, 128).transpose(0, 1, 3, 2, 4).reshape(steps * ROWS * 8, 128)


def unview(y, steps):
    return y.reshape(steps, ROWS // 8, 8, 8, 128).transpose(0, 1, 3, 2, 4).reshape(steps, ROWS, 1024)


def tile_at(step, tile, row):
    return pl.ds(step * ROWS * 8 + tile * 64 + row, 8, 8)


def beside_maker():
    lane = lax.broadcasted_iota(jnp.int32, (8, 128), 1)
    sub = lax.broadcasted_iota(jnp.int32, (8, 128), 0)
    first, last = lane == 0, lane == 127
    top, bottom = sub == 0, sub == 7

    def beside(x):
        before = jnp.where(top, 0.0, pltpu.roll(x, 1, 0))
        after = jnp.where(bottom, 0.0, pltpu.roll(x, 7, 0))
        return pltpu.roll(jnp.where(last, before, x), 1, 1) + pltpu.roll(jnp.where(first, after, x), 127, 1)

    return beside


def around(beside, ref, step, r):
    return ref[step, r - 1] + ref[step, r + 1] + beside(ref[step, r])


def sweep(low, high, unroll, body):
    low, high = low + HALO, high + HALO
    count = high - low
    unroll = min(unroll, count)
    blocks = -(-count // unroll)
    if blocks == 1:
        for j in range(unroll):
            body(low + j)
        return

    def step(i, carry):
        start = jnp.minimum(low + i * unroll, high - unroll)
        for j in range(unroll):
            body(start + j)
        return carry

    lax.fori_loop(0, blocks, step, 0)


def coefficients(co, r, c):
    diag = 1.0 + 4.0 * c
    coarse = 1.0 + 8.0 * c
    recip = 1.0 / diag
    coarse_recip = 1.0 / coarse
    co[C, r] = c
    co[D, r] = diag
    co[INV, r] = DAMP * recip
    co[Q, r] = c * recip
    co[K, r] = 2.0 * c
    co[KD, r] = coarse
    co[KINV, r] = DAMP * coarse_recip
    co[KQ, r] = 2.0 * c * coarse_recip


class Stages:
    def __init__(self, beside, co):
        self.beside, self.co = beside, co

    def fine_defect(self, out, field, earlier, source, steps):
        def body(r):
            c, d, inv = self.co[C, r], self.co[D, r], self.co[INV, r]
            for t in steps:
                out[t, r] = (source[t, r] + earlier(t, r) - d * field[t, r] + c * around(self.beside, field, t, r)) * inv

        return body

    def coarse_defect(self, out, field, earlier, rhs, steps):
        def body(r):
            k, kd, kinv = self.co[K, r], self.co[KD, r], self.co[KINV, r]
            for m in steps:
                out[m, r] = (rhs[m, r] + earlier(m, r) - kd * field[m, r] + k * around(self.beside, field, m, r)) * kinv

        return body

    def smoothed(self, out, field, defect, steps, plane):
        def body(r):
            q = self.co[plane, r]
            for t in steps:
                base = defect[t, r] if field is None else field[t, r] + defect[t, r]
                out[t, r] = base + q * around(self.beside, defect, t, r)

        return body

    def restricted(self, out, scaled, field, earlier, source, pairs):
        def body(r):
            c, d, kinv = self.co[C, r], self.co[D, r], self.co[KINV, r]
            for m in pairs:
                parts = [
                    source[t, r] + earlier(t, r) - d * field[t, r] + c * around(self.beside, field, t, r)
                    for t in (2 * m, 2 * m + 1)
                ]
                both = parts[0] + parts[1]
                out[m, r] = both
                scaled[m, r] = both * kinv

        return body


def edge_pack(is_first, is_odd, guess, source, start, conduct, near, far, gb, sb, tb, cb, sems):
    copies = []
    for n, (src, dst) in enumerate(((guess, gb), (source, sb), (start, tb), (conduct, cb))):
        for m, low in enumerate((0, 384)):
            copies.append(pltpu.make_async_copy(src.at[:, pl.ds(low, 128)], dst.at[:, m], sems.at[n, m]))
    for copy in copies:
        copy.start()
    for copy in copies:
        copy.wait()
    odd = is_odd[0]
    for out, side in ((near, 1 - odd), (far, odd)):

        def body(j, carry):
            r = j + 5 * side
            here = pl.ds((r // 8) * 64 + r % 8, 8, 8)
            for t in range(8):
                out[t, j] = gb[t, side, here, :]
                out[8 + t, j] = sb[t, side, here, :]
            out[16, j] = cb[0, side, here, :]
            out[17, j] = tb[0, side, here, :] * is_first[0]
            return carry

        lax.fori_loop(0, HALO, body, 0)


def last_step_pack(guess, source, conduct, out, g, e):
    beside = beside_maker()

    def fill(i, carry):
        for j in range(8):
            r = 8 * i + j
            for t in (6, 7):
                g[t - 6, r] = guess[tile_at(t, i, j), :]
            out[r] = g[1, r]
        return carry

    lax.fori_loop(0, ROWS // 8, fill, 0)

    def cond_at(r):
        return conduct[pl.ds((r // 8) * 64 + r % 8, 8, 8), :]

    def defect(i, carry):
        start = jnp.minimum(1 + i * 16, 63 - 16)
        for j in range(16):
            r = start + j
            c = cond_at(r)
            d = 1.0 + 4.0 * c
            right = source[pl.ds(7 * 512 + (r // 8) * 64 + r % 8, 8, 8), :]
            e[r] = (right + g[0, r] - d * g[1, r] + c * around(beside, g, 1, r)) * (DAMP / d)
        return carry

    lax.fori_loop(0, 4, defect, 0)

    def smooth(i, carry):
        start = jnp.minimum(2 + i * 16, 62 - 16)
        for j in range(16):
            r = start + j
            c = cond_at(r)
            q = c / (1.0 + 4.0 * c)
            out[ROWS - 2 + r] = g[1, r] + e[r] + q * (e[r - 1] + e[r + 1] + beside(e[r]))
        return carry

    lax.fori_loop(0, 4, smooth, 0)


def interior(is_first, guess, source, start, conduct, g, s, co, u, rs, e0, e1, tmp):
    beside = beside_maker()

    def fill(i, carry):
        for j in range(8):
            r = HALO + 8 * i + j
            for t in range(8):
                g[t, r] = guess[tile_at(t, i, j), :]
                s[t, r] = source[tile_at(t, i, j), :]
            coefficients(co, r, conduct[tile_at(0, i, j), :])
            co[ST, r] = start[tile_at(0, i, j), :] * is_first[0]
        return carry

    lax.fori_loop(0, ROWS // 8, fill, 0)
    st = Stages(beside, co)
    sweep(1, 63, 16, st.fine_defect(tmp, g, lambda t, r: g[t - 1, r], s, range(3, 8)))
    sweep(2, 62, 15, st.smoothed(u, g, tmp, range(3, 8), Q))
    sweep(3, 61, 15, st.restricted(rs, tmp, u, lambda t, r: u[t - 1, r], s, (2, 3)))
    sweep(4, 60, 28, st.smoothed(e0, None, tmp, (2, 3), KQ))
    sweep(5, 59, 27, st.coarse_defect(tmp, e0, lambda m, r: e0[m - 1, r], rs, (3,)))
    sweep(6, 58, 26, st.smoothed(e1, e0, tmp, (3,), KQ))


def edge_first(is_odd, near, far, g_in, s_in, co_in, u_in, g, s, co, u, out, tmp):
    del g_in, s_in, co_in, u_in
    beside = beside_maker()
    odd = is_odd[0]
    for source, side in ((near, 1 - odd), (far, odd)):
        low = side * (HALO + ROWS)

        def fill(j, carry):
            for t in range(8):
                g[t, low + j] = source[t, j]
                s[t, low + j] = source[8 + t, j]
            coefficients(co, low + j, source[16, j])
            co[ST, low + j] = source[17, j]
            return carry

        lax.fori_loop(0, HALO, fill, 0)
    st = Stages(beside, co)
    for low, high in ((-10, 3), (61, 74)):
        sweep(low, high, 16, st.fine_defect(tmp, g, lambda t, r: g[t - 1, r], s, (7,)))
    for low, high in ((-9, 2), (62, 73)):
        sweep(low, high, 16, st.smoothed(u, g, tmp, (7,), Q))
    for j in range(10):
        out[j] = g[7, HALO - 10 + j]
        out[10 + j] = g[7, HALO + ROWS + j]
        out[20 + j] = u[7, HALO - 8 + j]
        out[30 + j] = u[7, HALO + 62 + j]


def edges(g, s, co, u_in, rs_in, e0_in, e1_in, u, rs, e0, e1, out, tmp):
    del u_in, rs_in, e0_in, e1_in
    beside = beside_maker()
    st = Stages(beside, co)

    def both(inner, depth, unroll, body):
        sweep(-depth, inner, unroll, body)
        sweep(ROWS - inner, ROWS + depth, unroll, body)

    both(3, 10, 13, st.fine_defect(tmp, g, lambda t, r: g[t - 1, r], s, range(3, 7)))
    both(2, 9, 11, st.smoothed(u, g, tmp, range(3, 7), Q))
    both(3, 8, 11, st.restricted(rs, tmp, u, lambda t, r: u[t - 1, r], s, (2, 3)))

    def scale(r):
        for m in (2, 3):
            tmp[m, r] = rs[m, r] * co[KINV, r]

    sweep(3, 5, 2, scale)
    sweep(59, 61, 2, scale)
    both(4, 7, 11, st.smoothed(e0, None, tmp, (2, 3), KQ))
    both(7, 6, 13, st.coarse_defect(tmp, e0, lambda m, r: e0[m - 1, r], rs, (3,)))
    both(6, 5, 11, st.smoothed(e1, e0, tmp, (3,), KQ))

    def copy(i, carry):
        for j in range(19):
            r = i * 19 + j
            out[r] = e0[3, HALO - 6 + r]
            q = jnp.minimum(r, 71)
            out[76 + q] = e1[3, HALO - 4 + q]
        return carry

    lax.fori_loop(0, 4, copy, 0)


def rest(g, s, co, u_in, rs_in, e0_in, e1_in, u, rs, e0, e1, e2, tmp):
    del u_in, rs_in, e0_in, e1_in
    beside = beside_maker()
    st = Stages(beside, co)
    sweep(-10, 74, 28, st.fine_defect(tmp, g, lambda t, r: g[t - 1, r], s, (1, 2)))
    sweep(-9, 73, 28, st.smoothed(u, g, tmp, (1, 2), Q))
    sweep(-8, 72, 20, st.restricted(rs, tmp, u, lambda t, r: u[t - 1, r], s, (1,)))
    sweep(-7, 71, 26, st.smoothed(e0, None, tmp, (1,), KQ))
    sweep(-6, 70, 26, st.coarse_defect(tmp, e0, lambda m, r: e0[m - 1, r], rs, (2,)))
    sweep(-5, 69, 25, st.smoothed(e1, e0, tmp, (2,), KQ))
    sweep(-4, 68, 24, st.coarse_defect(tmp, e1, lambda m, r: e1[m - 1, r], rs, (3,)))
    sweep(-3, 67, 24, st.smoothed(e2, e1, tmp, (3,), KQ))


def middle(t0, t1, g, s, co, u_in, rs_in, e0_in, e1_in, e2_in, u, rs, e0, e1, e2, before, sol7, send, gb, tmp, u2):
    del u_in, rs_in, e0_in, e1_in, e2_in
    beside = beside_maker()
    st = Stages(beside, co)

    def fill(i, carry):
        for j in range(8):
            r = i * 8 + j
            gb[HALO + r] = t0[r] + co[ST, HALO + r]
            q = jnp.minimum(r, 59)
            before[HALO + 2 + q] = t0[ROWS + q] + co[ST, HALO + 2 + q]
        return carry

    lax.fori_loop(0, ROWS // 8, fill, 0)
    for j in range(10):
        gb[HALO - 10 + j] = t1[j] + co[ST, HALO - 10 + j]
        gb[HALO + ROWS + j] = t1[10 + j] + co[ST, HALO + ROWS + j]
        before[HALO - 8 + j] = t1[20 + j] + co[ST, HALO - 8 + j]
        before[HALO + 62 + j] = t1[30 + j] + co[ST, HALO + 62 + j]
    sweep(-10, 74, 28, st.fine_defect(tmp, g, lambda t, r: gb[r], s, (0,)))
    sweep(-9, 73, 28, st.smoothed(u, g, tmp, (0,), Q))
    sweep(-8, 72, 20, st.restricted(rs, tmp, u, lambda t, r: u[0, r] if t else before[r], s, (0,)))
    sweep(-7, 71, 26, st.smoothed(e0, None, tmp, (0,), KQ))
    sweep(-6, 70, 26, st.coarse_defect(tmp, e0, lambda m, r: e0[0, r], rs, (1,)))
    sweep(-5, 69, 25, st.smoothed(e1, e0, tmp, (1,), KQ))
    sweep(-4, 68, 24, st.coarse_defect(tmp, e1, lambda m, r: e1[1, r], rs, (2,)))

    def corrected(r):
        q = co[KQ, r]
        late = e1[2, r] + tmp[2, r] + q * around(beside, tmp, 2, r)
        e2[2, r] = late
        u2[0, r] = u[6, r] + 0.5 * (late + e2[3, r])
        u2[1, r] = u[7, r] + e2[3, r]

    sweep(-3, 67, 24, corrected)

    def defect(r):
        tmp[0, r] = (
            s[7, r] + u2[0, r] - co[D, r] * u2[1, r] + co[C, r] * around(beside, u2, 1, r)
        ) * co[INV, r]

    sweep(-2, 66, 23, defect)

    def final(r):
        sol7[0, r] = u2[1, r] + tmp[0, r] + co[Q, r] * around(beside, tmp, 0, r)

    sweep(-1, 65, 22, final)

    def copy(i, carry):
        for j in range(10):
            r = i * 10 + j
            send[r] = e2[3, HALO - 3 + r]
            q = jnp.minimum(r, 63)
            send[70 + q] = sol7[0, HALO + q]
        return carry

    lax.fori_loop(0, 7, copy, 0)


def late(t2, s, co, u, rs, e0, e1_in, e2_in, sol7, sol_out, res_out, u2_out, sol2, e1, u2, tmp, sol, sol_nat, res_nat, sems):
    beside = beside_maker()
    st = Stages(beside, co)

    def first_defect(r):
        tmp[0, r] = (
            rs[0, r] + t2[r - (HALO - 6)] - co[KD, r] * e0[0, r] + co[K, r] * around(beside, e0, 0, r)
        ) * co[KINV, r]

    sweep(-6, 70, 26, first_defect)

    def first_smooth(r):
        e1[0, r] = e0[0, r] + tmp[0, r] + co[KQ, r] * around(beside, tmp, 0, r)
        e1[1, r] = e1_in[1, r]

    sweep(-5, 69, 25, first_smooth)

    def second_defect(r):
        k, kd, kinv = co[K, r], co[KD, r], co[KINV, r]
        earlier = (t2[76 + r - (HALO - 4)], e1[0, r])
        for m in (0, 1):
            tmp[m, r] = (rs[m, r] + earlier[m] - kd * e1[m, r] + k * around(beside, e1, m, r)) * kinv

    sweep(-4, 68, 24, second_defect)

    def corrected(r):
        q = co[KQ, r]
        e20 = e1[0, r] + tmp[0, r] + q * around(beside, tmp, 0, r)
        e21 = e1[1, r] + tmp[1, r] + q * around(beside, tmp, 1, r)
        e22, e23 = e2_in[2, r], e2_in[3, r]
        u2_out[0, r] = u[0, r] + 0.5 * e20
        first = u[1, r] + e20
        u2_out[1, r] = first
        u2[1, r] = first
        u2[2, r] = u[2, r] + 0.5 * (e20 + e21)
        u2[3, r] = u[3, r] + e21
        u2[4, r] = u[4, r] + 0.5 * (e21 + e22)
        u2[5, r] = u[5, r] + e22
        u2[6, r] = u[6, r] + 0.5 * (e22 + e23)

    sweep(-3, 67, 18, corrected)
    sweep(-2, 66, 17, st.fine_defect(tmp, u2, lambda t, r: u2[t - 1, r], s, range(2, 7)))
    final = st.smoothed(sol, u2, tmp, range(2, 7), Q)

    def final_all(r):
        final(r)
        sol[7, r] = sol7[0, r]
        sol2[0, r] = sol[2, r]

    sweep(-1, 0, 1, final_all)
    sweep(64, 65, 1, final_all)

    def solve(i, carry):
        for h in range(2):
            for j in range(8):
                r = HALO + 16 * i + 8 * h + j
                final_all(r)
                for t in range(2, 8):
                    sol_nat[tile_at(t - 2, 2 * i + h, j), :] = sol[t, r]
        return carry

    lax.fori_loop(0, ROWS // 16, solve, 0)
    copy_sol = pltpu.make_async_copy(sol_nat, sol_out.at[pl.ds(2 * ROWS * 8, 6 * ROWS * 8)], sems.at[0])
    copy_sol.start()

    def resid(i, carry):
        for h in range(2):
            for j in range(8):
                r = HALO + 16 * i + 8 * h + j
                c, d = co[C, r], co[D, r]
                for t in range(3, 8):
                    res_nat[tile_at(t - 3, 2 * i + h, j), :] = (
                        s[t, r] + sol[t - 1, r] - d * sol[t, r] + c * around(beside, sol, t, r)
                    )
        return carry

    lax.fori_loop(0, ROWS // 16, resid, 0)
    copy_res = pltpu.make_async_copy(res_nat, res_out.at[pl.ds(3 * ROWS * 8, 5 * ROWS * 8)], sems.at[1])
    copy_res.start()
    copy_sol.wait()
    copy_res.wait()


def finish(t3, s, co, before, u2_in, sol2, sol_in, res_in, sol_out, res_out, u2, tmp, sol, sol_nat, res_nat, sems):
    del sol_in, res_in
    beside = beside_maker()

    def corrected(r):
        boundary = t3[r - (HALO - 3)]
        u2[0, r] = before[r] + boundary
        u2[1, r] = u2_in[0, r] + 0.5 * boundary

    sweep(-3, 67, 14, corrected)

    def defect(r):
        c, d, inv = co[C, r], co[D, r], co[INV, r]
        tmp[0, r] = (s[0, r] + u2[0, r] - d * u2[1, r] + c * around(beside, u2, 1, r)) * inv
        tmp[1, r] = (s[1, r] + u2[1, r] - d * u2_in[1, r] + c * around(beside, u2_in, 1, r)) * inv

    sweep(-2, 66, 34, defect)

    def final(r):
        q = co[Q, r]
        sol[0, r] = u2[1, r] + tmp[0, r] + q * around(beside, tmp, 0, r)
        sol[1, r] = u2_in[1, r] + tmp[1, r] + q * around(beside, tmp, 1, r)

    sweep(-1, 65, 33, final)

    def resid(i, carry):
        for h in range(4):
            for j in range(8):
                r = HALO + 32 * i + 8 * h + j
                c, d = co[C, r], co[D, r]
                spot = lambda t: tile_at(t, 4 * i + h, j)
                old = t3[r - HALO + 70] + co[ST, r]
                first, second = sol[0, r], sol[1, r]
                sol_nat[spot(0), :] = first
                sol_nat[spot(1), :] = second
                res_nat[spot(0), :] = s[0, r] + old - d * first + c * around(beside, sol, 0, r)
                res_nat[spot(1), :] = s[1, r] + first - d * second + c * around(beside, sol, 1, r)
                res_nat[spot(2), :] = s[2, r] + second - d * sol2[0, r] + c * around(beside, sol2, 0, r)
        return carry

    lax.fori_loop(0, ROWS // 32, resid, 0)
    copies = (
        pltpu.make_async_copy(sol_nat, sol_out.at[pl.ds(0, 2 * ROWS * 8)], sems.at[0]),
        pltpu.make_async_copy(res_nat, res_out.at[pl.ds(0, 3 * ROWS * 8)], sems.at[1]),
    )
    for copy in copies:
        copy.start()
    for copy in copies:
        copy.wait()


def call(kernel, ins, outs, scratch=(), aliases=None, specs=None, out_specs=None, limit=24):
    return pl.pallas_call(
        kernel,
        out_shape=outs,
        in_specs=specs or [FULL] * len(ins),
        out_specs=out_specs or [FULL] * len(outs),
        scratch_shapes=list(scratch),
        input_output_aliases=aliases or {},
        compiler_params=pltpu.CompilerParams(vmem_limit_bytes=limit * 2**20),
    )(*ins)


def along(block, axis, route):
    count = lax.axis_size(axis)
    pairs = [(i, route(i)) for i in range(count)]
    return lax.ppermute(block, axis, [(i, j) for i, j in pairs if 0 <= j < count])


def ahead(i):
    return i + 1


def on_chip(i):
    return i ^ 1


def off_chip(i):
    return ((i + 1) ^ 1) - 1


def cycle(source, guess, start_state, conduct):
    is_first = (lax.axis_index("tm") == 0).astype(F32).reshape(1)
    is_odd = (lax.axis_index("space") % 2).astype(jnp.int32).reshape(1)
    guess_v, source_v = view(guess), view(source)
    start_v, conduct_v = view(start_state[None]), view(conduct[None])
    halo = jax.ShapeDtypeStruct((18, HALO, 8, 128), F32)
    vmem = lambda steps: pltpu.VMEM((steps, EXT, 8, 128), F32)
    plain = lambda rows: pltpu.VMEM((rows * 8, 128), F32)
    dma = pltpu.SemaphoreType.DMA

    by_step = lambda x: pltpu.with_memory_space_constraint(x.reshape(-1, ROWS * 8, 128), pltpu.HBM)
    near, far = call(
        edge_pack,
        (is_first, is_odd, by_step(guess_v), by_step(source_v), by_step(start_v), by_step(conduct_v)),
        [halo, halo],
        [pltpu.VMEM((n, 2, 128, 128), F32) for n in (8, 8, 1, 1)] + [dma((4, 2))],
        specs=[SMEM, SMEM] + [ANY] * 4,
        limit=6,
    )
    far_in = along(far, "space", off_chip)
    near_in = along(near, "space", on_chip)
    (send0,) = call(
        last_step_pack,
        (guess_v, source_v, conduct_v),
        [rows_of(124)],
        [pltpu.VMEM((2, ROWS, 8, 128), F32), pltpu.VMEM((ROWS, 8, 128), F32)],
        limit=4,
    )
    t0 = along(send0, "tm", ahead)
    g, s, co, u, rs, e0, e1 = call(
        interior,
        (is_first, guess_v, source_v, start_v, conduct_v),
        [ext(8), ext(8), ext(9), ext(8), ext(4), ext(4), ext(4)],
        [vmem(8)],
        specs=[SMEM] + [FULL] * 4,
        limit=6,
    )
    g, s, co, u, send1 = call(
        edge_first,
        (is_odd, near_in, far_in, g, s, co, u),
        [ext(8), ext(8), ext(9), ext(8), rows_of(40)],
        [vmem(8)],
        aliases={3: 0, 4: 1, 5: 2, 6: 3},
        specs=[SMEM] + [FULL] * 6,
        limit=6,
    )
    t1 = along(send1, "tm", ahead)
    u, rs, e0, e1, send2 = call(
        edges,
        (g, s, co, u, rs, e0, e1),
        [ext(8), ext(4), ext(4), ext(4), rows_of(148)],
        [vmem(8)],
        aliases={3: 0, 4: 1, 5: 2, 6: 3},
        limit=6,
    )
    t2 = along(send2, "tm", ahead)
    u, rs, e0, e1, e2 = call(
        rest,
        (g, s, co, u, rs, e0, e1),
        [ext(8), ext(4), ext(4), ext(4), ext(4)],
        [vmem(4)],
        aliases={3: 0, 4: 1, 5: 2, 6: 3},
        limit=4,
    )
    u, rs, e0, e1, e2, before, sol7, send3 = call(
        middle,
        (t0, t1, g, s, co, u, rs, e0, e1, e2),
        [ext(8), ext(4), ext(4), ext(4), ext(4), rows_of(EXT), ext(1), rows_of(134)],
        [pltpu.VMEM((EXT, 8, 128), F32), vmem(4), vmem(2)],
        aliases={5: 0, 6: 1, 7: 2, 8: 3, 9: 4},
        limit=6,
    )
    t3 = along(send3, "tm", ahead)
    nat = jax.ShapeDtypeStruct((8 * ROWS * 8, 128), F32)
    sol, res, u2, sol2 = call(
        late,
        (t2, s, co, u, rs, e0, e1, e2, sol7),
        [nat, nat, ext(2), ext(1)],
        [vmem(2), vmem(8), vmem(8), vmem(8), plain(6 * ROWS), plain(5 * ROWS), dma((2,))],
        out_specs=[ANY, ANY, FULL, FULL],
        limit=16,
    )
    sol, res = call(
        finish,
        (t3, s, co, before, u2, sol2, sol, res),
        [nat, nat],
        [vmem(2), vmem(2), vmem(2), plain(2 * ROWS), plain(3 * ROWS), dma((2,))],
        aliases={6: 0, 7: 1},
        specs=[FULL] * 6 + [ANY] * 2,
        out_specs=[ANY, ANY],
        limit=6,
    )
    return unview(sol, 8), unview(res, 8)


def solution(mesh):
    return jax.shard_map(
        cycle,
        mesh=mesh,
        in_specs=(P("tm", "space", None), P("tm", "space", None), P("space", None), P("space", None)),
        out_specs=(P("tm", "space", None), P("tm", "space", None)),
        check_vma=False,
    )
```

time: 82.5 us -> 54.8 us (0.66)
  the two profiles are of different devices: /device:TPU:32 before, /device:TPU:91 now
where the time goes in v2:
time: 54.8 us; the launch traced here: 54.6 us
  Pallas kernels  26.9 us (49%)
  starting transfers between devices  14.5 us (26%)
  waiting for transfers between devices  12.3 us (22%)
  between operations  0.83 us (2%)
    pallas_call x9, Pallas kernels, call(): pl.pallas_call(kernel, out_shape=outs, in_specs=specs or [FULL] * len(ins...  26.9 us
    ppermute x6, starting transfers between devices, along(): lax.ppermute(block, axis, [(i, j) for i, j in pairs if 0 <= j < count])  14.5 us
    ppermute x6, waiting for transfers between devices, along(): lax.ppermute(block, axis, [(i, j) for i, j in pairs if 0 <= j < count])  12.3 us
  transfers between devices with their start and end apart: 6, of which 3 were waited for; matrix products, arithmetic and copies ran while one was open for 0% of the time, Pallas kernels for 40%

profile of v2, /device:TPU:91, one launch (start us, length us, event | category | flops | bytes accessed | tf_op | source)
XLA Modules:
  0.0 54.6 jit_solution(10881052788774851907)
XLA Ops:
  0.6 0.0 copy-start
  0.7 0.0 copy-start.1
  0.7 0.0 copy-start.2
  0.7 2.4 %shard_map.60 = (f32[18,11,8,128]{3,2,1,0:T(8,128)S(1)}, f32[18,11,8,128]{3,2,1,0:T(8,128)S(1)}) custom-call(f32[1]{0:T(128)} %bitcast.10.is_first, s32[1]{0:T(128)} %bitcast.9.is_odd, f32[8,512,128]{2,1,0:T(8,128)} %bitcast.40, f32[8,512,128]{2,1,0:T(8,128)} %bitcast.43, f32[1,512,128]{2,1,0:T(8,128)} %bitcast.49, f32[1,512,128]{2,1,0:T(8,128)} %bitcast.46), custom_call_target="tpu_custom_call" | custom-call | tf_op jit(solution)/shard_map/pallas_call | solution.py:495
  3.1 0.8 %collective-permute-start.1 = (f32[18,11,8,128]{3,2,1,0:T(8,128)S(1)}, f32[18,11,8,128]{3,2,1,0:T(8,128)S(1)}, u32[]{:S(2)}, u32[]{:S(2)}) collective-permute-start(f32[18,11,8,128]{3,2,1,0:T(8,128)S(1)} %get-tuple-element.40), channel_id=1, source_target_pairs={{0,1},{1,0},{2,3},{3,2},{4,5},{5,4},{6,7},{7,6},{8,9},{9,8},{10,11... | collective-permute-start | bytes 2433032 | tf_op jit(solution)/shard_map/ppermute | solution.py:509
  3.9 2.8 %collective-permute-start.2 = (f32[18,11,8,128]{3,2,1,0:T(8,128)S(1)}, f32[18,11,8,128]{3,2,1,0:T(8,128)S(1)}, u32[]{:S(2)}, u32[]{:S(2)}) collective-permute-start(f32[18,11,8,128]{3,2,1,0:T(8,128)S(1)} %get-tuple-element.41), channel_id=1, source_target_pairs={{1,2},{2,1},{3,4},{4,3},{5,6},{6,5},{7,8},{8,7},{9,10},{10,9},{11,... | collective-permute-start | bytes 2433032 | tf_op jit(solution)/shard_map/ppermute | solution.py:509
  6.7 0.0 copy-done
  6.7 0.0 copy-done.1
  6.7 0.0 copy-done.2
  6.7 0.0 copy-start.3
  6.7 1.1 %shard_map.59 = f32[124,8,128]{2,1,0:T(8,128)S(1)} custom-call(f32[4096,128]{1,0:T(8,128)S(1)} %bitcast.41, f32[4096,128]{1,0:T(8,128)S(1)} %bitcast.44, f32[512,128]{1,0:T(8,128)S(1)} %bitcast.47), custom_call_target="tpu_custom_call" | custom-call | tf_op jit(solution)/shard_map/pallas_call | solution.py:495
  7.8 3.1 %collective-permute-start = (f32[124,8,128]{2,1,0:T(8,128)S(1)}, f32[124,8,128]{2,1,0:T(8,128)S(1)}, u32[]{:S(2)}, u32[]{:S(2)}) collective-permute-start(f32[124,8,128]{2,1,0:T(8,128)S(1)} %shard_map.59), channel_id=1, source_target_pairs={{0,32},{32,64},{64,96},{1,33},{33,65},{65,97},{2,34},{34,66},{66,9... | collective-permute-start | bytes 1523720 | tf_op jit(solution)/shard_map/ppermute | solution.py:509
  10.9 0.0 copy-done.3
  10.9 4.7 %shard_map.61 = (f32[8,86,8,128]{3,2,1,0:T(8,128)S(1)}, f32[8,86,8,128]{3,2,1,0:T(8,128)S(1)}, f32[9,86,8,128]{3,2,1,0:T(8,128)S(1)}, f32[8,86,8,128]{3,2,1,0:T(...) custom-call(f32[1]{0:T(128)} %bitcast.10.is_first, ...), custom_call_target="tpu_custom_call" | custom-call | tf_op jit(solution)/shard_map/pallas_call | solution.py:495
  15.7 0.0 collective-permute-done.1.near
  15.7 3.9 %collective-permute-done.2.far = f32[18,11,8,128]{3,2,1,0:T(8,128)S(1)} collective-permute-done((f32[18,11,8,128]{3,2,1,0:T(8,128)S(1)}, f32[18,11,8,128]{3,2,1,0:T(8,128)S(1)}, u32[]{:S(2)}, u32[]{:S(2)}) %collective-permute-start.2) | collective-permute-done | bytes 811040 | tf_op jit(solution)/shard_map/ppermute | solution.py:509
  19.5 0.5 shard_map.62
  20.0 3.1 %collective-permute-start.3 = (f32[40,8,128]{2,1,0:T(8,128)S(1)}, f32[40,8,128]{2,1,0:T(8,128)S(1)}, u32[]{:S(2)}, u32[]{:S(2)}) collective-permute-start(f32[40,8,128]{2,1,0:T(8,128)S(1)} %get-tuple-element.46), channel_id=1, source_target_pairs={{0,32},{32,64},{64,96},{1,33},{33,65},{65,97},{2,34},{34,66},{66,9... | collective-permute-start | bytes 491528 | tf_op jit(solution)/shard_map/ppermute | solution.py:509
  23.2 1.1 %shard_map.63 = (f32[8,86,8,128]{3,2,1,0:T(8,128)S(1)}, f32[4,86,8,128]{3,2,1,0:T(8,128)S(1)}, f32[4,86,8,128]{3,2,1,0:T(8,128)S(1)}, f32[4,86,8,128]{3,2,1,0:T(8,128)S(1)}, f32[148,8,128]{2,1,0:T(8,128)S(1)}) custom-call(f32[8,86,8,128]{3,2,1,0:T(8,128)S(1)} %get-tuple-element.47.g, ...), custom_call_target="tpu_custom_call", output_to_operand_aliasing={{0}: (3, {}), {1}: (4, {}), {2}: (5, {}), {3}: (6, {})} | custom-call | tf_op jit(solution)/shard_map/pallas_call | solution.py:495
  24.3 2.8 %collective-permute-start.5 = (f32[148,8,128]{2,1,0:T(8,128)S(1)}, f32[148,8,128]{2,1,0:T(8,128)S(1)}, u32[]{:S(2)}, u32[]{:S(2)}) collective-permute-start(f32[148,8,128]{2,1,0:T(8,128)S(1)} %get-tuple-element.65), channel_id=1, source_target_pairs={{0,32},{32,64},{64,96},{1,33},{33,65},{65,97},{2,34},{34,66},{66,9... | collective-permute-start | bytes 1818632 | tf_op jit(solution)/shard_map/ppermute | solution.py:509
  27.2 3.8 %shard_map.64 = (f32[8,86,8,128]{3,2,1,0:T(8,128)S(1)}, f32[4,86,8,128]{3,2,1,0:T(8,128)S(1)}, f32[4,86,8,128]{3,2,1,0:T(8,128)S(1)}, f32[4,86,8,128]{3,2,1,0:T(8,128)S(1)}, f32[4,86,8,128]{3,2,1,0:T(8,128)S(1)}) custom-call(f32[8,86,8,128]{3,2,1,0:T(8,128)S(1)} %get-tuple-element.47.g, ...), custom_call_target="tpu_custom_call", output_to_operand_aliasing={{0}: (3, {}), {1}: (4, {}), {2}: (5, {}), {3}: (6, {})} | custom-call | tf_op jit(solution)/shard_map/pallas_call | solution.py:495
  31.0 0.0 collective-permute-done.t0
  31.0 0.0 collective-permute-done.3.t1
  31.0 4.5 %shard_map.65 = (f32[8,86,8,128]{3,2,1,0:T(8,128)S(1)}, f32[4,86,8,128]{3,2,1,0:T(8,128)S(1)}, f32[4,86,8,128]{3,2,1,0:T(8,128)S(1)}, f32[4,86,8,128]{3,2,1,0:T(...) custom-call(f32[124,8,128]{2,1,0:T(8,128)S(1)} %collective-permute-d, ...), custom_call_target="tpu_custom_call", output_to_operand_aliasing={{0}: (5, {}), {1}: (6, {}), {2}: (7, {}), {3}: (8, {}), {4}... | custom-call | tf_op jit(solution)/shard_map/pallas_call | solution.py:495
  35.5 1.9 %collective-permute-start.4 = (f32[134,8,128]{2,1,0:T(8,128)S(1)}, f32[134,8,128]{2,1,0:T(8,128)S(1)}, u32[]{:S(2)}, u32[]{:S(2)}) collective-permute-start(f32[134,8,128]{2,1,0:T(8,128)S(1)} %get-tuple-element.63), channel_id=1, source_target_pairs={{0,32},{32,64},{64,96},{1,33},{33,65},{65,97},{2,34},{34,66},{66,9... | collective-permute-start | bytes 1646600 | tf_op jit(solution)/shard_map/ppermute | solution.py:509
  37.4 4.5 %collective-permute-done.5.t2 = f32[148,8,128]{2,1,0:T(8,128)S(1)} collective-permute-done((f32[148,8,128]{2,1,0:T(8,128)S(1)}, f32[148,8,128]{2,1,0:T(8,128)S(1)}, u32[]{:S(2)}, u32[]{:S(2)}) %collective-permute-start.5) | collective-permute-done | bytes 606240 | tf_op jit(solution)/shard_map/ppermute | solution.py:509
  41.9 6.2 %shard_map.66 = (f32[4096,128]{1,0:T(8,128)}, f32[4096,128]{1,0:T(8,128)}, f32[2,86,8,128]{3,2,1,0:T(8,128)S(1)}, f32[1,86,8,128]{3,2,1,0:T(8,128)S(1)}) custom-call(f32[148,8,128]{2,1,0:T(8,128)S(1)} %collective-permute-done.5.t2, f32[8,86,8,128]{3,2,1,0:T(8,128)S(1)} %get-tuple-element.48.s, f32[9,86,8,128]{3,2,1,0:T(8,128)S(1)} %get-tuple-element.49.co, ...), custom_call_target="tpu_custom_call" | custom-call | tf_op jit(solution)/shard_map/pallas_call | solution.py:495
  48.1 4.0 %collective-permute-done.4.t3 = f32[134,8,128]{2,1,0:T(8,128)S(1)} collective-permute-done((f32[134,8,128]{2,1,0:T(8,128)S(1)}, f32[134,8,128]{2,1,0:T(8,128)S(1)}, u32[]{:S(2)}, u32[]{:S(2)}) %collective-permute-start.4) | collective-permute-done | bytes 548896 | tf_op jit(solution)/shard_map/ppermute | solution.py:509
  52.0 2.6 %shard_map.67 = (f32[4096,128]{1,0:T(8,128)}, f32[4096,128]{1,0:T(8,128)}) custom-call(f32[134,8,128]{2,1,0:T(8,128)S(1)} %collective-permute-done.4.t3, f32[8,86,8,128]{3,2,1,0:T(8,128)S(1)} %get-tuple-element.48.s, f32[9,86,8,128]{3,2,1,0:T(8,128)S(1)} %get-tuple-element.49.co, ...), custom_call_target="tpu_custom_call", output_to_operand_aliasing={{0}: (6, {}), {1}: (7, {})} | custom-call | tf_op jit(solution)/shard_map/pallas_call | solution.py:495
Async XLA Ops:
  0.6 6.0 %copy-start = (f32[8,64,1024]{2,1,0:T(8,128)S(1)}, f32[8,64,1024]{2,1,0:T(8,128)}, u32[]{:S(2)}) copy-start(f32[8,64,1024]{2,1,0:T(8,128)} %param.5) | copy-start | bytes 6291460
  0.7 6.0 %copy-start.1 = (f32[8,64,1024]{2,1,0:T(8,128)S(1)}, f32[8,64,1024]{2,1,0:T(8,128)}, u32[]{:S(2)}) copy-start(f32[8,64,1024]{2,1,0:T(8,128)} %param.4) | copy-start | bytes 6291460
  0.7 6.0 %copy-start.2 = (f32[64,1024]{1,0:T(8,128)S(1)}, f32[64,1024]{1,0:T(8,128)}, u32[]{:S(2)}) copy-start(f32[64,1024]{1,0:T(8,128)} %param.7) | copy-start | bytes 786436
  3.1 12.5 %collective-permute-start.1 = (f32[18,11,8,128]{3,2,1,0:T(8,128)S(1)}, f32[18,11,8,128]{3,2,1,0:T(8,128)S(1)}, u32[]{:S(2)}, u32[]{:S(2)}) collective-permute-start(f32[18,11,8,128]{3,2,1,0:T(8,128)S(1)} %get-tuple-element.40), channel_id=1, source_target_pairs={{0,1},{1,0},{2,3},{3,2},{4,5},{5,4},{6,7},{7,6},{8,9},{9,8},{10,11... | collective-permute-start | bytes 2433032 | tf_op jit(solution)/shard_map/ppermute | solution.py:509
  3.9 15.7 %collective-permute-start.2 = (f32[18,11,8,128]{3,2,1,0:T(8,128)S(1)}, f32[18,11,8,128]{3,2,1,0:T(8,128)S(1)}, u32[]{:S(2)}, u32[]{:S(2)}) collective-permute-start(f32[18,11,8,128]{3,2,1,0:T(8,128)S(1)} %get-tuple-element.41), channel_id=1, source_target_pairs={{1,2},{2,1},{3,4},{4,3},{5,6},{6,5},{7,8},{8,7},{9,10},{10,9},{11,... | collective-permute-start | bytes 2433032 | tf_op jit(solution)/shard_map/ppermute | solution.py:509
  6.7 4.2 %copy-start.3 = (f32[64,1024]{1,0:T(8,128)S(1)}, f32[64,1024]{1,0:T(8,128)}, u32[]{:S(2)}) copy-start(f32[64,1024]{1,0:T(8,128)} %param.6) | copy-start | bytes 786436
  7.8 23.2 %collective-permute-start = (f32[124,8,128]{2,1,0:T(8,128)S(1)}, f32[124,8,128]{2,1,0:T(8,128)S(1)}, u32[]{:S(2)}, u32[]{:S(2)}) collective-permute-start(f32[124,8,128]{2,1,0:T(8,128)S(1)} %shard_map.59), channel_id=1, source_target_pairs={{0,32},{32,64},{64,96},{1,33},{33,65},{65,97},{2,34},{34,66},{66,9... | collective-permute-start | bytes 1523720 | tf_op jit(solution)/shard_map/ppermute | solution.py:509
  20.0 10.9 %collective-permute-start.3 = (f32[40,8,128]{2,1,0:T(8,128)S(1)}, f32[40,8,128]{2,1,0:T(8,128)S(1)}, u32[]{:S(2)}, u32[]{:S(2)}) collective-permute-start(f32[40,8,128]{2,1,0:T(8,128)S(1)} %get-tuple-element.46), channel_id=1, source_target_pairs={{0,32},{32,64},{64,96},{1,33},{33,65},{65,97},{2,34},{34,66},{66,9... | collective-permute-start | bytes 491528 | tf_op jit(solution)/shard_map/ppermute | solution.py:509
  24.3 17.6 %collective-permute-start.5 = (f32[148,8,128]{2,1,0:T(8,128)S(1)}, f32[148,8,128]{2,1,0:T(8,128)S(1)}, u32[]{:S(2)}, u32[]{:S(2)}) collective-permute-start(f32[148,8,128]{2,1,0:T(8,128)S(1)} %get-tuple-element.65), channel_id=1, source_target_pairs={{0,32},{32,64},{64,96},{1,33},{33,65},{65,97},{2,34},{34,66},{66,9... | collective-permute-start | bytes 1818632 | tf_op jit(solution)/shard_map/ppermute | solution.py:509
  35.5 16.5 %collective-permute-start.4 = (f32[134,8,128]{2,1,0:T(8,128)S(1)}, f32[134,8,128]{2,1,0:T(8,128)S(1)}, u32[]{:S(2)}, u32[]{:S(2)}) collective-permute-start(f32[134,8,128]{2,1,0:T(8,128)S(1)} %get-tuple-element.63), channel_id=1, source_target_pairs={{0,32},{32,64},{64,96},{1,33},{33,65},{65,97},{2,34},{34,66},{66,9... | collective-permute-start | bytes 1646600 | tf_op jit(solution)/shard_map/ppermute | solution.py:509

commit v3 on v2

--- a/solution.py
+++ b/solution.py
@@ -146,17 +146,24 @@
     odd = is_odd[0]
     for out, side in ((near, 1 - odd), (far, odd)):
 
-        def body(j, carry):
+        def outer(j, carry):
             r = j + 5 * side
             here = pl.ds((r // 8) * 64 + r % 8, 8, 8)
             for t in range(8):
-                out[t, j] = gb[t, side, here, :]
-                out[8 + t, j] = sb[t, side, here, :]
-            out[16, j] = cb[0, side, here, :]
-            out[17, j] = tb[0, side, here, :] * is_first[0]
+                out[t * HALO + j] = gb[t, side, here, :]
             return carry
 
-        lax.fori_loop(0, HALO, body, 0)
+        def inner(j, carry):
+            r = j + 6 * side
+            here = pl.ds((r // 8) * 64 + r % 8, 8, 8)
+            for t in range(8):
+                out[8 * HALO + t * 10 + j] = sb[t, side, here, :]
+            out[8 * HALO + 80 + j] = cb[0, side, here, :]
+            out[8 * HALO + 90 + j] = tb[0, side, here, :] * is_first[0]
+            return carry
+
+        lax.fori_loop(0, HALO, outer, 0)
+        lax.fori_loop(0, 10, inner, 0)
 
 
 def last_step_pack(guess, source, conduct, out, g, e):
@@ -228,16 +235,22 @@
     odd = is_odd[0]
     for source, side in ((near, 1 - odd), (far, odd)):
         low = side * (HALO + ROWS)
-
-        def fill(j, carry):
+        low_inner = side * (HALO + ROWS - 1) + 1
+
+        def outer(j, carry):
             for t in range(8):
-                g[t, low + j] = source[t, j]
-                s[t, low + j] = source[8 + t, j]
-            coefficients(co, low + j, source[16, j])
-            co[ST, low + j] = source[17, j]
+                g[t, low + j] = source[t * HALO + j]
             return carry
 
-        lax.fori_loop(0, HALO, fill, 0)
+        def inner(j, carry):
+            for t in range(8):
+                s[t, low_inner + j] = source[8 * HALO + t * 10 + j]
+            coefficients(co, low_inner + j, source[8 * HALO + 80 + j])
+            co[ST, low_inner + j] = source[8 * HALO + 90 + j]
+            return carry
+
+        lax.fori_loop(0, HALO, outer, 0)
+        lax.fori_loop(0, 10, inner, 0)
     st = Stages(beside, co)
     for low, high in ((-10, 3), (61, 74)):
         sweep(low, high, 16, st.fine_defect(tmp, g, lambda t, r: g[t - 1, r], s, (7,)))
@@ -284,7 +297,7 @@
     lax.fori_loop(0, 4, copy, 0)
 
 
-def rest(g, s, co, u_in, rs_in, e0_in, e1_in, u, rs, e0, e1, e2, tmp):
+def rest(g, s, co, u_in, rs_in, e0_in, e1_in, u, rs, e0, e1, e2, send, tmp):
     del u_in, rs_in, e0_in, e1_in
     beside = beside_maker()
     st = Stages(beside, co)
@@ -295,7 +308,13 @@
     sweep(-6, 70, 26, st.coarse_defect(tmp, e0, lambda m, r: e0[m - 1, r], rs, (2,)))
     sweep(-5, 69, 25, st.smoothed(e1, e0, tmp, (2,), KQ))
     sweep(-4, 68, 24, st.coarse_defect(tmp, e1, lambda m, r: e1[m - 1, r], rs, (3,)))
-    sweep(-3, 67, 24, st.smoothed(e2, e1, tmp, (3,), KQ))
+    smooth = st.smoothed(e2, e1, tmp, (3,), KQ)
+
+    def final(r):
+        smooth(r)
+        send[r - (HALO - 3)] = e2[3, r]
+
+    sweep(-3, 67, 24, final)
 
 
 def middle(t0, t1, g, s, co, u_in, rs_in, e0_in, e1_in, e2_in, u, rs, e0, e1, e2, before, sol7, send, gb, tmp, u2):
@@ -347,14 +366,11 @@
     sweep(-1, 65, 22, final)
 
     def copy(i, carry):
-        for j in range(10):
-            r = i * 10 + j
-            send[r] = e2[3, HALO - 3 + r]
-            q = jnp.minimum(r, 63)
-            send[70 + q] = sol7[0, HALO + q]
-        return carry
-
-    lax.fori_loop(0, 7, copy, 0)
+        for j in range(8):
+            send[tile_at(0, i, j), :] = sol7[0, HALO + 8 * i + j]
+        return carry
+
+    lax.fori_loop(0, ROWS // 8, copy, 0)
 
 
 def late(t2, s, co, u, rs, e0, e1_in, e2_in, sol7, sol_out, res_out, u2_out, sol2, e1, u2, tmp, sol, sol_nat, res_nat, sems):
@@ -440,7 +456,7 @@
     copy_res.wait()
 
 
-def finish(t3, s, co, before, u2_in, sol2, sol_in, res_in, sol_out, res_out, u2, tmp, sol, sol_nat, res_nat, sems):
+def finish(t3, s, co, before, u2_in, sol2, sol_in, res_in, sol_out, res_out, base, u2, tmp, sol, sol_nat, res_nat, sems):
     del sol_in, res_in
     beside = beside_maker()
 
@@ -471,24 +487,31 @@
                 r = HALO + 32 * i + 8 * h + j
                 c, d = co[C, r], co[D, r]
                 spot = lambda t: tile_at(t, 4 * i + h, j)
-                old = t3[r - HALO + 70] + co[ST, r]
                 first, second = sol[0, r], sol[1, r]
                 sol_nat[spot(0), :] = first
                 sol_nat[spot(1), :] = second
-                res_nat[spot(0), :] = s[0, r] + old - d * first + c * around(beside, sol, 0, r)
-                res_nat[spot(1), :] = s[1, r] + first - d * second + c * around(beside, sol, 1, r)
-                res_nat[spot(2), :] = s[2, r] + second - d * sol2[0, r] + c * around(beside, sol2, 0, r)
+                base[spot(0), :] = s[0, r] + co[ST, r] - d * first + c * around(beside, sol, 0, r)
+                res_nat[spot(0), :] = s[1, r] + first - d * second + c * around(beside, sol, 1, r)
+                res_nat[spot(1), :] = s[2, r] + second - d * sol2[0, r] + c * around(beside, sol2, 0, r)
         return carry
 
     lax.fori_loop(0, ROWS // 32, resid, 0)
     copies = (
         pltpu.make_async_copy(sol_nat, sol_out.at[pl.ds(0, 2 * ROWS * 8)], sems.at[0]),
-        pltpu.make_async_copy(res_nat, res_out.at[pl.ds(0, 3 * ROWS * 8)], sems.at[1]),
+        pltpu.make_async_copy(res_nat, res_out.at[pl.ds(ROWS * 8, 2 * ROWS * 8)], sems.at[1]),
     )
     for copy in copies:
         copy.start()
     for copy in copies:
         copy.wait()
+
+
+def tail(t4, base, res_in, res_out, total, sem):
+    del res_in
+    total[...] = base[...] + t4[...]
+    copy = pltpu.make_async_copy(total, res_out.at[pl.ds(0, ROWS * 8)], sem)
+    copy.start()
+    copy.wait()
 
 
 def call(kernel, ins, outs, scratch=(), aliases=None, specs=None, out_specs=None, limit=24):
@@ -526,10 +549,12 @@
     is_odd = (lax.axis_index("space") % 2).astype(jnp.int32).reshape(1)
     guess_v, source_v = view(guess), view(source)
     start_v, conduct_v = view(start_state[None]), view(conduct[None])
-    halo = jax.ShapeDtypeStruct((18, HALO, 8, 128), F32)
+    halo = rows_of(8 * HALO + 100)
     vmem = lambda steps: pltpu.VMEM((steps, EXT, 8, 128), F32)
     plain = lambda rows: pltpu.VMEM((rows * 8, 128), F32)
     dma = pltpu.SemaphoreType.DMA
+    nat = jax.ShapeDtypeStruct((8 * ROWS * 8, 128), F32)
+    one = jax.ShapeDtypeStruct((ROWS * 8, 128), F32)
 
     by_step = lambda x: pltpu.with_memory_space_constraint(x.reshape(-1, ROWS * 8, 128), pltpu.HBM)
     near, far = call(
@@ -577,24 +602,24 @@
         limit=6,
     )
     t2 = along(send2, "tm", ahead)
-    u, rs, e0, e1, e2 = call(
+    u, rs, e0, e1, e2, send3 = call(
         rest,
         (g, s, co, u, rs, e0, e1),
-        [ext(8), ext(4), ext(4), ext(4), ext(4)],
+        [ext(8), ext(4), ext(4), ext(4), ext(4), rows_of(70)],
         [vmem(4)],
         aliases={3: 0, 4: 1, 5: 2, 6: 3},
         limit=4,
     )
-    u, rs, e0, e1, e2, before, sol7, send3 = call(
+    t3 = along(send3, "tm", ahead)
+    u, rs, e0, e1, e2, before, sol7, send4 = call(
         middle,
         (t0, t1, g, s, co, u, rs, e0, e1, e2),
-        [ext(8), ext(4), ext(4), ext(4), ext(4), rows_of(EXT), ext(1), rows_of(134)],
+        [ext(8), ext(4), ext(4), ext(4), ext(4), rows_of(EXT), ext(1), one],
         [pltpu.VMEM((EXT, 8, 128), F32), vmem(4), vmem(2)],
         aliases={5: 0, 6: 1, 7: 2, 8: 3, 9: 4},
         limit=6,
     )
-    t3 = along(send3, "tm", ahead)
-    nat = jax.ShapeDtypeStruct((8 * ROWS * 8, 128), F32)
+    t4 = along(send4, "tm", ahead)
     sol, res, u2, sol2 = call(
         late,
         (t2, s, co, u, rs, e0, e1, e2, sol7),
@@ -603,15 +628,25 @@
         out_specs=[ANY, ANY, FULL, FULL],
         limit=16,
     )
-    sol, res = call(
+    sol, res, base = call(
         finish,
         (t3, s, co, before, u2, sol2, sol, res),
-        [nat, nat],
-        [vmem(2), vmem(2), vmem(2), plain(2 * ROWS), plain(3 * ROWS), dma((2,))],
+        [nat, nat, one],
+        [vmem(2), vmem(2), vmem(2), plain(2 * ROWS), plain(2 * ROWS), dma((2,))],
         aliases={6: 0, 7: 1},
         specs=[FULL] * 6 + [ANY] * 2,
-        out_specs=[ANY, ANY],
+        out_specs=[ANY, ANY, FULL],
         limit=6,
+    )
+    (res,) = call(
+        tail,
+        (t4, base, res),
+        [nat],
+        [plain(ROWS), dma],
+        aliases={2: 0},
+        specs=[FULL, FULL, ANY],
+        out_specs=[ANY],
+        limit=2,
     )
     return unview(sol, 8), unview(res, 8)
 

time: 54.8 us -> 59.9 us (1.093)
  the two profiles are of different devices: /device:TPU:91 before, /device:TPU:64 now
where the time goes in v3:
time: 59.9 us; the launch traced here: 59.6 us
  Pallas kernels  27.7 us (46%)
  starting transfers between devices  22.4 us (37%)
  waiting for transfers between devices  8.63 us (14%)
  between operations  0.87 us (1%)
    pallas_call x10, Pallas kernels, call(): pl.pallas_call(kernel, out_shape=outs, in_specs=specs or [FULL] * len(ins...  27.7 us
    ppermute x7, starting transfers between devices, along(): lax.ppermute(block, axis, [(i, j) for i, j in pairs if 0 <= j < count])  22.4 us
    ppermute x7, waiting for transfers between devices, along(): lax.ppermute(block, axis, [(i, j) for i, j in pairs if 0 <= j < count])  8.63 us
  transfers between devices with their start and end apart: 7, of which 2 were waited for; matrix products, arithmetic and copies ran while one was open for 0% of the time, Pallas kernels for 41%

profile of v3, /device:TPU:64, one launch (start us, length us, event | category | flops | bytes accessed | tf_op | source)
XLA Modules:
  0.0 59.6 jit_solution(4599303812591721596)
XLA Ops:
  0.6 0.0 copy-start
  0.7 0.0 copy-start.1
  0.7 0.0 copy-start.2
  0.7 2.6 %shard_map.59 = (f32[188,8,128]{2,1,0:T(8,128)S(1)}, f32[188,8,128]{2,1,0:T(8,128)S(1)}) custom-call(f32[1]{0:T(128)} %bitcast.1.is_first, s32[1]{0:T(128)} %bitcast.is_odd, f32[8,512,128]{2,1,0:T(8,128)} %bitcast.40, f32[8,512,128]{2,1,0:T(8,128)} %bitcast.43, f32[1,512,128]{2,1,0:T(8,128)} %bitcast.49, f32[1,512,128]{2,1,0:T(8,128)} %bitcast.46), custom_call_target="tpu_custom_call" | custom-call | tf_op jit(solution)/shard_map/pallas_call | solution.py:518
  3.3 0.1 collective-permute-start
  3.4 4.6 %collective-permute-start.1 = (f32[188,8,128]{2,1,0:T(8,128)S(1)}, f32[188,8,128]{2,1,0:T(8,128)S(1)}, u32[]{:S(2)}, u32[]{:S(2)}) collective-permute-start(f32[188,8,128]{2,1,0:T(8,128)S(1)} %get-tuple-element.43), channel_id=1, source_target_pairs={{1,2},{2,1},{3,4},{4,3},{5,6},{6,5},{7,8},{8,7},{9,10},{10,9},{11,... | collective-permute-start | bytes 2310152 | tf_op jit(solution)/shard_map/ppermute | solution.py:532
  8.0 0.0 copy-done
  8.0 0.0 copy-done.1
  8.0 0.0 copy-done.2
  8.0 0.0 copy-start.3
  8.0 1.1 %shard_map.64 = f32[124,8,128]{2,1,0:T(8,128)S(1)} custom-call(f32[4096,128]{1,0:T(8,128)S(1)} %bitcast.41, f32[4096,128]{1,0:T(8,128)S(1)} %bitcast.44, f32[512,128]{1,0:T(8,128)S(1)} %bitcast.47), custom_call_target="tpu_custom_call" | custom-call | tf_op jit(solution)/shard_map/pallas_call | solution.py:518
  9.1 3.4 %collective-permute-start.3 = (f32[124,8,128]{2,1,0:T(8,128)S(1)}, f32[124,8,128]{2,1,0:T(8,128)S(1)}, u32[]{:S(2)}, u32[]{:S(2)}) collective-permute-start(f32[124,8,128]{2,1,0:T(8,128)S(1)} %shard_map.64), channel_id=1, source_target_pairs={{0,32},{32,64},{64,96},{1,33},{33,65},{65,97},{2,34},{34,66},{66,9... | collective-permute-start | bytes 1523720 | tf_op jit(solution)/shard_map/ppermute | solution.py:532
  12.5 0.0 copy-done.3
  12.5 4.7 %shard_map.60 = (f32[8,86,8,128]{3,2,1,0:T(8,128)S(1)}, f32[8,86,8,128]{3,2,1,0:T(8,128)S(1)}, f32[9,86,8,128]{3,2,1,0:T(8,128)S(1)}, f32[8,86,8,128]{3,2,1,0:T(...) custom-call(f32[1]{0:T(128)} %bitcast.1.is_first, ...), custom_call_target="tpu_custom_call" | custom-call | tf_op jit(solution)/shard_map/pallas_call | solution.py:518
  17.3 0.0 collective-permute-done.near
  17.3 1.4 %collective-permute-done.1.far = f32[188,8,128]{2,1,0:T(8,128)S(1)} collective-permute-done((f32[188,8,128]{2,1,0:T(8,128)S(1)}, f32[188,8,128]{2,1,0:T(8,128)S(1)}, u32[]{:S(2)}, u32[]{:S(2)}) %collective-permute-start.1) | collective-permute-done | bytes 770080 | tf_op jit(solution)/shard_map/ppermute | solution.py:532
  18.7 0.6 shard_map.61
  19.2 1.1 %shard_map.62 = (f32[8,86,8,128]{3,2,1,0:T(8,128)S(1)}, f32[4,86,8,128]{3,2,1,0:T(8,128)S(1)}, f32[4,86,8,128]{3,2,1,0:T(8,128)S(1)}, f32[4,86,8,128]{3,2,1,0:T(8,128)S(1)}, f32[148,8,128]{2,1,0:T(8,128)S(1)}) custom-call(f32[8,86,8,128]{3,2,1,0:T(8,128)S(1)} %get-tuple-element.48.g, ...), custom_call_target="tpu_custom_call", output_to_operand_aliasing={{0}: (3, {}), {1}: (4, {}), {2}: (5, {}), {3}: (6, {})} | custom-call | tf_op jit(solution)/shard_map/pallas_call | solution.py:518
  20.4 3.4 %collective-permute-start.5 = (f32[148,8,128]{2,1,0:T(8,128)S(1)}, f32[148,8,128]{2,1,0:T(8,128)S(1)}, u32[]{:S(2)}, u32[]{:S(2)}) collective-permute-start(f32[148,8,128]{2,1,0:T(8,128)S(1)} %get-tuple-element.67), channel_id=1, source_target_pairs={{0,32},{32,64},{64,96},{1,33},{33,65},{65,97},{2,34},{34,66},{66,9... | collective-permute-start | bytes 1818632 | tf_op jit(solution)/shard_map/ppermute | solution.py:532
  23.8 3.4 %collective-permute-start.4 = (f32[40,8,128]{2,1,0:T(8,128)S(1)}, f32[40,8,128]{2,1,0:T(8,128)S(1)}, u32[]{:S(2)}, u32[]{:S(2)}) collective-permute-start(f32[40,8,128]{2,1,0:T(8,128)S(1)} %get-tuple-element.60), channel_id=1, source_target_pairs={{0,32},{32,64},{64,96},{1,33},{33,65},{65,97},{2,34},{34,66},{66,9... | collective-permute-start | bytes 491528 | tf_op jit(solution)/shard_map/ppermute | solution.py:532
  27.2 3.8 %shard_map.63 = (f32[8,86,8,128]{3,2,1,0:T(8,128)S(1)}, f32[4,86,8,128]{3,2,1,0:T(8,128)S(1)}, f32[4,86,8,128]{3,2,1,0:T(8,128)S(1)}, f32[4,86,8,128]{3,2,1,0:T(...) custom-call(f32[8,86,8,128]{3,2,1,0:T(8,128)S(1)} %get-tuple-element, ...), custom_call_target="tpu_custom_call", output_to_operand_aliasing={{0}: (3, {}), {1}: (4, {}), {2}: (5, {}), {3}: (6, {})} | custom-call | tf_op jit(solution)/shard_map/pallas_call | solution.py:518
  31.0 3.1 %collective-permute-start.2 = (f32[70,8,128]{2,1,0:T(8,128)S(1)}, f32[70,8,128]{2,1,0:T(8,128)S(1)}, u32[]{:S(2)}, u32[]{:S(2)}) collective-permute-start(f32[70,8,128]{2,1,0:T(8,128)S(1)} %get-tuple-element.59), channel_id=1, source_target_pairs={{0,32},{32,64},{64,96},{1,33},{33,65},{65,97},{2,34},{34,66},{66,9... | collective-permute-start | bytes 860168 | tf_op jit(solution)/shard_map/ppermute | solution.py:532
  34.1 0.0 collective-permute-done.3.t0
  34.1 7.2 %collective-permute-done.4.t1 = f32[40,8,128]{2,1,0:T(8,128)S(1)} collective-permute-done((f32[40,8,128]{2,1,0:T(8,128)S(1)}, f32[40,8,128]{2,1,0:T(8,128)S(1)}, u32[]{:S(2)}, u32[]{:S(2)}) %collective-permute-start.4) | collective-permute-done | bytes 163872 | tf_op jit(solution)/shard_map/ppermute | solution.py:532
  41.3 4.4 %shard_map.65 = (f32[8,86,8,128]{3,2,1,0:T(8,128)S(1)}, f32[4,86,8,128]{3,2,1,0:T(8,128)S(1)}, f32[4,86,8,128]{3,2,1,0:T(8,128)S(1)}, f32[4,86,8,128]{3,2,1,0:T(...) custom-call(f32[124,8,128]{2,1,0:T(8,128)S(1)} %collective-permute-d, ...), custom_call_target="tpu_custom_call", output_to_operand_aliasing={{0}: (5, {}), {1}: (6, {}), {2}: (7, {}), {3}: (8, {}), {4}... | custom-call | tf_op jit(solution)/shard_map/pallas_call | solution.py:518
  45.8 4.4 %collective-permute-start.6 = (f32[512,128]{1,0:T(8,128)S(1)}, f32[512,128]{1,0:T(8,128)S(1)}, u32[]{:S(2)}, u32[]{:S(2)}) collective-permute-start(f32[512,128]{1,0:T(8,128)S(1)} %get-tuple-element.79), channel_id=1, source_target_pairs={{0,32},{32,64},{64,96},{1,33},{33,65},{65,97},{2,34},{34,66},{66,9... | collective-permute-start | bytes 786440 | tf_op jit(solution)/shard_map/ppermute | solution.py:532
  50.2 0.0 collective-permute-done.5.t2
  50.2 6.2 %shard_map.66 = (f32[4096,128]{1,0:T(8,128)}, f32[4096,128]{1,0:T(8,128)}, f32[2,86,8,128]{3,2,1,0:T(8,128)S(1)}, f32[1,86,8,128]{3,2,1,0:T(8,128)S(1)}) custom-call(f32[148,8,128]{2,1,0:T(8,128)S(1)} %collective-permute-done.5.t2, f32[8,86,8,128]{3,2,1,0:T(8,128)S(1)} %get-tuple-element.49.s, f32[9,86,8,128]{3,2,1,0:T(8,128)S(1)} %get-tuple-element.50.co, ...), custom_call_target="tpu_custom_call" | custom-call | tf_op jit(solution)/shard_map/pallas_call | solution.py:518
  56.4 0.0 collective-permute-done.2.t3
  56.4 2.5 %shard_map.67 = (f32[4096,128]{1,0:T(8,128)}, f32[4096,128]{1,0:T(8,128)}, f32[512,128]{1,0:T(8,128)S(1)}) custom-call(f32[70,8,128]{2,1,0:T(8,128)S(1)} %collective-permute-done.2.t3, f32[8,86,8,128]{3,2,1,0:T(8,128)S(1)} %get-tuple-element.49.s, f32[9,86,8,128]{3,2,1,0:T(8,128)S(1)} %get-tuple-element.50.co, ...), custom_call_target="tpu_custom_call", output_to_operand_aliasing={{0}: (6, {}), {1}: (7, {})} | custom-call | tf_op jit(solution)/shard_map/pallas_call | solution.py:518
  58.9 0.0 collective-permute-done.6.t4
  58.9 0.7 %shard_map.68 = f32[4096,128]{1,0:T(8,128)} custom-call(f32[512,128]{1,0:T(8,128)S(1)} %collective-permute-done.6.t4, f32[512,128]{1,0:T(8,128)S(1)} %get-tuple-element.80.base, f32[4096,128]{1,0:T(8,128)} %get-tuple-element.81.res_in), custom_call_target="tpu_custom_call", output_to_operand_aliasing={{}: (2, {})} | custom-call | tf_op jit(solution)/shard_map/pallas_call | solution.py:518
Async XLA Ops:
  0.6 7.3 %copy-start = (f32[8,64,1024]{2,1,0:T(8,128)S(1)}, f32[8,64,1024]{2,1,0:T(8,128)}, u32[]{:S(2)}) copy-start(f32[8,64,1024]{2,1,0:T(8,128)} %param.5) | copy-start | bytes 6291460
  0.7 7.3 %copy-start.1 = (f32[8,64,1024]{2,1,0:T(8,128)S(1)}, f32[8,64,1024]{2,1,0:T(8,128)}, u32[]{:S(2)}) copy-start(f32[8,64,1024]{2,1,0:T(8,128)} %param.4) | copy-start | bytes 6291460
  0.7 7.3 %copy-start.2 = (f32[64,1024]{1,0:T(8,128)S(1)}, f32[64,1024]{1,0:T(8,128)}, u32[]{:S(2)}) copy-start(f32[64,1024]{1,0:T(8,128)} %param.7) | copy-start | bytes 786436
  3.3 13.9 %collective-permute-start = (f32[188,8,128]{2,1,0:T(8,128)S(1)}, f32[188,8,128]{2,1,0:T(8,128)S(1)}, u32[]{:S(2)}, u32[]{:S(2)}) collective-permute-start(f32[188,8,128]{2,1,0:T(8,128)S(1)} %get-tuple-element.42), channel_id=1, source_target_pairs={{0,1},{1,0},{2,3},{3,2},{4,5},{5,4},{6,7},{7,6},{8,9},{9,8},{10,11... | collective-permute-start | bytes 2310152 | tf_op jit(solution)/shard_map/ppermute | solution.py:532
  3.4 15.2 %collective-permute-start.1 = (f32[188,8,128]{2,1,0:T(8,128)S(1)}, f32[188,8,128]{2,1,0:T(8,128)S(1)}, u32[]{:S(2)}, u32[]{:S(2)}) collective-permute-start(f32[188,8,128]{2,1,0:T(8,128)S(1)} %get-tuple-element.43), channel_id=1, source_target_pairs={{1,2},{2,1},{3,4},{4,3},{5,6},{6,5},{7,8},{8,7},{9,10},{10,9},{11,... | collective-permute-start | bytes 2310152 | tf_op jit(solution)/shard_map/ppermute | solution.py:532
  8.0 4.5 %copy-start.3 = (f32[64,1024]{1,0:T(8,128)S(1)}, f32[64,1024]{1,0:T(8,128)}, u32[]{:S(2)}) copy-start(f32[64,1024]{1,0:T(8,128)} %param.6) | copy-start | bytes 786436
  9.1 25.0 %collective-permute-start.3 = (f32[124,8,128]{2,1,0:T(8,128)S(1)}, f32[124,8,128]{2,1,0:T(8,128)S(1)}, u32[]{:S(2)}, u32[]{:S(2)}) collective-permute-start(f32[124,8,128]{2,1,0:T(8,128)S(1)} %shard_map.64), channel_id=1, source_target_pairs={{0,32},{32,64},{64,96},{1,33},{33,65},{65,97},{2,34},{34,66},{66,9... | collective-permute-start | bytes 1523720 | tf_op jit(solution)/shard_map/ppermute | solution.py:532
  20.4 29.8 %collective-permute-start.5 = (f32[148,8,128]{2,1,0:T(8,128)S(1)}, f32[148,8,128]{2,1,0:T(8,128)S(1)}, u32[]{:S(2)}, u32[]{:S(2)}) collective-permute-start(f32[148,8,128]{2,1,0:T(8,128)S(1)} %get-tuple-element.67), channel_id=1, source_target_pairs={{0,32},{32,64},{64,96},{1,33},{33,65},{65,97},{2,34},{34,66},{66,9... | collective-permute-start | bytes 1818632 | tf_op jit(solution)/shard_map/ppermute | solution.py:532
  23.8 17.5 %collective-permute-start.4 = (f32[40,8,128]{2,1,0:T(8,128)S(1)}, f32[40,8,128]{2,1,0:T(8,128)S(1)}, u32[]{:S(2)}, u32[]{:S(2)}) collective-permute-start(f32[40,8,128]{2,1,0:T(8,128)S(1)} %get-tuple-element.60), channel_id=1, source_target_pairs={{0,32},{32,64},{64,96},{1,33},{33,65},{65,97},{2,34},{34,66},{66,9... | collective-permute-start | bytes 491528 | tf_op jit(solution)/shard_map/ppermute | solution.py:532
  31.0 25.4 %collective-permute-start.2 = (f32[70,8,128]{2,1,0:T(8,128)S(1)}, f32[70,8,128]{2,1,0:T(8,128)S(1)}, u32[]{:S(2)}, u32[]{:S(2)}) collective-permute-start(f32[70,8,128]{2,1,0:T(8,128)S(1)} %get-tuple-element.59), channel_id=1, source_target_pairs={{0,32},{32,64},{64,96},{1,33},{33,65},{65,97},{2,34},{34,66},{66,9... | collective-permute-start | bytes 860168 | tf_op jit(solution)/shard_map/ppermute | solution.py:532
  45.8 13.1 %collective-permute-start.6 = (f32[512,128]{1,0:T(8,128)S(1)}, f32[512,128]{1,0:T(8,128)S(1)}, u32[]{:S(2)}, u32[]{:S(2)}) collective-permute-start(f32[512,128]{1,0:T(8,128)S(1)} %get-tuple-element.79), channel_id=1, source_target_pairs={{0,32},{32,64},{64,96},{1,33},{33,65},{65,97},{2,34},{34,66},{66,9... | collective-permute-start | bytes 786440 | tf_op jit(solution)/shard_map/ppermute | solution.py:532

commit v4 on v3

--- a/solution.py
+++ b/solution.py
@@ -32,6 +32,10 @@
 
 def unview(y, steps):
     return y.reshape(steps, ROWS // 8, 8, 8, 128).transpose(0, 1, 3, 2, 4).reshape(steps, ROWS, 1024)
+
+
+def at(ref, step, row):
+    return ref[pl.ds(step * ROWS * 8 + (row // 8) * 64 + row % 8, 8, 8), :]
 
 
 def tile_at(step, tile, row):
@@ -183,8 +187,8 @@
         return conduct[pl.ds((r // 8) * 64 + r % 8, 8, 8), :]
 
     def defect(i, carry):
-        start = jnp.minimum(1 + i * 16, 63 - 16)
-        for j in range(16):
+        start = 1 + i * 31
+        for j in range(31):
             r = start + j
             c = cond_at(r)
             d = 1.0 + 4.0 * c
@@ -192,18 +196,22 @@
             e[r] = (right + g[0, r] - d * g[1, r] + c * around(beside, g, 1, r)) * (DAMP / d)
         return carry
 
-    lax.fori_loop(0, 4, defect, 0)
+    lax.fori_loop(0, 2, defect, 0)
 
     def smooth(i, carry):
-        start = jnp.minimum(2 + i * 16, 62 - 16)
-        for j in range(16):
+        start = 2 + i * 30
+        for j in range(30):
             r = start + j
             c = cond_at(r)
             q = c / (1.0 + 4.0 * c)
             out[ROWS - 2 + r] = g[1, r] + e[r] + q * (e[r - 1] + e[r + 1] + beside(e[r]))
         return carry
 
-    lax.fori_loop(0, 4, smooth, 0)
+    lax.fori_loop(0, 2, smooth, 0)
+    for n, r in enumerate((0, ROWS - 1)):
+        out[124 + n] = at(source, 7, r) + g[0, r]
+    for n, r in enumerate((1, 2, 61, 62)):
+        out[126 + n] = e[r]
 
 
 def interior(is_first, guess, source, start, conduct, g, s, co, u, rs, e0, e1, tmp):
@@ -229,8 +237,8 @@
     sweep(6, 58, 26, st.smoothed(e1, e0, tmp, (3,), KQ))
 
 
-def edge_first(is_odd, near, far, g_in, s_in, co_in, u_in, g, s, co, u, out, tmp):
-    del g_in, s_in, co_in, u_in
+def edges(is_odd, near, far, g_in, s_in, co_in, u_in, rs_in, e0_in, e1_in, g, s, co, u, rs, e0, e1, out, tmp):
+    del g_in, s_in, co_in, u_in, rs_in, e0_in, e1_in
     beside = beside_maker()
     odd = is_odd[0]
     for source, side in ((near, 1 - odd), (far, odd)):
@@ -252,28 +260,13 @@
         lax.fori_loop(0, HALO, outer, 0)
         lax.fori_loop(0, 10, inner, 0)
     st = Stages(beside, co)
-    for low, high in ((-10, 3), (61, 74)):
-        sweep(low, high, 16, st.fine_defect(tmp, g, lambda t, r: g[t - 1, r], s, (7,)))
-    for low, high in ((-9, 2), (62, 73)):
-        sweep(low, high, 16, st.smoothed(u, g, tmp, (7,), Q))
-    for j in range(10):
-        out[j] = g[7, HALO - 10 + j]
-        out[10 + j] = g[7, HALO + ROWS + j]
-        out[20 + j] = u[7, HALO - 8 + j]
-        out[30 + j] = u[7, HALO + 62 + j]
-
-
-def edges(g, s, co, u_in, rs_in, e0_in, e1_in, u, rs, e0, e1, out, tmp):
-    del u_in, rs_in, e0_in, e1_in
-    beside = beside_maker()
-    st = Stages(beside, co)
 
     def both(inner, depth, unroll, body):
         sweep(-depth, inner, unroll, body)
         sweep(ROWS - inner, ROWS + depth, unroll, body)
 
-    both(3, 10, 13, st.fine_defect(tmp, g, lambda t, r: g[t - 1, r], s, range(3, 7)))
-    both(2, 9, 11, st.smoothed(u, g, tmp, range(3, 7), Q))
+    both(3, 10, 13, st.fine_defect(tmp, g, lambda t, r: g[t - 1, r], s, range(3, 8)))
+    both(2, 9, 11, st.smoothed(u, g, tmp, range(3, 8), Q))
     both(3, 8, 11, st.restricted(rs, tmp, u, lambda t, r: u[t - 1, r], s, (2, 3)))
 
     def scale(r):
@@ -301,48 +294,77 @@
     del u_in, rs_in, e0_in, e1_in
     beside = beside_maker()
     st = Stages(beside, co)
-    sweep(-10, 74, 28, st.fine_defect(tmp, g, lambda t, r: g[t - 1, r], s, (1, 2)))
-    sweep(-9, 73, 28, st.smoothed(u, g, tmp, (1, 2), Q))
-    sweep(-8, 72, 20, st.restricted(rs, tmp, u, lambda t, r: u[t - 1, r], s, (1,)))
-    sweep(-7, 71, 26, st.smoothed(e0, None, tmp, (1,), KQ))
-    sweep(-6, 70, 26, st.coarse_defect(tmp, e0, lambda m, r: e0[m - 1, r], rs, (2,)))
-    sweep(-5, 69, 25, st.smoothed(e1, e0, tmp, (2,), KQ))
-    sweep(-4, 68, 24, st.coarse_defect(tmp, e1, lambda m, r: e1[m - 1, r], rs, (3,)))
+    sweep(-10, 74, 42, st.fine_defect(tmp, g, lambda t, r: g[t - 1, r], s, (1, 2)))
+    sweep(-9, 73, 41, st.smoothed(u, g, tmp, (1, 2), Q))
+    sweep(-8, 72, 90, st.restricted(rs, tmp, u, lambda t, r: u[t - 1, r], s, (1,)))
+    sweep(-7, 71, 90, st.smoothed(e0, None, tmp, (1,), KQ))
+    sweep(-6, 70, 90, st.coarse_defect(tmp, e0, lambda m, r: e0[m - 1, r], rs, (2,)))
+    sweep(-5, 69, 90, st.smoothed(e1, e0, tmp, (2,), KQ))
+    sweep(-4, 68, 90, st.coarse_defect(tmp, e1, lambda m, r: e1[m - 1, r], rs, (3,)))
     smooth = st.smoothed(e2, e1, tmp, (3,), KQ)
 
     def final(r):
         smooth(r)
         send[r - (HALO - 3)] = e2[3, r]
 
-    sweep(-3, 67, 24, final)
-
-
-def middle(t0, t1, g, s, co, u_in, rs_in, e0_in, e1_in, e2_in, u, rs, e0, e1, e2, before, sol7, send, gb, tmp, u2):
+    sweep(-3, 67, 90, final)
+
+
+def relay(is_odd, t0, near, far):
+    odd = is_odd[0]
+    for out, side in ((near, 1 - odd), (far, odd)):
+        for j in range(10):
+            out[j] = t0[54 * side + j]
+        for j in range(6):
+            out[10 + j] = t0[ROWS + 54 * side + j]
+        for j in range(2):
+            out[16 + j] = t0[126 + 2 * side + j]
+        out[18] = t0[124 + side]
+
+
+def middle(
+    is_odd, t0, near, far, g, s, co, u_in, rs_in, e0_in, e1_in, e2_in,
+    u, rs, e0, e1, e2, before, sol7, send, gb, er, br, tmp, u2,
+):
     del u_in, rs_in, e0_in, e1_in, e2_in
     beside = beside_maker()
     st = Stages(beside, co)
+    odd = is_odd[0]
 
     def fill(i, carry):
-        for j in range(8):
-            r = i * 8 + j
-            gb[HALO + r] = t0[r] + co[ST, HALO + r]
+        for j in range(16):
+            r = i * 16 + j
+            gb[0, HALO + r] = t0[r]
             q = jnp.minimum(r, 59)
             before[HALO + 2 + q] = t0[ROWS + q] + co[ST, HALO + 2 + q]
         return carry
 
-    lax.fori_loop(0, ROWS // 8, fill, 0)
-    for j in range(10):
-        gb[HALO - 10 + j] = t1[j] + co[ST, HALO - 10 + j]
-        gb[HALO + ROWS + j] = t1[10 + j] + co[ST, HALO + ROWS + j]
-        before[HALO - 8 + j] = t1[20 + j] + co[ST, HALO - 8 + j]
-        before[HALO + 62 + j] = t1[30 + j] + co[ST, HALO + 62 + j]
-    sweep(-10, 74, 28, st.fine_defect(tmp, g, lambda t, r: gb[r], s, (0,)))
-    sweep(-9, 73, 28, st.smoothed(u, g, tmp, (0,), Q))
-    sweep(-8, 72, 20, st.restricted(rs, tmp, u, lambda t, r: u[0, r] if t else before[r], s, (0,)))
-    sweep(-7, 71, 26, st.smoothed(e0, None, tmp, (0,), KQ))
-    sweep(-6, 70, 26, st.coarse_defect(tmp, e0, lambda m, r: e0[0, r], rs, (1,)))
-    sweep(-5, 69, 25, st.smoothed(e1, e0, tmp, (1,), KQ))
-    sweep(-4, 68, 24, st.coarse_defect(tmp, e1, lambda m, r: e1[1, r], rs, (2,)))
+    lax.fori_loop(0, ROWS // 16, fill, 0)
+    for source, side in ((near, 1 - odd), (far, odd)):
+        for j in range(10):
+            gb[0, 1 + 74 * side + j] = source[j]
+        for j in range(6):
+            r = 3 + 74 * side + j
+            before[r] = source[10 + j] + co[ST, r]
+        for j in range(2):
+            er[8 + 68 * side + j] = source[16 + j]
+        br[10 + 65 * side] = source[18]
+    for n, r in enumerate((HALO, HALO + 63)):
+        br[r] = t0[124 + n]
+    for n, r in enumerate((1, 2, 61, 62)):
+        er[HALO + r] = t0[126 + n]
+    for r in (10, 11, 74, 75):
+        er[r] = (br[r] - co[D, r] * gb[0, r] + co[C, r] * around(beside, gb, 0, r)) * co[INV, r]
+    for r in (9, 10, 11, 12, 73, 74, 75, 76):
+        edge = gb[0, r] + er[r] + co[Q, r] * (er[r - 1] + er[r + 1] + beside(er[r]))
+        before[r] = edge + co[ST, r]
+    sweep(-10, 74, 90, st.fine_defect(tmp, g, lambda t, r: gb[0, r] + co[ST, r], s, (0,)))
+    sweep(-9, 73, 90, st.smoothed(u, g, tmp, (0,), Q))
+    sweep(-8, 72, 90, st.restricted(rs, tmp, u, lambda t, r: u[0, r] if t else before[r], s, (0,)))
+    sweep(-7, 71, 90, st.smoothed(e0, None, tmp, (0,), KQ))
+    sweep(-6, 70, 90, st.coarse_defect(tmp, e0, lambda m, r: e0[0, r], rs, (1,)))
+    sweep(-5, 69, 90, st.smoothed(e1, e0, tmp, (1,), KQ))
+    sweep(-4, 68, 90, st.coarse_defect(tmp, e1, lambda m, r: e1[1, r], rs, (2,)))
 
     def corrected(r):
         q = co[KQ, r]
@@ -351,19 +373,19 @@
         u2[0, r] = u[6, r] + 0.5 * (late + e2[3, r])
         u2[1, r] = u[7, r] + e2[3, r]
 
-    sweep(-3, 67, 24, corrected)
+    sweep(-3, 67, 90, corrected)
 
     def defect(r):
         tmp[0, r] = (
             s[7, r] + u2[0, r] - co[D, r] * u2[1, r] + co[C, r] * around(beside, u2, 1, r)
         ) * co[INV, r]
 
-    sweep(-2, 66, 23, defect)
+    sweep(-2, 66, 90, defect)
 
     def final(r):
         sol7[0, r] = u2[1, r] + tmp[0, r] + co[Q, r] * around(beside, tmp, 0, r)
 
-    sweep(-1, 65, 22, final)
+    sweep(-1, 65, 90, final)
 
     def copy(i, carry):
         for j in range(8):
@@ -570,7 +592,7 @@
     (send0,) = call(
         last_step_pack,
         (guess_v, source_v, conduct_v),
-        [rows_of(124)],
+        [rows_of(130)],
         [pltpu.VMEM((2, ROWS, 8, 128), F32), pltpu.VMEM((ROWS, 8, 128), F32)],
         limit=4,
     )
@@ -583,25 +605,19 @@
         specs=[SMEM] + [FULL] * 4,
         limit=6,
     )
-    g, s, co, u, send1 = call(
-        edge_first,
-        (is_odd, near_in, far_in, g, s, co, u),
-        [ext(8), ext(8), ext(9), ext(8), rows_of(40)],
+    g, s, co, u, rs, e0, e1, send2 = call(
+        edges,
+        (is_odd, near_in, far_in, g, s, co, u, rs, e0, e1),
+        [ext(8), ext(8), ext(9), ext(8), ext(4), ext(4), ext(4), rows_of(148)],
         [vmem(8)],
-        aliases={3: 0, 4: 1, 5: 2, 6: 3},
-        specs=[SMEM] + [FULL] * 6,
+        aliases={n + 3: n for n in range(7)},
+        specs=[SMEM] + [FULL] * 9,
         limit=6,
     )
-    t1 = along(send1, "tm", ahead)
-    u, rs, e0, e1, send2 = call(
-        edges,
-        (g, s, co, u, rs, e0, e1),
-        [ext(8), ext(4), ext(4), ext(4), rows_of(148)],
-        [vmem(8)],
-        aliases={3: 0, 4: 1, 5: 2, 6: 3},
-        limit=6,
-    )
     t2 = along(send2, "tm", ahead)
+    near, far = call(relay, (is_odd, t0), [rows_of(19), rows_of(19)], specs=[SMEM, FULL], limit=1)
+    far_in = along(far, "space", off_chip)
+    near_in = along(near, "space", on_chip)
     u, rs, e0, e1, e2, send3 = call(
         rest,
         (g, s, co, u, rs, e0, e1),
@@ -613,10 +629,11 @@
     t3 = along(send3, "tm", ahead)
     u, rs, e0, e1, e2, before, sol7, send4 = call(
         middle,
-        (t0, t1, g, s, co, u, rs, e0, e1, e2),
+        (is_odd, t0, near_in, far_in, g, s, co, u, rs, e0, e1, e2),
         [ext(8), ext(4), ext(4), ext(4), ext(4), rows_of(EXT), ext(1), one],
-        [pltpu.VMEM((EXT, 8, 128), F32), vmem(4), vmem(2)],
-        aliases={5: 0, 6: 1, 7: 2, 8: 3, 9: 4},
+        [vmem(1), pltpu.VMEM((EXT, 8, 128), F32), pltpu.VMEM((EXT, 8, 128), F32), vmem(4), vmem(2)],
+        aliases={n + 7: n for n in range(5)},
+        specs=[SMEM] + [FULL] * 11,
         limit=6,
     )
     t4 = along(send4, "tm", ahead)

time: 59.9 us -> 50.1 us (0.84)
  the two profiles are of different devices: /device:TPU:64 before, /device:TPU:96 now
where the time goes in v4:
time: 50.1 us; the launch traced here: 49.8 us
  Pallas kernels  24.3 us (49%)
  starting transfers between devices  23.4 us (47%)
  waiting for transfers between devices  1.21 us (2%)
  between operations  0.89 us (2%)
    pallas_call x10, Pallas kernels, call(): pl.pallas_call(kernel, out_shape=outs, in_specs=specs or [FULL] * len(ins...  24.3 us
    ppermute x8, starting transfers between devices, along(): lax.ppermute(block, axis, [(i, j) for i, j in pairs if 0 <= j < count])  23.4 us
    ppermute x8, waiting for transfers between devices, along(): lax.ppermute(block, axis, [(i, j) for i, j in pairs if 0 <= j < count])  1.21 us
  transfers between devices with their start and end apart: 8, of which 1 were waited for; matrix products, arithmetic and copies ran while one was open for 0% of the time, Pallas kernels for 42%

profile of v4, /device:TPU:96, one launch (start us, length us, event | category | flops | bytes accessed | tf_op | source)
XLA Modules:
  0.0 49.8 jit_solution(12866062158642800161)
XLA Ops:
  0.6 0.0 copy-start
  0.7 0.0 copy-start.1
  0.7 0.0 copy-start.2
  0.7 2.6 %shard_map.59 = (f32[188,8,128]{2,1,0:T(8,128)S(1)}, f32[188,8,128]{2,1,0:T(8,128)S(1)}) custom-call(f32[1]{0:T(128)} %bitcast.1.is_first, s32[1]{0:T(128)} %bitcast.is_odd, f32[8,512,128]{2,1,0:T(8,128)} %bitcast.40, f32[8,512,128]{2,1,0:T(8,128)} %bitcast.43, f32[1,512,128]{2,1,0:T(8,128)} %bitcast.49, f32[1,512,128]{2,1,0:T(8,128)} %bitcast.46), custom_call_target="tpu_custom_call" | custom-call | tf_op jit(solution)/shard_map/pallas_call | solution.py:540
  3.3 0.1 collective-permute-start
  3.4 4.9 %collective-permute-start.1 = (f32[188,8,128]{2,1,0:T(8,128)S(1)}, f32[188,8,128]{2,1,0:T(8,128)S(1)}, u32[]{:S(2)}, u32[]{:S(2)}) collective-permute-start(f32[188,8,128]{2,1,0:T(8,128)S(1)} %get-tuple-element.43), channel_id=1, source_target_pairs={{1,2},{2,1},{3,4},{4,3},{5,6},{6,5},{7,8},{8,7},{9,10},{10,9},{11,... | collective-permute-start | bytes 2310152 | tf_op jit(solution)/shard_map/ppermute | solution.py:554
  8.3 0.0 copy-done
  8.3 0.0 copy-done.1
  8.3 0.0 copy-done.2
  8.3 0.0 copy-start.3
  8.3 1.0 %shard_map.63 = f32[130,8,128]{2,1,0:T(8,128)S(1)} custom-call(f32[4096,128]{1,0:T(8,128)S(1)} %bitcast.41, f32[4096,128]{1,0:T(8,128)S(1)} %bitcast.44, f32[512,128]{1,0:T(8,128)S(1)} %bitcast.47), custom_call_target="tpu_custom_call" | custom-call | tf_op jit(solution)/shard_map/pallas_call | solution.py:540
  9.3 3.4 %collective-permute-start.3 = (f32[130,8,128]{2,1,0:T(8,128)S(1)}, f32[130,8,128]{2,1,0:T(8,128)S(1)}, u32[]{:S(2)}, u32[]{:S(2)}) collective-permute-start(f32[130,8,128]{2,1,0:T(8,128)S(1)} %shard_map.63), channel_id=1, source_target_pairs={{0,32},{32,64},{64,96},{1,33},{33,65},{65,97},{2,34},{34,66},{66,9... | collective-permute-start | bytes 1597448 | tf_op jit(solution)/shard_map/ppermute | solution.py:554
  12.7 0.0 copy-done.3
  12.7 4.7 %shard_map.60 = (f32[8,86,8,128]{3,2,1,0:T(8,128)S(1)}, f32[8,86,8,128]{3,2,1,0:T(8,128)S(1)}, f32[9,86,8,128]{3,2,1,0:T(8,128)S(1)}, f32[8,86,8,128]{3,2,1,0:T(...) custom-call(f32[1]{0:T(128)} %bitcast.1.is_first, ...), custom_call_target="tpu_custom_call" | custom-call | tf_op jit(solution)/shard_map/pallas_call | solution.py:540
  17.5 0.0 collective-permute-done.near
  17.5 1.2 %collective-permute-done.1.far = f32[188,8,128]{2,1,0:T(8,128)S(1)} collective-permute-done((f32[188,8,128]{2,1,0:T(8,128)S(1)}, f32[188,8,128]{2,1,0:T(8,128)S(1)}, u32[]{:S(2)}, u32[]{:S(2)}) %collective-permute-start.1) | collective-permute-done | bytes 770080 | tf_op jit(solution)/shard_map/ppermute | solution.py:554
  18.7 1.6 %shard_map.61 = (f32[8,86,8,128]{3,2,1,0:T(8,128)S(1)}, f32[8,86,8,128]{3,2,1,0:T(8,128)S(1)}, f32[9,86,8,128]{3,2,1,0:T(8,128)S(1)}, f32[8,86,8,128]{3,2,1,0:T(...) custom-call(s32[1]{0:T(128)} %bitcast.is_odd, ...), custom_call_target="tpu_custom_call", output_to_operand_aliasing={{0}: (3, {}), {1}: (4, {}), {2}: (5, {}), {3}: (6, {}), {4}... | custom-call | tf_op jit(solution)/shard_map/pallas_call | solution.py:540
  20.3 3.4 %collective-permute-start.6 = (f32[148,8,128]{2,1,0:T(8,128)S(1)}, f32[148,8,128]{2,1,0:T(8,128)S(1)}, u32[]{:S(2)}, u32[]{:S(2)}) collective-permute-start(f32[148,8,128]{2,1,0:T(8,128)S(1)} %get-tuple-element.67), channel_id=1, source_target_pairs={{0,32},{32,64},{64,96},{1,33},{33,65},{65,97},{2,34},{34,66},{66,9... | collective-permute-start | bytes 1818632 | tf_op jit(solution)/shard_map/ppermute | solution.py:554
  23.7 0.0 collective-permute-done.3.t0
  23.8 0.1 collective-permute-start.4
  23.9 4.6 %collective-permute-start.5 = (f32[19,8,128]{2,1,0:T(8,128)S(1)}, f32[19,8,128]{2,1,0:T(8,128)S(1)}, u32[]{:S(2)}, u32[]{:S(2)}) collective-permute-start(f32[19,8,128]{2,1,0:T(8,128)S(1)} %get-tuple-element.60), channel_id=1, source_target_pairs={{1,2},{2,1},{3,4},{4,3},{5,6},{6,5},{7,8},{8,7},{9,10},{10,9},{11,... | collective-permute-start | bytes 233480 | tf_op jit(solution)/shard_map/ppermute | solution.py:554
  28.5 2.4 %shard_map.62 = (f32[8,86,8,128]{3,2,1,0:T(8,128)S(1)}, f32[4,86,8,128]{3,2,1,0:T(8,128)S(1)}, f32[4,86,8,128]{3,2,1,0:T(8,128)S(1)}, f32[4,86,8,128]{3,2,1,0:T(...) custom-call(f32[8,86,8,128]{3,2,1,0:T(8,128)S(1)} %get-tuple-element, ...), custom_call_target="tpu_custom_call", output_to_operand_aliasing={{0}: (3, {}), {1}: (4, {}), {2}: (5, {}), {3}: (6, {})} | custom-call | tf_op jit(solution)/shard_map/pallas_call | solution.py:540
  30.9 3.6 %collective-permute-start.2 = (f32[70,8,128]{2,1,0:T(8,128)S(1)}, f32[70,8,128]{2,1,0:T(8,128)S(1)}, u32[]{:S(2)}, u32[]{:S(2)}) collective-permute-start(f32[70,8,128]{2,1,0:T(8,128)S(1)} %get-tuple-element.58), channel_id=1, source_target_pairs={{0,32},{32,64},{64,96},{1,33},{33,65},{65,97},{2,34},{34,66},{66,9... | collective-permute-start | bytes 860168 | tf_op jit(solution)/shard_map/ppermute | solution.py:554
  34.4 0.0 collective-permute-done.4.near
  34.4 0.0 collective-permute-done.5.far
  34.5 2.5 %shard_map.65 = (f32[8,86,8,128]{3,2,1,0:T(8,128)S(1)}, f32[4,86,8,128]{3,2,1,0:T(8,128)S(1)}, f32[4,86,8,128]{3,2,1,0:T(8,128)S(1)}, f32[4,86,8,128]{3,2,1,0:T(...) custom-call(s32[1]{0:T(128)} %bitcast.is_odd, ...), custom_call_target="tpu_custom_call", output_to_operand_aliasing={{0}: (7, {}), {1}: (8, {}), {2}: (9, {}), {3}: (10, {}), {4... | custom-call | tf_op jit(solution)/shard_map/pallas_call | solution.py:540
  37.0 3.4 %collective-permute-start.7 = (f32[512,128]{1,0:T(8,128)S(1)}, f32[512,128]{1,0:T(8,128)S(1)}, u32[]{:S(2)}, u32[]{:S(2)}) collective-permute-start(f32[512,128]{1,0:T(8,128)S(1)} %get-tuple-element.79), channel_id=1, source_target_pairs={{0,32},{32,64},{64,96},{1,33},{33,65},{65,97},{2,34},{34,66},{66,9... | collective-permute-start | bytes 786440 | tf_op jit(solution)/shard_map/ppermute | solution.py:554
  40.4 0.0 collective-permute-done.6.t2
  40.4 6.2 %shard_map.66 = (f32[4096,128]{1,0:T(8,128)}, f32[4096,128]{1,0:T(8,128)}, f32[2,86,8,128]{3,2,1,0:T(8,128)S(1)}, f32[1,86,8,128]{3,2,1,0:T(8,128)S(1)}) custom-call(f32[148,8,128]{2,1,0:T(8,128)S(1)} %collective-permute-done.6.t2, f32[8,86,8,128]{3,2,1,0:T(8,128)S(1)} %get-tuple-element.52.s, f32[9,86,8,128]{3,2,1,0:T(8,128)S(1)} %get-tuple-element.53.co, ...), custom_call_target="tpu_custom_call" | custom-call | tf_op jit(solution)/shard_map/pallas_call | solution.py:540
  46.6 0.0 collective-permute-done.2.t3
  46.6 2.5 %shard_map.67 = (f32[4096,128]{1,0:T(8,128)}, f32[4096,128]{1,0:T(8,128)}, f32[512,128]{1,0:T(8,128)S(1)}) custom-call(f32[70,8,128]{2,1,0:T(8,128)S(1)} %collective-permute-done.2.t3, f32[8,86,8,128]{3,2,1,0:T(8,128)S(1)} %get-tuple-element.52.s, f32[9,86,8,128]{3,2,1,0:T(8,128)S(1)} %get-tuple-element.53.co, ...), custom_call_target="tpu_custom_call", output_to_operand_aliasing={{0}: (6, {}), {1}: (7, {})} | custom-call | tf_op jit(solution)/shard_map/pallas_call | solution.py:540
  49.0 0.0 collective-permute-done.7.t4
  49.1 0.7 %shard_map.68 = f32[4096,128]{1,0:T(8,128)} custom-call(f32[512,128]{1,0:T(8,128)S(1)} %collective-permute-done.7.t4, f32[512,128]{1,0:T(8,128)S(1)} %get-tuple-element.80.base, f32[4096,128]{1,0:T(8,128)} %get-tuple-element.81.res_in), custom_call_target="tpu_custom_call", output_to_operand_aliasing={{}: (2, {})} | custom-call | tf_op jit(solution)/shard_map/pallas_call | solution.py:540
  (1 shorter events, 0.0 us)
Async XLA Ops:
  0.6 7.6 %copy-start = (f32[8,64,1024]{2,1,0:T(8,128)S(1)}, f32[8,64,1024]{2,1,0:T(8,128)}, u32[]{:S(2)}) copy-start(f32[8,64,1024]{2,1,0:T(8,128)} %param.5) | copy-start | bytes 6291460
  0.7 7.6 %copy-start.1 = (f32[8,64,1024]{2,1,0:T(8,128)S(1)}, f32[8,64,1024]{2,1,0:T(8,128)}, u32[]{:S(2)}) copy-start(f32[8,64,1024]{2,1,0:T(8,128)} %param.4) | copy-start | bytes 6291460
  0.7 7.6 %copy-start.2 = (f32[64,1024]{1,0:T(8,128)S(1)}, f32[64,1024]{1,0:T(8,128)}, u32[]{:S(2)}) copy-start(f32[64,1024]{1,0:T(8,128)} %param.7) | copy-start | bytes 786436
  3.3 14.1 %collective-permute-start = (f32[188,8,128]{2,1,0:T(8,128)S(1)}, f32[188,8,128]{2,1,0:T(8,128)S(1)}, u32[]{:S(2)}, u32[]{:S(2)}) collective-permute-start(f32[188,8,128]{2,1,0:T(8,128)S(1)} %get-tuple-element.42), channel_id=1, source_target_pairs={{0,1},{1,0},{2,3},{3,2},{4,5},{5,4},{6,7},{7,6},{8,9},{9,8},{10,11... | collective-permute-start | bytes 2310152 | tf_op jit(solution)/shard_map/ppermute | solution.py:554
  3.4 15.2 %collective-permute-start.1 = (f32[188,8,128]{2,1,0:T(8,128)S(1)}, f32[188,8,128]{2,1,0:T(8,128)S(1)}, u32[]{:S(2)}, u32[]{:S(2)}) collective-permute-start(f32[188,8,128]{2,1,0:T(8,128)S(1)} %get-tuple-element.43), channel_id=1, source_target_pairs={{1,2},{2,1},{3,4},{4,3},{5,6},{6,5},{7,8},{8,7},{9,10},{10,9},{11,... | collective-permute-start | bytes 2310152 | tf_op jit(solution)/shard_map/ppermute | solution.py:554
  8.3 4.4 %copy-start.3 = (f32[64,1024]{1,0:T(8,128)S(1)}, f32[64,1024]{1,0:T(8,128)}, u32[]{:S(2)}) copy-start(f32[64,1024]{1,0:T(8,128)} %param.6) | copy-start | bytes 786436
  9.3 14.5 %collective-permute-start.3 = (f32[130,8,128]{2,1,0:T(8,128)S(1)}, f32[130,8,128]{2,1,0:T(8,128)S(1)}, u32[]{:S(2)}, u32[]{:S(2)}) collective-permute-start(f32[130,8,128]{2,1,0:T(8,128)S(1)} %shard_map.63), channel_id=1, source_target_pairs={{0,32},{32,64},{64,96},{1,33},{33,65},{65,97},{2,34},{34,66},{66,9... | collective-permute-start | bytes 1597448 | tf_op jit(solution)/shard_map/ppermute | solution.py:554
  20.3 20.1 %collective-permute-start.6 = (f32[148,8,128]{2,1,0:T(8,128)S(1)}, f32[148,8,128]{2,1,0:T(8,128)S(1)}, u32[]{:S(2)}, u32[]{:S(2)}) collective-permute-start(f32[148,8,128]{2,1,0:T(8,128)S(1)} %get-tuple-element.67), channel_id=1, source_target_pairs={{0,32},{32,64},{64,96},{1,33},{33,65},{65,97},{2,34},{34,66},{66,9... | collective-permute-start | bytes 1818632 | tf_op jit(solution)/shard_map/ppermute | solution.py:554
  23.8 10.7 %collective-permute-start.4 = (f32[19,8,128]{2,1,0:T(8,128)S(1)}, f32[19,8,128]{2,1,0:T(8,128)S(1)}, u32[]{:S(2)}, u32[]{:S(2)}) collective-permute-start(f32[19,8,128]{2,1,0:T(8,128)S(1)} %get-tuple-element.59), channel_id=1, source_target_pairs={{0,1},{1,0},{2,3},{3,2},{4,5},{5,4},{6,7},{7,6},{8,9},{9,8},{10,11... | collective-permute-start | bytes 233480 | tf_op jit(solution)/shard_map/ppermute | solution.py:554
  23.9 10.6 %collective-permute-start.5 = (f32[19,8,128]{2,1,0:T(8,128)S(1)}, f32[19,8,128]{2,1,0:T(8,128)S(1)}, u32[]{:S(2)}, u32[]{:S(2)}) collective-permute-start(f32[19,8,128]{2,1,0:T(8,128)S(1)} %get-tuple-element.60), channel_id=1, source_target_pairs={{1,2},{2,1},{3,4},{4,3},{5,6},{6,5},{7,8},{8,7},{9,10},{10,9},{11,... | collective-permute-start | bytes 233480 | tf_op jit(solution)/shard_map/ppermute | solution.py:554
  30.9 15.7 %collective-permute-start.2 = (f32[70,8,128]{2,1,0:T(8,128)S(1)}, f32[70,8,128]{2,1,0:T(8,128)S(1)}, u32[]{:S(2)}, u32[]{:S(2)}) collective-permute-start(f32[70,8,128]{2,1,0:T(8,128)S(1)} %get-tuple-element.58), channel_id=1, source_target_pairs={{0,32},{32,64},{64,96},{1,33},{33,65},{65,97},{2,34},{34,66},{66,9... | collective-permute-start | bytes 860168 | tf_op jit(solution)/shard_map/ppermute | solution.py:554
  37.0 12.1 %collective-permute-start.7 = (f32[512,128]{1,0:T(8,128)S(1)}, f32[512,128]{1,0:T(8,128)S(1)}, u32[]{:S(2)}, u32[]{:S(2)}) collective-permute-start(f32[512,128]{1,0:T(8,128)S(1)} %get-tuple-element.79), channel_id=1, source_target_pairs={{0,32},{32,64},{64,96},{1,33},{33,65},{65,97},{2,34},{34,66},{66,9... | collective-permute-start | bytes 786440 | tf_op jit(solution)/shard_map/ppermute | solution.py:554

commit v5 on v4

--- a/solution.py
+++ b/solution.py
@@ -139,35 +139,43 @@
 
 
 def edge_pack(is_first, is_odd, guess, source, start, conduct, near, far, gb, sb, tb, cb, sems):
-    copies = []
-    for n, (src, dst) in enumerate(((guess, gb), (source, sb), (start, tb), (conduct, cb))):
-        for m, low in enumerate((0, 384)):
-            copies.append(pltpu.make_async_copy(src.at[:, pl.ds(low, 128)], dst.at[:, m], sems.at[n, m]))
-    for copy in copies:
+    pairs = ((guess, gb), (source, sb), (start, tb), (conduct, cb))
+
+    def copies(spans):
+        return [
+            pltpu.make_async_copy(src.at[:, pl.ds(low, size)], dst.at[:, pl.ds(low, size)], sems.at[n, k])
+            for k, low, size in spans
+            for n, (src, dst) in enumerate(pairs)
+        ]
+
+    outer_tiles, inner_tiles = copies(((0, 0, 128), (1, 384, 128))), copies(((2, 128, 256),))
+    for copy in outer_tiles + inner_tiles:
         copy.start()
-    for copy in copies:
+    for copy in outer_tiles:
         copy.wait()
     odd = is_odd[0]
     for out, side in ((near, 1 - odd), (far, odd)):
 
         def outer(j, carry):
-            r = j + 5 * side
+            r = j + 53 * side
             here = pl.ds((r // 8) * 64 + r % 8, 8, 8)
             for t in range(8):
-                out[t * HALO + j] = gb[t, side, here, :]
+                out[t * HALO + j] = gb[t, here, :]
             return carry
 
         def inner(j, carry):
-            r = j + 6 * side
+            r = j + 54 * side
             here = pl.ds((r // 8) * 64 + r % 8, 8, 8)
             for t in range(8):
-                out[8 * HALO + t * 10 + j] = sb[t, side, here, :]
-            out[8 * HALO + 80 + j] = cb[0, side, here, :]
-            out[8 * HALO + 90 + j] = tb[0, side, here, :] * is_first[0]
+                out[8 * HALO + t * 10 + j] = sb[t, here, :]
+            out[8 * HALO + 80 + j] = cb[0, here, :]
+            out[8 * HALO + 90 + j] = tb[0, here, :] * is_first[0]
             return carry
 
         lax.fori_loop(0, HALO, outer, 0)
         lax.fori_loop(0, 10, inner, 0)
+    for copy in inner_tiles:
+        copy.wait()
 
 
 def last_step_pack(guess, source, conduct, out, g, e):
@@ -229,12 +237,12 @@
 
     lax.fori_loop(0, ROWS // 8, fill, 0)
     st = Stages(beside, co)
-    sweep(1, 63, 16, st.fine_defect(tmp, g, lambda t, r: g[t - 1, r], s, range(3, 8)))
-    sweep(2, 62, 15, st.smoothed(u, g, tmp, range(3, 8), Q))
-    sweep(3, 61, 15, st.restricted(rs, tmp, u, lambda t, r: u[t - 1, r], s, (2, 3)))
-    sweep(4, 60, 28, st.smoothed(e0, None, tmp, (2, 3), KQ))
-    sweep(5, 59, 27, st.coarse_defect(tmp, e0, lambda m, r: e0[m - 1, r], rs, (3,)))
-    sweep(6, 58, 26, st.smoothed(e1, e0, tmp, (3,), KQ))
+    sweep(1, 63, 90, st.fine_defect(tmp, g, lambda t, r: g[t - 1, r], s, range(3, 8)))
+    sweep(2, 62, 90, st.smoothed(u, g, tmp, range(3, 8), Q))
+    sweep(3, 61, 90, st.restricted(rs, tmp, u, lambda t, r: u[t - 1, r], s, (2, 3)))
+    sweep(4, 60, 90, st.smoothed(e0, None, tmp, (2, 3), KQ))
+    sweep(5, 59, 90, st.coarse_defect(tmp, e0, lambda m, r: e0[m - 1, r], rs, (3,)))
+    sweep(6, 58, 90, st.smoothed(e1, e0, tmp, (3,), KQ))
 
 
 def edges(is_odd, near, far, g_in, s_in, co_in, u_in, rs_in, e0_in, e1_in, g, s, co, u, rs, e0, e1, out, tmp):
@@ -404,13 +412,13 @@
             rs[0, r] + t2[r - (HALO - 6)] - co[KD, r] * e0[0, r] + co[K, r] * around(beside, e0, 0, r)
         ) * co[KINV, r]
 
-    sweep(-6, 70, 26, first_defect)
+    sweep(-6, 70, 90, first_defect)
 
     def first_smooth(r):
         e1[0, r] = e0[0, r] + tmp[0, r] + co[KQ, r] * around(beside, tmp, 0, r)
         e1[1, r] = e1_in[1, r]
 
-    sweep(-5, 69, 25, first_smooth)
+    sweep(-5, 69, 90, first_smooth)
 
     def second_defect(r):
         k, kd, kinv = co[K, r], co[KD, r], co[KINV, r]
@@ -418,7 +426,7 @@
         for m in (0, 1):
             tmp[m, r] = (rs[m, r] + earlier[m] - kd * e1[m, r] + k * around(beside, e1, m, r)) * kinv
 
-    sweep(-4, 68, 24, second_defect)
+    sweep(-4, 68, 90, second_defect)
 
     def corrected(r):
         q = co[KQ, r]
@@ -435,8 +443,8 @@
         u2[5, r] = u[5, r] + e22
         u2[6, r] = u[6, r] + 0.5 * (e22 + e23)
 
-    sweep(-3, 67, 18, corrected)
-    sweep(-2, 66, 17, st.fine_defect(tmp, u2, lambda t, r: u2[t - 1, r], s, range(2, 7)))
+    sweep(-3, 67, 90, corrected)
+    sweep(-2, 66, 90, st.fine_defect(tmp, u2, lambda t, r: u2[t - 1, r], s, range(2, 7)))
     final = st.smoothed(sol, u2, tmp, range(2, 7), Q)
 
     def final_all(r):
@@ -444,42 +452,35 @@
         sol[7, r] = sol7[0, r]
         sol2[0, r] = sol[2, r]
 
-    sweep(-1, 0, 1, final_all)
-    sweep(64, 65, 1, final_all)
-
-    def solve(i, carry):
-        for h in range(2):
+    sweep(-1, 0, 90, final_all)
+    sweep(64, 65, 90, final_all)
+
+    for i in range(ROWS // 8):
+        for j in range(8):
+            r = HALO + 8 * i + j
+            final_all(r)
+            for t in range(2, 8):
+                sol_nat[t - 2, tile_at(0, i, j), :] = sol[t, r]
+    copies = [pltpu.make_async_copy(sol_nat, sol_out.at[pl.ds(2, 6)], sems.at[0])]
+    copies[0].start()
+    for part in range(2):
+        for i in range(4 * part, 4 * part + 4):
             for j in range(8):
-                r = HALO + 16 * i + 8 * h + j
-                final_all(r)
-                for t in range(2, 8):
-                    sol_nat[tile_at(t - 2, 2 * i + h, j), :] = sol[t, r]
-        return carry
-
-    lax.fori_loop(0, ROWS // 16, solve, 0)
-    copy_sol = pltpu.make_async_copy(sol_nat, sol_out.at[pl.ds(2 * ROWS * 8, 6 * ROWS * 8)], sems.at[0])
-    copy_sol.start()
-
-    def resid(i, carry):
-        for h in range(2):
-            for j in range(8):
-                r = HALO + 16 * i + 8 * h + j
+                r = HALO + 8 * i + j
                 c, d = co[C, r], co[D, r]
                 for t in range(3, 8):
-                    res_nat[tile_at(t - 3, 2 * i + h, j), :] = (
+                    res_nat[t - 3, tile_at(0, i, j), :] = (
                         s[t, r] + sol[t - 1, r] - d * sol[t, r] + c * around(beside, sol, t, r)
                     )
-        return carry
-
-    lax.fori_loop(0, ROWS // 16, resid, 0)
-    copy_res = pltpu.make_async_copy(res_nat, res_out.at[pl.ds(3 * ROWS * 8, 5 * ROWS * 8)], sems.at[1])
-    copy_res.start()
-    copy_sol.wait()
-    copy_res.wait()
-
-
-def finish(t3, s, co, before, u2_in, sol2, sol_in, res_in, sol_out, res_out, base, u2, tmp, sol, sol_nat, res_nat, sems):
-    del sol_in, res_in
+        rows = pl.ds(part * ROWS * 4, ROWS * 4)
+        copies.append(pltpu.make_async_copy(res_nat.at[:, rows], res_out.at[pl.ds(3, 5), rows], sems.at[1 + part]))
+        copies[-1].start()
+    for copy in copies:
+        copy.wait()
+
+
+def finish(t3, s, co, before, u2_in, sol2, sol_in, sol_out, res, u2, tmp, sol, sol_nat, sem):
+    del sol_in
     beside = beside_maker()
 
     def corrected(r):
@@ -487,52 +488,47 @@
         u2[0, r] = before[r] + boundary
         u2[1, r] = u2_in[0, r] + 0.5 * boundary
 
-    sweep(-3, 67, 14, corrected)
+    sweep(-3, 67, 90, corrected)
 
     def defect(r):
         c, d, inv = co[C, r], co[D, r], co[INV, r]
         tmp[0, r] = (s[0, r] + u2[0, r] - d * u2[1, r] + c * around(beside, u2, 1, r)) * inv
         tmp[1, r] = (s[1, r] + u2[1, r] - d * u2_in[1, r] + c * around(beside, u2_in, 1, r)) * inv
 
-    sweep(-2, 66, 34, defect)
+    sweep(-2, 66, 90, defect)
 
     def final(r):
         q = co[Q, r]
         sol[0, r] = u2[1, r] + tmp[0, r] + q * around(beside, tmp, 0, r)
         sol[1, r] = u2_in[1, r] + tmp[1, r] + q * around(beside, tmp, 1, r)
-
-    sweep(-1, 65, 33, final)
-
-    def resid(i, carry):
-        for h in range(4):
-            for j in range(8):
-                r = HALO + 32 * i + 8 * h + j
-                c, d = co[C, r], co[D, r]
-                spot = lambda t: tile_at(t, 4 * i + h, j)
-                first, second = sol[0, r], sol[1, r]
-                sol_nat[spot(0), :] = first
-                sol_nat[spot(1), :] = second
-                base[spot(0), :] = s[0, r] + co[ST, r] - d * first + c * around(beside, sol, 0, r)
-                res_nat[spot(0), :] = s[1, r] + first - d * second + c * around(beside, sol, 1, r)
-                res_nat[spot(1), :] = s[2, r] + second - d * sol2[0, r] + c * around(beside, sol2, 0, r)
-        return carry
-
-    lax.fori_loop(0, ROWS // 32, resid, 0)
-    copies = (
-        pltpu.make_async_copy(sol_nat, sol_out.at[pl.ds(0, 2 * ROWS * 8)], sems.at[0]),
-        pltpu.make_async_copy(res_nat, res_out.at[pl.ds(ROWS * 8, 2 * ROWS * 8)], sems.at[1]),
-    )
-    for copy in copies:
-        copy.start()
-    for copy in copies:
-        copy.wait()
-
-
-def tail(t4, base, res_in, res_out, total, sem):
+        if HALO <= r < HALO + ROWS:
+            sol_nat[0, tile_at(0, (r - HALO) // 8, (r - HALO) % 8), :] = sol[0, r]
+            sol_nat[1, tile_at(0, (r - HALO) // 8, (r - HALO) % 8), :] = sol[1, r]
+
+    sweep(-1, 65, 90, final)
+
+    copy = pltpu.make_async_copy(sol_nat, sol_out.at[pl.ds(0, 2)], sem)
+    copy.start()
+    for i in range(ROWS // 8):
+        for j in range(8):
+            r = HALO + 8 * i + j
+            c, d = co[C, r], co[D, r]
+            first, second = sol[0, r], sol[1, r]
+            spot = tile_at(0, i, j)
+            res[0, spot, :] = s[0, r] + co[ST, r] - d * first + c * around(beside, sol, 0, r)
+            res[1, spot, :] = s[1, r] + first - d * second + c * around(beside, sol, 1, r)
+            res[2, spot, :] = s[2, r] + second - d * sol2[0, r] + c * around(beside, sol2, 0, r)
+    copy.wait()
+
+
+def tail(t4, res, res_in, res_out, total, sems):
     del res_in
-    total[...] = base[...] + t4[...]
-    copy = pltpu.make_async_copy(total, res_out.at[pl.ds(0, ROWS * 8)], sem)
+    ready = pltpu.make_async_copy(res.at[pl.ds(1, 2)], res_out.at[pl.ds(1, 2)], sems.at[0])
+    ready.start()
+    total[...] = res[pl.ds(0, 1)] + t4[...][None]
+    copy = pltpu.make_async_copy(total, res_out.at[pl.ds(0, 1)], sems.at[1])
     copy.start()
+    ready.wait()
     copy.wait()
 
 
@@ -573,20 +569,20 @@
     start_v, conduct_v = view(start_state[None]), view(conduct[None])
     halo = rows_of(8 * HALO + 100)
     vmem = lambda steps: pltpu.VMEM((steps, EXT, 8, 128), F32)
-    plain = lambda rows: pltpu.VMEM((rows * 8, 128), F32)
     dma = pltpu.SemaphoreType.DMA
-    nat = jax.ShapeDtypeStruct((8 * ROWS * 8, 128), F32)
     one = jax.ShapeDtypeStruct((ROWS * 8, 128), F32)
 
     by_step = lambda x: pltpu.with_memory_space_constraint(x.reshape(-1, ROWS * 8, 128), pltpu.HBM)
-    near, far = call(
+    stepped = lambda steps: jax.ShapeDtypeStruct((steps, ROWS * 8, 128), F32)
+    near, far, guess_v, source_v, start_v, conduct_v = call(
         edge_pack,
         (is_first, is_odd, by_step(guess_v), by_step(source_v), by_step(start_v), by_step(conduct_v)),
-        [halo, halo],
-        [pltpu.VMEM((n, 2, 128, 128), F32) for n in (8, 8, 1, 1)] + [dma((4, 2))],
+        [halo, halo, stepped(8), stepped(8), stepped(1), stepped(1)],
+        [dma((4, 3))],
         specs=[SMEM, SMEM] + [ANY] * 4,
-        limit=6,
-    )
+        limit=1,
+    )
+    guess_v, source_v, start_v, conduct_v = (x.reshape(-1, 128) for x in (guess_v, source_v, start_v, conduct_v))
     far_in = along(far, "space", off_chip)
     near_in = along(near, "space", on_chip)
     (send0,) = call(
@@ -637,29 +633,30 @@
         limit=6,
     )
     t4 = along(send4, "tm", ahead)
+    nat3 = lambda steps: pltpu.VMEM((steps, ROWS * 8, 128), F32)
     sol, res, u2, sol2 = call(
         late,
         (t2, s, co, u, rs, e0, e1, e2, sol7),
-        [nat, nat, ext(2), ext(1)],
-        [vmem(2), vmem(8), vmem(8), vmem(8), plain(6 * ROWS), plain(5 * ROWS), dma((2,))],
+        [stepped(8), stepped(8), ext(2), ext(1)],
+        [vmem(2), vmem(8), vmem(8), vmem(8), nat3(6), nat3(5), dma((3,))],
         out_specs=[ANY, ANY, FULL, FULL],
         limit=16,
     )
-    sol, res, base = call(
+    sol, first_res = call(
         finish,
-        (t3, s, co, before, u2, sol2, sol, res),
-        [nat, nat, one],
-        [vmem(2), vmem(2), vmem(2), plain(2 * ROWS), plain(2 * ROWS), dma((2,))],
-        aliases={6: 0, 7: 1},
-        specs=[FULL] * 6 + [ANY] * 2,
-        out_specs=[ANY, ANY, FULL],
+        (t3, s, co, before, u2, sol2, sol),
+        [stepped(8), stepped(3)],
+        [vmem(2), vmem(2), vmem(2), nat3(2), dma],
+        aliases={6: 0},
+        specs=[FULL] * 6 + [ANY],
+        out_specs=[ANY, FULL],
         limit=6,
     )
     (res,) = call(
         tail,
-        (t4, base, res),
-        [nat],
-        [plain(ROWS), dma],
+        (t4, first_res, res),
+        [stepped(8)],
+        [nat3(1), dma((2,))],
         aliases={2: 0},
         specs=[FULL, FULL, ANY],
         out_specs=[ANY],

time: 50.1 us -> 49.9 us (level)
  the two profiles are of different devices: /device:TPU:96 before, /device:TPU:79 now
where the time goes in v5:
time: 49.9 us; the launch traced here: 49.6 us
  Pallas kernels  20.9 us (42%)
  waiting for transfers between devices  15 us (30%)
  starting transfers between devices  12.7 us (25%)
  between operations  0.93 us (2%)
    pallas_call x10, Pallas kernels, call(): pl.pallas_call(kernel, out_shape=outs, in_specs=specs or [FULL] * len(ins...  20.9 us
    ppermute x8, waiting for transfers between devices, along(): lax.ppermute(block, axis, [(i, j) for i, j in pairs if 0 <= j < count])  15 us
    ppermute x8, starting transfers between devices, along(): lax.ppermute(block, axis, [(i, j) for i, j in pairs if 0 <= j < count])  12.7 us
  transfers between devices with their start and end apart: 8, of which 5 were waited for; matrix products, arithmetic and copies ran while one was open for 0% of the time, Pallas kernels for 35%

profile of v5, /device:TPU:79, one launch (start us, length us, event | category | flops | bytes accessed | tf_op | source)
XLA Modules:
  0.0 49.6 jit_solution(17915497632471959176)
XLA Ops:
  0.6 2.5 %shard_map.59 = (f32[188,8,128]{2,1,0:T(8,128)S(1)}, f32[188,8,128]{2,1,0:T(8,128)S(1)}, f32[8,512,128]{2,1,0:T(8,128)S(1)}, f32[8,512,128]{2,1,0:T(8,128)S(1)},...) custom-call(f32[1]{0:T(128)} %bitcast.1.is_first, s32[1]{0:T(128)} %bitcast.is_odd, f32[8,512,128]{2,1,0:T(8,128)} %bitcast.44, ...), custom_call_target="tpu_custom_call" | custom-call | tf_op jit(solution)/shard_map/pallas_call | solution.py:536
  3.2 0.8 %collective-permute-start = (f32[188,8,128]{2,1,0:T(8,128)S(1)}, f32[188,8,128]{2,1,0:T(8,128)S(1)}, u32[]{:S(2)}, u32[]{:S(2)}) collective-permute-start(f32[188,8,128]{2,1,0:T(8,128)S(1)} %get-tuple-element.45), channel_id=1, source_target_pairs={{0,1},{1,0},{2,3},{3,2},{4,5},{5,4},{6,7},{7,6},{8,9},{9,8},{10,11... | collective-permute-start | bytes 2310152 | tf_op jit(solution)/shard_map/ppermute | solution.py:550
  3.9 3.1 %collective-permute-start.1 = (f32[188,8,128]{2,1,0:T(8,128)S(1)}, f32[188,8,128]{2,1,0:T(8,128)S(1)}, u32[]{:S(2)}, u32[]{:S(2)}) collective-permute-start(f32[188,8,128]{2,1,0:T(8,128)S(1)} %get-tuple-element.46), channel_id=1, source_target_pairs={{1,2},{2,1},{3,4},{4,3},{5,6},{6,5},{7,8},{8,7},{9,10},{10,9},{11,... | collective-permute-start | bytes 2310152 | tf_op jit(solution)/shard_map/ppermute | solution.py:550
  7.1 1.0 %shard_map.63 = f32[130,8,128]{2,1,0:T(8,128)S(1)} custom-call(f32[4096,128]{1,0:T(8,128)S(1)} %bitcast.36, f32[4096,128]{1,0:T(8,128)S(1)} %bitcast.38, f32[512,128]{1,0:T(8,128)S(1)} %bitcast.40), custom_call_target="tpu_custom_call" | custom-call | tf_op jit(solution)/shard_map/pallas_call | solution.py:536
  8.0 1.3 %collective-permute-start.3 = (f32[130,8,128]{2,1,0:T(8,128)S(1)}, f32[130,8,128]{2,1,0:T(8,128)S(1)}, u32[]{:S(2)}, u32[]{:S(2)}) collective-permute-start(f32[130,8,128]{2,1,0:T(8,128)S(1)} %shard_map.63), channel_id=1, source_target_pairs={{0,32},{32,64},{64,96},{1,33},{33,65},{65,97},{2,34},{34,66},{66,9... | collective-permute-start | bytes 1597448 | tf_op jit(solution)/shard_map/ppermute | solution.py:550
  9.3 3.7 %shard_map.60 = (f32[8,86,8,128]{3,2,1,0:T(8,128)S(1)}, f32[8,86,8,128]{3,2,1,0:T(8,128)S(1)}, f32[9,86,8,128]{3,2,1,0:T(8,128)S(1)}, f32[8,86,8,128]{3,2,1,0:T(...) custom-call(f32[1]{0:T(128)} %bitcast.1.is_first, ...), custom_call_target="tpu_custom_call" | custom-call | tf_op jit(solution)/shard_map/pallas_call | solution.py:536
  13.0 0.0 collective-permute-done.near
  13.0 4.3 %collective-permute-done.1.far = f32[188,8,128]{2,1,0:T(8,128)S(1)} collective-permute-done((f32[188,8,128]{2,1,0:T(8,128)S(1)}, f32[188,8,128]{2,1,0:T(8,128)S(1)}, u32[]{:S(2)}, u32[]{:S(2)}) %collective-permute-start.1) | collective-permute-done | bytes 770080 | tf_op jit(solution)/shard_map/ppermute | solution.py:550
  17.4 1.6 %shard_map.61 = (f32[8,86,8,128]{3,2,1,0:T(8,128)S(1)}, f32[8,86,8,128]{3,2,1,0:T(8,128)S(1)}, f32[9,86,8,128]{3,2,1,0:T(8,128)S(1)}, f32[8,86,8,128]{3,2,1,0:T(...) custom-call(s32[1]{0:T(128)} %bitcast.is_odd, ...), custom_call_target="tpu_custom_call", output_to_operand_aliasing={{0}: (3, {}), {1}: (4, {}), {2}: (5, {}), {3}: (6, {}), {4}... | custom-call | tf_op jit(solution)/shard_map/pallas_call | solution.py:536
  19.0 1.3 %collective-permute-start.6 = (f32[148,8,128]{2,1,0:T(8,128)S(1)}, f32[148,8,128]{2,1,0:T(8,128)S(1)}, u32[]{:S(2)}, u32[]{:S(2)}) collective-permute-start(f32[148,8,128]{2,1,0:T(8,128)S(1)} %get-tuple-element.74), channel_id=1, source_target_pairs={{0,32},{32,64},{64,96},{1,33},{33,65},{65,97},{2,34},{34,66},{66,9... | collective-permute-start | bytes 1818632 | tf_op jit(solution)/shard_map/ppermute | solution.py:550
  20.3 3.6 %collective-permute-done.3.t0 = f32[130,8,128]{2,1,0:T(8,128)S(1)} collective-permute-done((f32[130,8,128]{2,1,0:T(8,128)S(1)}, f32[130,8,128]{2,1,0:T(8,128)S(1)}, u32[]{:S(2)}, u32[]{:S(2)}) %collective-permute-start.3) | collective-permute-done | bytes 532512 | tf_op jit(solution)/shard_map/ppermute | solution.py:550
  23.9 0.2 collective-permute-start.4
  24.2 3.3 %collective-permute-start.5 = (f32[19,8,128]{2,1,0:T(8,128)S(1)}, f32[19,8,128]{2,1,0:T(8,128)S(1)}, u32[]{:S(2)}, u32[]{:S(2)}) collective-permute-start(f32[19,8,128]{2,1,0:T(8,128)S(1)} %get-tuple-element.67), channel_id=1, source_target_pairs={{1,2},{2,1},{3,4},{4,3},{5,6},{6,5},{7,8},{8,7},{9,10},{10,9},{11,... | collective-permute-start | bytes 233480 | tf_op jit(solution)/shard_map/ppermute | solution.py:550
  27.5 2.4 %shard_map.62 = (f32[8,86,8,128]{3,2,1,0:T(8,128)S(1)}, f32[4,86,8,128]{3,2,1,0:T(8,128)S(1)}, f32[4,86,8,128]{3,2,1,0:T(8,128)S(1)}, f32[4,86,8,128]{3,2,1,0:T(...) custom-call(f32[8,86,8,128]{3,2,1,0:T(8,128)S(1)} %get-tuple-element, ...), custom_call_target="tpu_custom_call", output_to_operand_aliasing={{0}: (3, {}), {1}: (4, {}), {2}: (5, {}), {3}: (6, {})} | custom-call | tf_op jit(solution)/shard_map/pallas_call | solution.py:536
  29.9 1.3 %collective-permute-start.2 = (f32[70,8,128]{2,1,0:T(8,128)S(1)}, f32[70,8,128]{2,1,0:T(8,128)S(1)}, u32[]{:S(2)}, u32[]{:S(2)}) collective-permute-start(f32[70,8,128]{2,1,0:T(8,128)S(1)} %get-tuple-element.65), channel_id=1, source_target_pairs={{0,32},{32,64},{64,96},{1,33},{33,65},{65,97},{2,34},{34,66},{66,9... | collective-permute-start | bytes 860168 | tf_op jit(solution)/shard_map/ppermute | solution.py:550
  31.2 0.0 collective-permute-done.4.near
  31.2 0.0 collective-permute-done.5.far
  31.2 2.5 %shard_map.65 = (f32[8,86,8,128]{3,2,1,0:T(8,128)S(1)}, f32[4,86,8,128]{3,2,1,0:T(8,128)S(1)}, f32[4,86,8,128]{3,2,1,0:T(8,128)S(1)}, f32[4,86,8,128]{3,2,1,0:T(...) custom-call(s32[1]{0:T(128)} %bitcast.is_odd, ...), custom_call_target="tpu_custom_call", output_to_operand_aliasing={{0}: (7, {}), {1}: (8, {}), {2}: (9, {}), {3}: (10, {}), {4... | custom-call | tf_op jit(solution)/shard_map/pallas_call | solution.py:536
  33.7 1.5 %collective-permute-start.7 = (f32[512,128]{1,0:T(8,128)S(1)}, f32[512,128]{1,0:T(8,128)S(1)}, u32[]{:S(2)}, u32[]{:S(2)}) collective-permute-start(f32[512,128]{1,0:T(8,128)S(1)} %get-tuple-element.85), channel_id=1, source_target_pairs={{0,32},{32,64},{64,96},{1,33},{33,65},{65,97},{2,34},{34,66},{66,9... | collective-permute-start | bytes 786440 | tf_op jit(solution)/shard_map/ppermute | solution.py:550
  35.2 1.7 %collective-permute-done.6.t2 = f32[148,8,128]{2,1,0:T(8,128)S(1)} collective-permute-done((f32[148,8,128]{2,1,0:T(8,128)S(1)}, f32[148,8,128]{2,1,0:T(8,128)S(1)}, u32[]{:S(2)}, u32[]{:S(2)}) %collective-permute-start.6) | collective-permute-done | bytes 606240 | tf_op jit(solution)/shard_map/ppermute | solution.py:550
  36.9 4.7 %shard_map.66 = (f32[8,512,128]{2,1,0:T(8,128)}, f32[8,512,128]{2,1,0:T(8,128)}, f32[2,86,8,128]{3,2,1,0:T(8,128)S(1)}, f32[1,86,8,128]{3,2,1,0:T(8,128)S(1)}) custom-call(f32[148,8,128]{2,1,0:T(8,128)S(1)} %collective-permute-done.6.t2, f32[8,86,8,128]{3,2,1,0:T(8,128)S(1)} %get-tuple-element.59.s, f32[9,86,8,128]{3,2,1,0:T(8,128)S(1)} %get-tuple-element.60.co, ...), custom_call_target="tpu_custom_call" | custom-call | tf_op jit(solution)/shard_map/pallas_call | solution.py:536
  41.6 1.4 %collective-permute-done.2.t3 = f32[70,8,128]{2,1,0:T(8,128)S(1)} collective-permute-done((f32[70,8,128]{2,1,0:T(8,128)S(1)}, f32[70,8,128]{2,1,0:T(8,128)S(1)}, u32[]{:S(2)}, u32[]{:S(2)}) %collective-permute-start.2) | collective-permute-done | bytes 286752 | tf_op jit(solution)/shard_map/ppermute | solution.py:550
  43.1 1.5 %shard_map.67 = (f32[8,512,128]{2,1,0:T(8,128)}, f32[3,512,128]{2,1,0:T(8,128)S(1)}) custom-call(f32[70,8,128]{2,1,0:T(8,128)S(1)} %collective-permute-done.2.t3, f32[8,86,8,128]{3,2,1,0:T(8,128)S(1)} %get-tuple-element.59.s, f32[9,86,8,128]{3,2,1,0:T(8,128)S(1)} %get-tuple-element.60.co, ...), custom_call_target="tpu_custom_call", output_to_operand_aliasing={{0}: (6, {})} | custom-call | tf_op jit(solution)/shard_map/pallas_call | solution.py:536
  44.6 3.9 %collective-permute-done.7.t4 = f32[512,128]{1,0:T(8,128)S(1)} collective-permute-done((f32[512,128]{1,0:T(8,128)S(1)}, f32[512,128]{1,0:T(8,128)S(1)}, u32[]{:S(2)}, u32[]{:S(2)}) %collective-permute-start.7) | collective-permute-done | bytes 262176 | tf_op jit(solution)/shard_map/ppermute | solution.py:550
  48.6 0.9 %shard_map.68 = f32[8,512,128]{2,1,0:T(8,128)} custom-call(f32[512,128]{1,0:T(8,128)S(1)} %collective-permute-done.7.t4, f32[3,512,128]{2,1,0:T(8,128)S(1)} %get-tuple-element.86.res, f32[8,512,128]{2,1,0:T(8,128)} %get-tuple-element.87.res_in), custom_call_target="tpu_custom_call", output_to_operand_aliasing={{}: (2, {})} | custom-call | tf_op jit(solution)/shard_map/pallas_call | solution.py:536
  (1 shorter events, 0.0 us)
Async XLA Ops:
  3.2 9.8 %collective-permute-start = (f32[188,8,128]{2,1,0:T(8,128)S(1)}, f32[188,8,128]{2,1,0:T(8,128)S(1)}, u32[]{:S(2)}, u32[]{:S(2)}) collective-permute-start(f32[188,8,128]{2,1,0:T(8,128)S(1)} %get-tuple-element.45), channel_id=1, source_target_pairs={{0,1},{1,0},{2,3},{3,2},{4,5},{5,4},{6,7},{7,6},{8,9},{9,8},{10,11... | collective-permute-start | bytes 2310152 | tf_op jit(solution)/shard_map/ppermute | solution.py:550
  3.9 13.4 %collective-permute-start.1 = (f32[188,8,128]{2,1,0:T(8,128)S(1)}, f32[188,8,128]{2,1,0:T(8,128)S(1)}, u32[]{:S(2)}, u32[]{:S(2)}) collective-permute-start(f32[188,8,128]{2,1,0:T(8,128)S(1)} %get-tuple-element.46), channel_id=1, source_target_pairs={{1,2},{2,1},{3,4},{4,3},{5,6},{6,5},{7,8},{8,7},{9,10},{10,9},{11,... | collective-permute-start | bytes 2310152 | tf_op jit(solution)/shard_map/ppermute | solution.py:550
  8.0 15.9 %collective-permute-start.3 = (f32[130,8,128]{2,1,0:T(8,128)S(1)}, f32[130,8,128]{2,1,0:T(8,128)S(1)}, u32[]{:S(2)}, u32[]{:S(2)}) collective-permute-start(f32[130,8,128]{2,1,0:T(8,128)S(1)} %shard_map.63), channel_id=1, source_target_pairs={{0,32},{32,64},{64,96},{1,33},{33,65},{65,97},{2,34},{34,66},{66,9... | collective-permute-start | bytes 1597448 | tf_op jit(solution)/shard_map/ppermute | solution.py:550
  19.0 17.9 %collective-permute-start.6 = (f32[148,8,128]{2,1,0:T(8,128)S(1)}, f32[148,8,128]{2,1,0:T(8,128)S(1)}, u32[]{:S(2)}, u32[]{:S(2)}) collective-permute-start(f32[148,8,128]{2,1,0:T(8,128)S(1)} %get-tuple-element.74), channel_id=1, source_target_pairs={{0,32},{32,64},{64,96},{1,33},{33,65},{65,97},{2,34},{34,66},{66,9... | collective-permute-start | bytes 1818632 | tf_op jit(solution)/shard_map/ppermute | solution.py:550
  23.9 7.2 %collective-permute-start.4 = (f32[19,8,128]{2,1,0:T(8,128)S(1)}, f32[19,8,128]{2,1,0:T(8,128)S(1)}, u32[]{:S(2)}, u32[]{:S(2)}) collective-permute-start(f32[19,8,128]{2,1,0:T(8,128)S(1)} %get-tuple-element.66), channel_id=1, source_target_pairs={{0,1},{1,0},{2,3},{3,2},{4,5},{5,4},{6,7},{7,6},{8,9},{9,8},{10,11... | collective-permute-start | bytes 233480 | tf_op jit(solution)/shard_map/ppermute | solution.py:550
  24.2 7.0 %collective-permute-start.5 = (f32[19,8,128]{2,1,0:T(8,128)S(1)}, f32[19,8,128]{2,1,0:T(8,128)S(1)}, u32[]{:S(2)}, u32[]{:S(2)}) collective-permute-start(f32[19,8,128]{2,1,0:T(8,128)S(1)} %get-tuple-element.67), channel_id=1, source_target_pairs={{1,2},{2,1},{3,4},{4,3},{5,6},{6,5},{7,8},{8,7},{9,10},{10,9},{11,... | collective-permute-start | bytes 233480 | tf_op jit(solution)/shard_map/ppermute | solution.py:550
  29.9 13.2 %collective-permute-start.2 = (f32[70,8,128]{2,1,0:T(8,128)S(1)}, f32[70,8,128]{2,1,0:T(8,128)S(1)}, u32[]{:S(2)}, u32[]{:S(2)}) collective-permute-start(f32[70,8,128]{2,1,0:T(8,128)S(1)} %get-tuple-element.65), channel_id=1, source_target_pairs={{0,32},{32,64},{64,96},{1,33},{33,65},{65,97},{2,34},{34,66},{66,9... | collective-permute-start | bytes 860168 | tf_op jit(solution)/shard_map/ppermute | solution.py:550
  33.7 14.8 %collective-permute-start.7 = (f32[512,128]{1,0:T(8,128)S(1)}, f32[512,128]{1,0:T(8,128)S(1)}, u32[]{:S(2)}, u32[]{:S(2)}) collective-permute-start(f32[512,128]{1,0:T(8,128)S(1)} %get-tuple-element.85), channel_id=1, source_target_pairs={{0,32},{32,64},{64,96},{1,33},{33,65},{65,97},{2,34},{34,66},{66,9... | collective-permute-start | bytes 786440 | tf_op jit(solution)/shard_map/ppermute | solution.py:550

commit v6 on v5

--- a/solution.py
+++ b/solution.py
@@ -138,7 +138,9 @@
         return body
 
 
-def edge_pack(is_first, is_odd, guess, source, start, conduct, near, far, gb, sb, tb, cb, sems):
+def edge_pack(
+    is_first, is_odd, guess, source, start, conduct, near, far, near_late, far_late, gb, sb, tb, cb, sems
+):
     pairs = ((guess, gb), (source, sb), (start, tb), (conduct, cb))
 
     def copies(spans):
@@ -154,26 +156,32 @@
     for copy in outer_tiles:
         copy.wait()
     odd = is_odd[0]
-    for out, side in ((near, 1 - odd), (far, odd)):
-
-        def outer(j, carry):
-            r = j + 53 * side
-            here = pl.ds((r // 8) * 64 + r % 8, 8, 8)
-            for t in range(8):
-                out[t * HALO + j] = gb[t, here, :]
+
+    def grab(out, base, ref, t, low, count, scale=None):
+        def body(j, carry):
+            r = low + j
+            value = ref[t, pl.ds((r // 8) * 64 + r % 8, 8, 8), :]
+            out[base + j] = value if scale is None else value * scale
             return carry
 
-        def inner(j, carry):
-            r = j + 54 * side
-            here = pl.ds((r // 8) * 64 + r % 8, 8, 8)
-            for t in range(8):
-                out[8 * HALO + t * 10 + j] = sb[t, here, :]
-            out[8 * HALO + 80 + j] = cb[0, here, :]
-            out[8 * HALO + 90 + j] = tb[0, here, :] * is_first[0]
-            return carry
-
-        lax.fori_loop(0, HALO, outer, 0)
-        lax.fori_loop(0, 10, inner, 0)
+        lax.fori_loop(0, count, body, 0, unroll=True)
+
+    for out, late_out, side in ((near, near_late, 1 - odd), (far, far_late, odd)):
+        for t in range(2, 8):
+            grab(out, (t - 2) * 6, gb, t, 58 * side, 6)
+        for t in range(3, 8):
+            grab(out, 36 + (t - 3) * 5, sb, t, 59 * side, 5)
+        grab(out, 61, cb, 0, 59 * side, 5)
+        for t in range(2):
+            grab(late_out, t * 11, gb, t, 53 * side, 11)
+        for t in range(2, 8):
+            grab(late_out, 22 + (t - 2) * 5, gb, t, 6 + 47 * side, 5)
+        for t in range(3):
+            grab(late_out, 52 + t * 10, sb, t, 54 * side, 10)
+        for t in range(3, 8):
+            grab(late_out, 82 + (t - 3) * 5, sb, t, 5 + 49 * side, 5)
+        grab(late_out, 107, cb, 0, 5 + 49 * side, 5)
+        grab(late_out, 112, tb, 0, 54 * side, 10, is_first[0])
     for copy in inner_tiles:
         copy.wait()
 
@@ -245,65 +253,75 @@
     sweep(6, 58, 90, st.smoothed(e1, e0, tmp, (3,), KQ))
 
 
+def both(inner, depth, body):
+    sweep(-depth, inner, 99, body)
+    sweep(ROWS - inner, ROWS + depth, 99, body)
+
+
+def scaled(co, rs, tmp):
+    def body(r):
+        for m in (2, 3):
+            tmp[m, r] = rs[m, r] * co[KINV, r]
+
+    return body
+
+
 def edges(is_odd, near, far, g_in, s_in, co_in, u_in, rs_in, e0_in, e1_in, g, s, co, u, rs, e0, e1, out, tmp):
     del g_in, s_in, co_in, u_in, rs_in, e0_in, e1_in
     beside = beside_maker()
     odd = is_odd[0]
     for source, side in ((near, 1 - odd), (far, odd)):
-        low = side * (HALO + ROWS)
-        low_inner = side * (HALO + ROWS - 1) + 1
-
-        def outer(j, carry):
-            for t in range(8):
-                g[t, low + j] = source[t * HALO + j]
-            return carry
-
-        def inner(j, carry):
-            for t in range(8):
-                s[t, low_inner + j] = source[8 * HALO + t * 10 + j]
-            coefficients(co, low_inner + j, source[8 * HALO + 80 + j])
-            co[ST, low_inner + j] = source[8 * HALO + 90 + j]
-            return carry
-
-        lax.fori_loop(0, HALO, outer, 0)
-        lax.fori_loop(0, 10, inner, 0)
+        for j in range(6):
+            for t in range(2, 8):
+                g[t, 5 + 70 * side + j] = source[(t - 2) * 6 + j]
+        for j in range(5):
+            for t in range(3, 8):
+                s[t, 6 + 69 * side + j] = source[36 + (t - 3) * 5 + j]
+            coefficients(co, 6 + 69 * side + j, source[61 + j])
     st = Stages(beside, co)
 
-    def both(inner, depth, unroll, body):
-        sweep(-depth, inner, unroll, body)
-        sweep(ROWS - inner, ROWS + depth, unroll, body)
-
-    both(3, 10, 13, st.fine_defect(tmp, g, lambda t, r: g[t - 1, r], s, range(3, 8)))
-    both(2, 9, 11, st.smoothed(u, g, tmp, range(3, 8), Q))
-    both(3, 8, 11, st.restricted(rs, tmp, u, lambda t, r: u[t - 1, r], s, (2, 3)))
-
-    def scale(r):
-        for m in (2, 3):
-            tmp[m, r] = rs[m, r] * co[KINV, r]
-
-    sweep(3, 5, 2, scale)
-    sweep(59, 61, 2, scale)
-    both(4, 7, 11, st.smoothed(e0, None, tmp, (2, 3), KQ))
-    both(7, 6, 13, st.coarse_defect(tmp, e0, lambda m, r: e0[m - 1, r], rs, (3,)))
-    both(6, 5, 11, st.smoothed(e1, e0, tmp, (3,), KQ))
-
-    def copy(i, carry):
-        for j in range(19):
-            r = i * 19 + j
-            out[r] = e0[3, HALO - 6 + r]
-            q = jnp.minimum(r, 71)
-            out[76 + q] = e1[3, HALO - 4 + q]
-        return carry
-
-    lax.fori_loop(0, 4, copy, 0)
-
-
-def rest(g, s, co, u_in, rs_in, e0_in, e1_in, u, rs, e0, e1, e2, send, tmp):
-    del u_in, rs_in, e0_in, e1_in
+    both(3, 5, st.fine_defect(tmp, g, lambda t, r: g[t - 1, r], s, range(3, 8)))
+    both(2, 4, st.smoothed(u, g, tmp, range(3, 8), Q))
+    both(3, 3, st.restricted(rs, tmp, u, lambda t, r: u[t - 1, r], s, (2, 3)))
+    both(5, -3, scaled(co, rs, tmp))
+    both(4, 2, st.smoothed(e0, None, tmp, (2, 3), KQ))
+    both(7, 1, st.coarse_defect(tmp, e0, lambda m, r: e0[m - 1, r], rs, (3,)))
+    both(6, 0, st.smoothed(e1, e0, tmp, (3,), KQ))
+    for r in range(ROWS):
+        out[r] = e0[3, HALO + r]
+        out[ROWS + r] = e1[3, HALO + r]
+
+
+def rest(
+    is_odd, near, far, g_in, s_in, co_in, u_in, rs_in, e0_in, e1_in, g, s, co, u, rs, e0, e1, e2, send, tmp
+):
+    del g_in, s_in, co_in, u_in, rs_in, e0_in, e1_in
     beside = beside_maker()
     st = Stages(beside, co)
-    sweep(-10, 74, 42, st.fine_defect(tmp, g, lambda t, r: g[t - 1, r], s, (1, 2)))
-    sweep(-9, 73, 41, st.smoothed(u, g, tmp, (1, 2), Q))
+    odd = is_odd[0]
+    for source, side in ((near, 1 - odd), (far, odd)):
+        for j in range(11):
+            for t in range(2):
+                g[t, 75 * side + j] = source[t * 11 + j]
+        for j in range(5):
+            for t in range(2, 8):
+                g[t, 81 * side + j] = source[22 + (t - 2) * 5 + j]
+            for t in range(3, 8):
+                s[t, 1 + 79 * side + j] = source[82 + (t - 3) * 5 + j]
+            coefficients(co, 1 + 79 * side + j, source[107 + j])
+        for j in range(10):
+            for t in range(3):
+                s[t, 1 + 74 * side + j] = source[52 + t * 10 + j]
+            co[ST, 1 + 74 * side + j] = source[112 + j]
+    both(-3, 10, st.fine_defect(tmp, g, lambda t, r: g[t - 1, r], s, range(3, 8)))
+    both(-4, 9, st.smoothed(u, g, tmp, range(3, 8), Q))
+    both(-3, 8, st.restricted(rs, tmp, u, lambda t, r: u[t - 1, r], s, (2, 3)))
+    both(-1, 3, scaled(co, rs, tmp))
+    both(-2, 7, st.smoothed(e0, None, tmp, (2, 3), KQ))
+    both(1, 6, st.coarse_defect(tmp, e0, lambda m, r: e0[m - 1, r], rs, (3,)))
+    both(0, 5, st.smoothed(e1, e0, tmp, (3,), KQ))
+    sweep(-10, 74, 90, st.fine_defect(tmp, g, lambda t, r: g[t - 1, r], s, (1, 2)))
+    sweep(-9, 73, 90, st.smoothed(u, g, tmp, (1, 2), Q))
     sweep(-8, 72, 90, st.restricted(rs, tmp, u, lambda t, r: u[t - 1, r], s, (1,)))
     sweep(-7, 71, 90, st.smoothed(e0, None, tmp, (1,), KQ))
     sweep(-6, 70, 90, st.coarse_defect(tmp, e0, lambda m, r: e0[m - 1, r], rs, (2,)))
@@ -403,13 +421,34 @@
     lax.fori_loop(0, ROWS // 8, copy, 0)
 
 
-def late(t2, s, co, u, rs, e0, e1_in, e2_in, sol7, sol_out, res_out, u2_out, sol2, e1, u2, tmp, sol, sol_nat, res_nat, sems):
+def relay_late(is_odd, t2, near, far):
+    odd = is_odd[0]
+    for out, side in ((near, 1 - odd), (far, odd)):
+        for j in range(6):
+            out[j] = t2[58 * side + j]
+        for j in range(4):
+            out[6 + j] = t2[ROWS + 60 * side + j]
+
+
+def late(
+    is_odd, t2, near, far, s, co, u, rs, e0, e1_in, e2_in, sol7, sol_out, res_out, u2_out, sol2,
+    old, e1, u2, tmp, sol, sol_nat, res_nat, sems,
+):
     beside = beside_maker()
     st = Stages(beside, co)
+    odd = is_odd[0]
+    for source, side in ((near, 1 - odd), (far, odd)):
+        for j in range(6):
+            old[0, 5 + 70 * side + j] = source[j]
+        for j in range(4):
+            old[1, 7 + 68 * side + j] = source[6 + j]
+
+    def earlier_step(n, r):
+        return t2[n * ROWS + r - HALO] if HALO <= r < HALO + ROWS else old[n, r]
 
     def first_defect(r):
         tmp[0, r] = (
-            rs[0, r] + t2[r - (HALO - 6)] - co[KD, r] * e0[0, r] + co[K, r] * around(beside, e0, 0, r)
+            rs[0, r] + earlier_step(0, r) - co[KD, r] * e0[0, r] + co[K, r] * around(beside, e0, 0, r)
         ) * co[KINV, r]
 
     sweep(-6, 70, 90, first_defect)
@@ -422,7 +461,7 @@
 
     def second_defect(r):
         k, kd, kinv = co[K, r], co[KD, r], co[KINV, r]
-        earlier = (t2[76 + r - (HALO - 4)], e1[0, r])
+        earlier = (earlier_step(1, r), e1[0, r])
         for m in (0, 1):
             tmp[m, r] = (rs[m, r] + earlier[m] - kd * e1[m, r] + k * around(beside, e1, m, r)) * kinv
 
@@ -567,24 +606,21 @@
     is_odd = (lax.axis_index("space") % 2).astype(jnp.int32).reshape(1)
     guess_v, source_v = view(guess), view(source)
     start_v, conduct_v = view(start_state[None]), view(conduct[None])
-    halo = rows_of(8 * HALO + 100)
     vmem = lambda steps: pltpu.VMEM((steps, EXT, 8, 128), F32)
     dma = pltpu.SemaphoreType.DMA
     one = jax.ShapeDtypeStruct((ROWS * 8, 128), F32)
 
     by_step = lambda x: pltpu.with_memory_space_constraint(x.reshape(-1, ROWS * 8, 128), pltpu.HBM)
     stepped = lambda steps: jax.ShapeDtypeStruct((steps, ROWS * 8, 128), F32)
-    near, far, guess_v, source_v, start_v, conduct_v = call(
+    near, far, near_late, far_late, guess_v, source_v, start_v, conduct_v = call(
         edge_pack,
         (is_first, is_odd, by_step(guess_v), by_step(source_v), by_step(start_v), by_step(conduct_v)),
-        [halo, halo, stepped(8), stepped(8), stepped(1), stepped(1)],
+        [rows_of(66), rows_of(66), rows_of(122), rows_of(122), stepped(8), stepped(8), stepped(1), stepped(1)],
         [dma((4, 3))],
         specs=[SMEM, SMEM] + [ANY] * 4,
         limit=1,
     )
     guess_v, source_v, start_v, conduct_v = (x.reshape(-1, 128) for x in (guess_v, source_v, start_v, conduct_v))
-    far_in = along(far, "space", off_chip)
-    near_in = along(near, "space", on_chip)
     (send0,) = call(
         last_step_pack,
         (guess_v, source_v, conduct_v),
@@ -593,6 +629,10 @@
         limit=4,
     )
     t0 = along(send0, "tm", ahead)
+    far_in = along(far, "space", off_chip)
+    near_in = along(near, "space", on_chip)
+    far_late_in = along(far_late, "space", off_chip)
+    near_late_in = along(near_late, "space", on_chip)
     g, s, co, u, rs, e0, e1 = call(
         interior,
         (is_first, guess_v, source_v, start_v, conduct_v),
@@ -604,7 +644,7 @@
     g, s, co, u, rs, e0, e1, send2 = call(
         edges,
         (is_odd, near_in, far_in, g, s, co, u, rs, e0, e1),
-        [ext(8), ext(8), ext(9), ext(8), ext(4), ext(4), ext(4), rows_of(148)],
+        [ext(8), ext(8), ext(9), ext(8), ext(4), ext(4), ext(4), rows_of(128)],
         [vmem(8)],
         aliases={n + 3: n for n in range(7)},
         specs=[SMEM] + [FULL] * 9,
@@ -614,13 +654,14 @@
     near, far = call(relay, (is_odd, t0), [rows_of(19), rows_of(19)], specs=[SMEM, FULL], limit=1)
     far_in = along(far, "space", off_chip)
     near_in = along(near, "space", on_chip)
-    u, rs, e0, e1, e2, send3 = call(
+    g, s, co, u, rs, e0, e1, e2, send3 = call(
         rest,
-        (g, s, co, u, rs, e0, e1),
-        [ext(8), ext(4), ext(4), ext(4), ext(4), rows_of(70)],
-        [vmem(4)],
-        aliases={3: 0, 4: 1, 5: 2, 6: 3},
-        limit=4,
+        (is_odd, near_late_in, far_late_in, g, s, co, u, rs, e0, e1),
+        [ext(8), ext(8), ext(9), ext(8), ext(4), ext(4), ext(4), ext(4), rows_of(70)],
+        [vmem(8)],
+        aliases={n + 3: n for n in range(7)},
+        specs=[SMEM] + [FULL] * 9,
+        limit=6,
     )
     t3 = along(send3, "tm", ahead)
     u, rs, e0, e1, e2, before, sol7, send4 = call(
@@ -634,11 +675,15 @@
     )
     t4 = along(send4, "tm", ahead)
     nat3 = lambda steps: pltpu.VMEM((steps, ROWS * 8, 128), F32)
+    near, far = call(relay_late, (is_odd, t2), [rows_of(10), rows_of(10)], specs=[SMEM, FULL], limit=1)
+    far_in = along(far, "space", off_chip)
+    near_in = along(near, "space", on_chip)
     sol, res, u2, sol2 = call(
         late,
-        (t2, s, co, u, rs, e0, e1, e2, sol7),
+        (is_odd, t2, near_in, far_in, s, co, u, rs, e0, e1, e2, sol7),
         [stepped(8), stepped(8), ext(2), ext(1)],
-        [vmem(2), vmem(8), vmem(8), vmem(8), nat3(6), nat3(5), dma((3,))],
+        [vmem(2), vmem(2), vmem(8), vmem(8), vmem(8), nat3(6), nat3(5), dma((3,))],
+        specs=[SMEM] + [FULL] * 11,
         out_specs=[ANY, ANY, FULL, FULL],
         limit=16,
     )

time: 49.9 us -> 54.3 us (1.088)
  the two profiles are of different devices: /device:TPU:79 before, /device:TPU:96 now
where the time goes in v6:
time: 54.3 us; the launch traced here: 54 us
  starting transfers between devices  27.4 us (50%)
  Pallas kernels  20.8 us (38%)
  waiting for transfers between devices  4.72 us (9%)
  between operations  1.05 us (2%)
    ppermute x12, starting transfers between devices, along(): lax.ppermute(block, axis, [(i, j) for i, j in pairs if 0 <= j < count])  27.4 us
    pallas_call x11, Pallas kernels, call(): pl.pallas_call(kernel, out_shape=outs, in_specs=specs or [FULL] * len(ins...  20.8 us
    ppermute x12, waiting for transfers between devices, along(): lax.ppermute(block, axis, [(i, j) for i, j in pairs if 0 <= j < count])  4.72 us
  transfers between devices with their start and end apart: 12, of which 1 were waited for; matrix products, arithmetic and copies ran while one was open for 0% of the time, Pallas kernels for 31%

profile of v6, /device:TPU:96, one launch (start us, length us, event | category | flops | bytes accessed | tf_op | source)
XLA Modules:
  0.0 54.0 jit_solution(6616994448892235078)
XLA Ops:
  0.6 2.4 %shard_map.59 = (f32[66,8,128]{2,1,0:T(8,128)S(1)}, f32[66,8,128]{2,1,0:T(8,128)S(1)}, f32[122,8,128]{2,1,0:T(8,128)S(1)}, f32[122,8,128]{2,1,0:T(8,128)S(1)}, f...) custom-call(f32[1]{0:T(128)} %bitcast.1.is_first, ...), custom_call_target="tpu_custom_call" | custom-call | tf_op jit(solution)/shard_map/pallas_call | solution.py:575
  3.0 1.0 %shard_map.63 = f32[130,8,128]{2,1,0:T(8,128)S(1)} custom-call(f32[4096,128]{1,0:T(8,128)S(1)} %bitcast.36, f32[4096,128]{1,0:T(8,128)S(1)} %bitcast.38, f32[512,128]{1,0:T(8,128)S(1)} %bitcast.40), custom_call_target="tpu_custom_call" | custom-call | tf_op jit(solution)/shard_map/pallas_call | solution.py:575
  4.0 3.4 %collective-permute-start.5 = (f32[130,8,128]{2,1,0:T(8,128)S(1)}, f32[130,8,128]{2,1,0:T(8,128)S(1)}, u32[]{:S(2)}, u32[]{:S(2)}) collective-permute-start(f32[130,8,128]{2,1,0:T(8,128)S(1)} %shard_map.63), channel_id=1, source_target_pairs={{0,32},{32,64},{64,96},{1,33},{33,65},{65,97},{2,34},{34,66},{66,9... | collective-permute-start | bytes 1597448 | tf_op jit(solution)/shard_map/ppermute | solution.py:589
  7.5 0.1 collective-permute-start.2
  7.5 4.9 %collective-permute-start.3 = (f32[66,8,128]{2,1,0:T(8,128)S(1)}, f32[66,8,128]{2,1,0:T(8,128)S(1)}, u32[]{:S(2)}, u32[]{:S(2)}) collective-permute-start(f32[66,8,128]{2,1,0:T(8,128)S(1)} %get-tuple-element.55), channel_id=1, source_target_pairs={{1,2},{2,1},{3,4},{4,3},{5,6},{6,5},{7,8},{8,7},{9,10},{10,9},{11,... | collective-permute-start | bytes 811016 | tf_op jit(solution)/shard_map/ppermute | solution.py:589
  12.4 0.1 collective-permute-start
  12.5 2.8 %collective-permute-start.1 = (f32[122,8,128]{2,1,0:T(8,128)S(1)}, f32[122,8,128]{2,1,0:T(8,128)S(1)}, u32[]{:S(2)}, u32[]{:S(2)}) collective-permute-start(f32[122,8,128]{2,1,0:T(8,128)S(1)} %get-tuple-element.53), channel_id=1, source_target_pairs={{1,2},{2,1},{3,4},{4,3},{5,6},{6,5},{7,8},{8,7},{9,10},{10,9},{11,... | collective-permute-start | bytes 1499144 | tf_op jit(solution)/shard_map/ppermute | solution.py:589
  15.3 3.7 %shard_map.60 = (f32[8,86,8,128]{3,2,1,0:T(8,128)S(1)}, f32[8,86,8,128]{3,2,1,0:T(8,128)S(1)}, f32[9,86,8,128]{3,2,1,0:T(8,128)S(1)}, f32[8,86,8,128]{3,2,1,0:T(...) custom-call(f32[1]{0:T(128)} %bitcast.1.is_first, ...), custom_call_target="tpu_custom_call" | custom-call | tf_op jit(solution)/shard_map/pallas_call | solution.py:575
  19.1 0.0 collective-permute-done.2.near
  19.1 0.0 collective-permute-done.3.far
  19.1 0.7 %shard_map.61 = (f32[8,86,8,128]{3,2,1,0:T(8,128)S(1)}, f32[8,86,8,128]{3,2,1,0:T(8,128)S(1)}, f32[9,86,8,128]{3,2,1,0:T(8,128)S(1)}, f32[8,86,8,128]{3,2,1,0:T(...) custom-call(s32[1]{0:T(128)} %bitcast.is_odd, ...), custom_call_target="tpu_custom_call", output_to_operand_aliasing={{0}: (3, {}), {1}: (4, {}), {2}: (5, {}), {3}: (6, {}), {4}... | custom-call | tf_op jit(solution)/shard_map/pallas_call | solution.py:575
  19.8 3.4 %collective-permute-start.8 = (f32[128,8,128]{2,1,0:T(8,128)S(1)}, f32[128,8,128]{2,1,0:T(8,128)S(1)}, u32[]{:S(2)}, u32[]{:S(2)}) collective-permute-start(f32[128,8,128]{2,1,0:T(8,128)S(1)} %get-tuple-element.86), channel_id=1, source_target_pairs={{0,32},{32,64},{64,96},{1,33},{33,65},{65,97},{2,34},{34,66},{66,9... | collective-permute-start | bytes 1572872 | tf_op jit(solution)/shard_map/ppermute | solution.py:589
  23.3 0.0 collective-permute-done.5.t0
  23.3 0.1 collective-permute-start.6
  23.4 4.6 %collective-permute-start.7 = (f32[19,8,128]{2,1,0:T(8,128)S(1)}, f32[19,8,128]{2,1,0:T(8,128)S(1)}, u32[]{:S(2)}, u32[]{:S(2)}) collective-permute-start(f32[19,8,128]{2,1,0:T(8,128)S(1)} %get-tuple-element.78), channel_id=1, source_target_pairs={{1,2},{2,1},{3,4},{4,3},{5,6},{6,5},{7,8},{8,7},{9,10},{10,9},{11,... | collective-permute-start | bytes 233480 | tf_op jit(solution)/shard_map/ppermute | solution.py:589
  28.0 0.0 collective-permute-done.near
  28.0 0.0 collective-permute-done.1.far
  28.0 3.0 %shard_map.62 = (f32[8,86,8,128]{3,2,1,0:T(8,128)S(1)}, f32[8,86,8,128]{3,2,1,0:T(8,128)S(1)}, f32[9,86,8,128]{3,2,1,0:T(8,128)S(1)}, f32[8,86,8,128]{3,2,1,0:T(...) custom-call(s32[1]{0:T(128)} %bitcast.is_odd, ...), custom_call_target="tpu_custom_call", output_to_operand_aliasing={{0}: (3, {}), {1}: (4, {}), {2}: (5, {}), {3}: (6, {}), {4}... | custom-call | tf_op jit(solution)/shard_map/pallas_call | solution.py:575
  31.0 3.1 %collective-permute-start.4 = (f32[70,8,128]{2,1,0:T(8,128)S(1)}, f32[70,8,128]{2,1,0:T(8,128)S(1)}, u32[]{:S(2)}, u32[]{:S(2)}) collective-permute-start(f32[70,8,128]{2,1,0:T(8,128)S(1)} %get-tuple-element.74), channel_id=1, source_target_pairs={{0,32},{32,64},{64,96},{1,33},{33,65},{65,97},{2,34},{34,66},{66,9... | collective-permute-start | bytes 860168 | tf_op jit(solution)/shard_map/ppermute | solution.py:589
  34.1 0.0 collective-permute-done.6.near
  34.1 0.0 collective-permute-done.7.far
  34.1 2.6 %shard_map.65 = (f32[8,86,8,128]{3,2,1,0:T(8,128)S(1)}, f32[4,86,8,128]{3,2,1,0:T(8,128)S(1)}, f32[4,86,8,128]{3,2,1,0:T(8,128)S(1)}, f32[4,86,8,128]{3,2,1,0:T(...) custom-call(s32[1]{0:T(128)} %bitcast.is_odd, ...), custom_call_target="tpu_custom_call", output_to_operand_aliasing={{0}: (7, {}), {1}: (8, {}), {2}: (9, {}), {3}: (10, {}), {4... | custom-call | tf_op jit(solution)/shard_map/pallas_call | solution.py:575
  36.7 2.2 %collective-permute-start.11 = (f32[512,128]{1,0:T(8,128)S(1)}, f32[512,128]{1,0:T(8,128)S(1)}, u32[]{:S(2)}, u32[]{:S(2)}) collective-permute-start(f32[512,128]{1,0:T(8,128)S(1)} %get-tuple-element.99), channel_id=1, source_target_pairs={{0,32},{32,64},{64,96},{1,33},{33,65},{65,97},{2,34},{34,66},{66,9... | collective-permute-start | bytes 786440 | tf_op jit(solution)/shard_map/ppermute | solution.py:589
  38.9 0.0 collective-permute-done.8.t2
  38.9 0.1 collective-permute-start.9
  39.0 2.7 %collective-permute-start.10 = (f32[10,8,128]{2,1,0:T(8,128)S(1)}, f32[10,8,128]{2,1,0:T(8,128)S(1)}, u32[]{:S(2)}, u32[]{:S(2)}) collective-permute-start(f32[10,8,128]{2,1,0:T(8,128)S(1)} %get-tuple-element.88), channel_id=1, source_target_pairs={{1,2},{2,1},{3,4},{4,3},{5,6},{6,5},{7,8},{8,7},{9,10},{10,9},{11,... | collective-permute-start | bytes 122888 | tf_op jit(solution)/shard_map/ppermute | solution.py:589
  41.7 0.0 collective-permute-done.9.near
  41.7 4.7 %collective-permute-done.10.far = f32[10,8,128]{2,1,0:T(8,128)S(1)} collective-permute-done((f32[10,8,128]{2,1,0:T(8,128)S(1)}, f32[10,8,128]{2,1,0:T(8,128)S(1)}, u32[]{:S(2)}, u32[]{:S(2)}) %collective-permute-start.10) | collective-permute-done | bytes 40992 | tf_op jit(solution)/shard_map/ppermute | solution.py:589
  46.4 4.9 %shard_map.67 = (f32[8,512,128]{2,1,0:T(8,128)}, f32[8,512,128]{2,1,0:T(8,128)}, f32[2,86,8,128]{3,2,1,0:T(8,128)S(1)}, f32[1,86,8,128]{3,2,1,0:T(8,128)S(1)}) custom-call(s32[1]{0:T(128)} %bitcast.is_odd, f32[128,8,128]{2,1,0:T(8,128)S(1)} %collective-permute-done.8.t2, f32[10,8,128]{2,1,0:T(8,128)S(1)} %collective-permute-done.9.near, ...), custom_call_target="tpu_custom_call" | custom-call | tf_op jit(solution)/shard_map/pallas_call | solution.py:575
  51.3 0.0 collective-permute-done.4.t3
  51.3 1.6 %shard_map.68 = (f32[8,512,128]{2,1,0:T(8,128)}, f32[3,512,128]{2,1,0:T(8,128)S(1)}) custom-call(f32[70,8,128]{2,1,0:T(8,128)S(1)} %collective-permute-done.4.t3, f32[8,86,8,128]{3,2,1,0:T(8,128)S(1)} %get-tuple-element.75.s, f32[9,86,8,128]{3,2,1,0:T(8,128)S(1)} %get-tuple-element.76.co, ...), custom_call_target="tpu_custom_call", output_to_operand_aliasing={{0}: (6, {})} | custom-call | tf_op jit(solution)/shard_map/pallas_call | solution.py:575
  52.9 0.0 collective-permute-done.11.t4
  52.9 0.9 %shard_map.69 = f32[8,512,128]{2,1,0:T(8,128)} custom-call(f32[512,128]{1,0:T(8,128)S(1)} %collective-permute-done.11.t4, f32[3,512,128]{2,1,0:T(8,128)S(1)} %get-tuple-element.100.res, f32[8,512,128]{2,1,0:T(8,128)} %get-tuple-element.101.res_in), custom_call_target="tpu_custom_call", output_to_operand_aliasing={{}: (2, {})} | custom-call | tf_op jit(solution)/shard_map/pallas_call | solution.py:575
  (2 shorter events, 0.0 us)
Async XLA Ops:
  4.0 19.2 %collective-permute-start.5 = (f32[130,8,128]{2,1,0:T(8,128)S(1)}, f32[130,8,128]{2,1,0:T(8,128)S(1)}, u32[]{:S(2)}, u32[]{:S(2)}) collective-permute-start(f32[130,8,128]{2,1,0:T(8,128)S(1)} %shard_map.63), channel_id=1, source_target_pairs={{0,32},{32,64},{64,96},{1,33},{33,65},{65,97},{2,34},{34,66},{66,9... | collective-permute-start | bytes 1597448 | tf_op jit(solution)/shard_map/ppermute | solution.py:589
  7.5 11.6 %collective-permute-start.2 = (f32[66,8,128]{2,1,0:T(8,128)S(1)}, f32[66,8,128]{2,1,0:T(8,128)S(1)}, u32[]{:S(2)}, u32[]{:S(2)}) collective-permute-start(f32[66,8,128]{2,1,0:T(8,128)S(1)} %get-tuple-element.54), channel_id=1, source_target_pairs={{0,1},{1,0},{2,3},{3,2},{4,5},{5,4},{6,7},{7,6},{8,9},{9,8},{10,11... | collective-permute-start | bytes 811016 | tf_op jit(solution)/shard_map/ppermute | solution.py:589
  7.5 11.5 %collective-permute-start.3 = (f32[66,8,128]{2,1,0:T(8,128)S(1)}, f32[66,8,128]{2,1,0:T(8,128)S(1)}, u32[]{:S(2)}, u32[]{:S(2)}) collective-permute-start(f32[66,8,128]{2,1,0:T(8,128)S(1)} %get-tuple-element.55), channel_id=1, source_target_pairs={{1,2},{2,1},{3,4},{4,3},{5,6},{6,5},{7,8},{8,7},{9,10},{10,9},{11,... | collective-permute-start | bytes 811016 | tf_op jit(solution)/shard_map/ppermute | solution.py:589
  12.4 15.6 %collective-permute-start = (f32[122,8,128]{2,1,0:T(8,128)S(1)}, f32[122,8,128]{2,1,0:T(8,128)S(1)}, u32[]{:S(2)}, u32[]{:S(2)}) collective-permute-start(f32[122,8,128]{2,1,0:T(8,128)S(1)} %get-tuple-element.52), channel_id=1, source_target_pairs={{0,1},{1,0},{2,3},{3,2},{4,5},{5,4},{6,7},{7,6},{8,9},{9,8},{10,11... | collective-permute-start | bytes 1499144 | tf_op jit(solution)/shard_map/ppermute | solution.py:589
  12.5 15.5 %collective-permute-start.1 = (f32[122,8,128]{2,1,0:T(8,128)S(1)}, f32[122,8,128]{2,1,0:T(8,128)S(1)}, u32[]{:S(2)}, u32[]{:S(2)}) collective-permute-start(f32[122,8,128]{2,1,0:T(8,128)S(1)} %get-tuple-element.53), channel_id=1, source_target_pairs={{1,2},{2,1},{3,4},{4,3},{5,6},{6,5},{7,8},{8,7},{9,10},{10,9},{11,... | collective-permute-start | bytes 1499144 | tf_op jit(solution)/shard_map/ppermute | solution.py:589
  19.8 19.0 %collective-permute-start.8 = (f32[128,8,128]{2,1,0:T(8,128)S(1)}, f32[128,8,128]{2,1,0:T(8,128)S(1)}, u32[]{:S(2)}, u32[]{:S(2)}) collective-permute-start(f32[128,8,128]{2,1,0:T(8,128)S(1)} %get-tuple-element.86), channel_id=1, source_target_pairs={{0,32},{32,64},{64,96},{1,33},{33,65},{65,97},{2,34},{34,66},{66,9... | collective-permute-start | bytes 1572872 | tf_op jit(solution)/shard_map/ppermute | solution.py:589
  23.3 10.8 %collective-permute-start.6 = (f32[19,8,128]{2,1,0:T(8,128)S(1)}, f32[19,8,128]{2,1,0:T(8,128)S(1)}, u32[]{:S(2)}, u32[]{:S(2)}) collective-permute-start(f32[19,8,128]{2,1,0:T(8,128)S(1)} %get-tuple-element.77), channel_id=1, source_target_pairs={{0,1},{1,0},{2,3},{3,2},{4,5},{5,4},{6,7},{7,6},{8,9},{9,8},{10,11... | collective-permute-start | bytes 233480 | tf_op jit(solution)/shard_map/ppermute | solution.py:589
  23.4 10.7 %collective-permute-start.7 = (f32[19,8,128]{2,1,0:T(8,128)S(1)}, f32[19,8,128]{2,1,0:T(8,128)S(1)}, u32[]{:S(2)}, u32[]{:S(2)}) collective-permute-start(f32[19,8,128]{2,1,0:T(8,128)S(1)} %get-tuple-element.78), channel_id=1, source_target_pairs={{1,2},{2,1},{3,4},{4,3},{5,6},{6,5},{7,8},{8,7},{9,10},{10,9},{11,... | collective-permute-start | bytes 233480 | tf_op jit(solution)/shard_map/ppermute | solution.py:589
  31.0 20.3 %collective-permute-start.4 = (f32[70,8,128]{2,1,0:T(8,128)S(1)}, f32[70,8,128]{2,1,0:T(8,128)S(1)}, u32[]{:S(2)}, u32[]{:S(2)}) collective-permute-start(f32[70,8,128]{2,1,0:T(8,128)S(1)} %get-tuple-element.74), channel_id=1, source_target_pairs={{0,32},{32,64},{64,96},{1,33},{33,65},{65,97},{2,34},{34,66},{66,9... | collective-permute-start | bytes 860168 | tf_op jit(solution)/shard_map/ppermute | solution.py:589
  36.7 16.3 %collective-permute-start.11 = (f32[512,128]{1,0:T(8,128)S(1)}, f32[512,128]{1,0:T(8,128)S(1)}, u32[]{:S(2)}, u32[]{:S(2)}) collective-permute-start(f32[512,128]{1,0:T(8,128)S(1)} %get-tuple-element.99), channel_id=1, source_target_pairs={{0,32},{32,64},{64,96},{1,33},{33,65},{65,97},{2,34},{34,66},{66,9... | collective-permute-start | bytes 786440 | tf_op jit(solution)/shard_map/ppermute | solution.py:589
  38.9 2.8 %collective-permute-start.9 = (f32[10,8,128]{2,1,0:T(8,128)S(1)}, f32[10,8,128]{2,1,0:T(8,128)S(1)}, u32[]{:S(2)}, u32[]{:S(2)}) collective-permute-start(f32[10,8,128]{2,1,0:T(8,128)S(1)} %get-tuple-element.87), channel_id=1, source_target_pairs={{0,1},{1,0},{2,3},{3,2},{4,5},{5,4},{6,7},{7,6},{8,9},{9,8},{10,11... | collective-permute-start | bytes 122888 | tf_op jit(solution)/shard_map/ppermute | solution.py:589
  39.0 7.4 %collective-permute-start.10 = (f32[10,8,128]{2,1,0:T(8,128)S(1)}, f32[10,8,128]{2,1,0:T(8,128)S(1)}, u32[]{:S(2)}, u32[]{:S(2)}) collective-permute-start(f32[10,8,128]{2,1,0:T(8,128)S(1)} %get-tuple-element.88), channel_id=1, source_target_pairs={{1,2},{2,1},{3,4},{4,3},{5,6},{6,5},{7,8},{8,7},{9,10},{10,9},{11,... | collective-permute-start | bytes 122888 | tf_op jit(solution)/shard_map/ppermute | solution.py:589

commit v7 on v6

--- a/solution.py
+++ b/solution.py
@@ -32,10 +32,6 @@
 
 def unview(y, steps):
     return y.reshape(steps, ROWS // 8, 8, 8, 128).transpose(0, 1, 3, 2, 4).reshape(steps, ROWS, 1024)
-
-
-def at(ref, step, row):
-    return ref[pl.ds(step * ROWS * 8 + (row // 8) * 64 + row % 8, 8, 8), :]
 
 
 def tile_at(step, tile, row):
@@ -168,66 +164,30 @@
 
     for out, late_out, side in ((near, near_late, 1 - odd), (far, far_late, odd)):
         for t in range(2, 8):
-            grab(out, (t - 2) * 6, gb, t, 58 * side, 6)
+            grab(out, (t - 2) * 10, gb, t, 54 * side, 10)
         for t in range(3, 8):
-            grab(out, 36 + (t - 3) * 5, sb, t, 59 * side, 5)
-        grab(out, 61, cb, 0, 59 * side, 5)
+            grab(out, 60 + (t - 3) * 9, sb, t, 55 * side, 9)
+        grab(out, 105, cb, 0, 55 * side, 9)
         for t in range(2):
             grab(late_out, t * 11, gb, t, 53 * side, 11)
         for t in range(2, 8):
-            grab(late_out, 22 + (t - 2) * 5, gb, t, 6 + 47 * side, 5)
+            grab(late_out, 20 + t, gb, t, 10 + 43 * side, 1)
         for t in range(3):
-            grab(late_out, 52 + t * 10, sb, t, 54 * side, 10)
+            grab(late_out, 28 + t * 10, sb, t, 54 * side, 10)
         for t in range(3, 8):
-            grab(late_out, 82 + (t - 3) * 5, sb, t, 5 + 49 * side, 5)
-        grab(late_out, 107, cb, 0, 5 + 49 * side, 5)
-        grab(late_out, 112, tb, 0, 54 * side, 10, is_first[0])
+            grab(late_out, 55 + t, sb, t, 9 + 45 * side, 1)
+        grab(late_out, 63, cb, 0, 9 + 45 * side, 1)
+        grab(late_out, 64, tb, 0, 54 * side, 10, is_first[0])
     for copy in inner_tiles:
         copy.wait()
 
 
-def last_step_pack(guess, source, conduct, out, g, e):
-    beside = beside_maker()
-
-    def fill(i, carry):
+def last_step_pack(guess, source, out):
+    for i in range(ROWS // 8):
         for j in range(8):
             r = 8 * i + j
-            for t in (6, 7):
-                g[t - 6, r] = guess[tile_at(t, i, j), :]
-            out[r] = g[1, r]
-        return carry
-
-    lax.fori_loop(0, ROWS // 8, fill, 0)
-
-    def cond_at(r):
-        return conduct[pl.ds((r // 8) * 64 + r % 8, 8, 8), :]
-
-    def defect(i, carry):
-        start = 1 + i * 31
-        for j in range(31):
-            r = start + j
-            c = cond_at(r)
-            d = 1.0 + 4.0 * c
-            right = source[pl.ds(7 * 512 + (r // 8) * 64 + r % 8, 8, 8), :]
-            e[r] = (right + g[0, r] - d * g[1, r] + c * around(beside, g, 1, r)) * (DAMP / d)
-        return carry
-
-    lax.fori_loop(0, 2, defect, 0)
-
-    def smooth(i, carry):
-        start = 2 + i * 30
-        for j in range(30):
-            r = start + j
-            c = cond_at(r)
-            q = c / (1.0 + 4.0 * c)
-            out[ROWS - 2 + r] = g[1, r] + e[r] + q * (e[r - 1] + e[r + 1] + beside(e[r]))
-        return carry
-
-    lax.fori_loop(0, 2, smooth, 0)
-    for n, r in enumerate((0, ROWS - 1)):
-        out[124 + n] = at(source, 7, r) + g[0, r]
-    for n, r in enumerate((1, 2, 61, 62)):
-        out[126 + n] = e[r]
+            out[r] = guess[tile_at(7, i, j), :]
+            out[ROWS + r] = source[tile_at(7, i, j), :] + guess[tile_at(6, i, j), :]
 
 
 def interior(is_first, guess, source, start, conduct, g, s, co, u, rs, e0, e1, tmp):
@@ -271,25 +231,25 @@
     beside = beside_maker()
     odd = is_odd[0]
     for source, side in ((near, 1 - odd), (far, odd)):
-        for j in range(6):
+        for j in range(10):
             for t in range(2, 8):
-                g[t, 5 + 70 * side + j] = source[(t - 2) * 6 + j]
-        for j in range(5):
+                g[t, 1 + 74 * side + j] = source[(t - 2) * 10 + j]
+        for j in range(9):
             for t in range(3, 8):
-                s[t, 6 + 69 * side + j] = source[36 + (t - 3) * 5 + j]
-            coefficients(co, 6 + 69 * side + j, source[61 + j])
+                s[t, 2 + 73 * side + j] = source[60 + (t - 3) * 9 + j]
+            coefficients(co, 2 + 73 * side + j, source[105 + j])
     st = Stages(beside, co)
-
-    both(3, 5, st.fine_defect(tmp, g, lambda t, r: g[t - 1, r], s, range(3, 8)))
-    both(2, 4, st.smoothed(u, g, tmp, range(3, 8), Q))
-    both(3, 3, st.restricted(rs, tmp, u, lambda t, r: u[t - 1, r], s, (2, 3)))
+    both(3, 9, st.fine_defect(tmp, g, lambda t, r: g[t - 1, r], s, range(3, 8)))
+    both(2, 8, st.smoothed(u, g, tmp, range(3, 8), Q))
+    both(3, 7, st.restricted(rs, tmp, u, lambda t, r: u[t - 1, r], s, (2, 3)))
     both(5, -3, scaled(co, rs, tmp))
-    both(4, 2, st.smoothed(e0, None, tmp, (2, 3), KQ))
-    both(7, 1, st.coarse_defect(tmp, e0, lambda m, r: e0[m - 1, r], rs, (3,)))
-    both(6, 0, st.smoothed(e1, e0, tmp, (3,), KQ))
-    for r in range(ROWS):
-        out[r] = e0[3, HALO + r]
-        out[ROWS + r] = e1[3, HALO + r]
+    both(4, 6, st.smoothed(e0, None, tmp, (2, 3), KQ))
+    both(7, 5, st.coarse_defect(tmp, e0, lambda m, r: e0[m - 1, r], rs, (3,)))
+    both(6, 4, st.smoothed(e1, e0, tmp, (3,), KQ))
+    for r in range(76):
+        out[r] = e0[3, HALO - 6 + r]
+    for r in range(72):
+        out[76 + r] = e1[3, HALO - 4 + r]
 
 
 def rest(
@@ -303,23 +263,22 @@
         for j in range(11):
             for t in range(2):
                 g[t, 75 * side + j] = source[t * 11 + j]
-        for j in range(5):
-            for t in range(2, 8):
-                g[t, 81 * side + j] = source[22 + (t - 2) * 5 + j]
-            for t in range(3, 8):
-                s[t, 1 + 79 * side + j] = source[82 + (t - 3) * 5 + j]
-            coefficients(co, 1 + 79 * side + j, source[107 + j])
+        for t in range(2, 8):
+            g[t, 85 * side] = source[20 + t]
+        for t in range(3, 8):
+            s[t, 1 + 83 * side] = source[55 + t]
+        coefficients(co, 1 + 83 * side, source[63])
         for j in range(10):
             for t in range(3):
-                s[t, 1 + 74 * side + j] = source[52 + t * 10 + j]
-            co[ST, 1 + 74 * side + j] = source[112 + j]
-    both(-3, 10, st.fine_defect(tmp, g, lambda t, r: g[t - 1, r], s, range(3, 8)))
-    both(-4, 9, st.smoothed(u, g, tmp, range(3, 8), Q))
-    both(-3, 8, st.restricted(rs, tmp, u, lambda t, r: u[t - 1, r], s, (2, 3)))
-    both(-1, 3, scaled(co, rs, tmp))
-    both(-2, 7, st.smoothed(e0, None, tmp, (2, 3), KQ))
-    both(1, 6, st.coarse_defect(tmp, e0, lambda m, r: e0[m - 1, r], rs, (3,)))
-    both(0, 5, st.smoothed(e1, e0, tmp, (3,), KQ))
+                s[t, 1 + 74 * side + j] = source[28 + t * 10 + j]
+            co[ST, 1 + 74 * side + j] = source[64 + j]
+    both(-7, 10, st.fine_defect(tmp, g, lambda t, r: g[t - 1, r], s, range(3, 8)))
+    both(-8, 9, st.smoothed(u, g, tmp, range(3, 8), Q))
+    both(-7, 8, st.restricted(rs, tmp, u, lambda t, r: u[t - 1, r], s, (2, 3)))
+    both(-5, 7, scaled(co, rs, tmp))
+    both(-6, 7, st.smoothed(e0, None, tmp, (2, 3), KQ))
+    both(-3, 6, st.coarse_defect(tmp, e0, lambda m, r: e0[m - 1, r], rs, (3,)))
+    both(-4, 5, st.smoothed(e1, e0, tmp, (3,), KQ))
     sweep(-10, 74, 90, st.fine_defect(tmp, g, lambda t, r: g[t - 1, r], s, (1, 2)))
     sweep(-9, 73, 90, st.smoothed(u, g, tmp, (1, 2), Q))
     sweep(-8, 72, 90, st.restricted(rs, tmp, u, lambda t, r: u[t - 1, r], s, (1,)))
@@ -341,11 +300,8 @@
     for out, side in ((near, 1 - odd), (far, odd)):
         for j in range(10):
             out[j] = t0[54 * side + j]
-        for j in range(6):
-            out[10 + j] = t0[ROWS + 54 * side + j]
-        for j in range(2):
-            out[16 + j] = t0[126 + 2 * side + j]
-        out[18] = t0[124 + side]
+        for j in range(9):
+            out[10 + j] = t0[ROWS + 55 * side + j]
 
 
 def middle(
@@ -357,33 +313,24 @@
     st = Stages(beside, co)
     odd = is_odd[0]
 
-    def fill(i, carry):
-        for j in range(16):
-            r = i * 16 + j
-            gb[0, HALO + r] = t0[r]
-            q = jnp.minimum(r, 59)
-            before[HALO + 2 + q] = t0[ROWS + q] + co[ST, HALO + 2 + q]
-        return carry
-
-    lax.fori_loop(0, ROWS // 16, fill, 0)
+    for r in range(ROWS):
+        gb[0, HALO + r] = t0[r]
+        br[0, HALO + r] = t0[ROWS + r]
     for source, side in ((near, 1 - odd), (far, odd)):
         for j in range(10):
             gb[0, 1 + 74 * side + j] = source[j]
-        for j in range(6):
-            r = 3 + 74 * side + j
-            before[r] = source[10 + j] + co[ST, r]
-        for j in range(2):
-            er[8 + 68 * side + j] = source[16 + j]
-        br[10 + 65 * side] = source[18]
-    for n, r in enumerate((HALO, HALO + 63)):
-        br[r] = t0[124 + n]
-    for n, r in enumerate((1, 2, 61, 62)):
-        er[HALO + r] = t0[126 + n]
-    for r in (10, 11, 74, 75):
-        er[r] = (br[r] - co[D, r] * gb[0, r] + co[C, r] * around(beside, gb, 0, r)) * co[INV, r]
-    for r in (9, 10, 11, 12, 73, 74, 75, 76):
-        edge = gb[0, r] + er[r] + co[Q, r] * (er[r - 1] + er[r + 1] + beside(er[r]))
-        before[r] = edge + co[ST, r]
+        for j in range(9):
+            br[0, 2 + 73 * side + j] = source[10 + j]
+
+    def earlier_defect(r):
+        er[0, r] = (br[0, r] - co[D, r] * gb[0, r] + co[C, r] * around(beside, gb, 0, r)) * co[INV, r]
+
+    def earlier_smooth(r):
+        value = gb[0, r] + er[0, r] + co[Q, r] * around(beside, er, 0, r)
+        before[r] = value + co[ST, r]
+
+    sweep(-9, 73, 90, earlier_defect)
+    sweep(-8, 72, 90, earlier_smooth)
     sweep(-10, 74, 90, st.fine_defect(tmp, g, lambda t, r: gb[0, r] + co[ST, r], s, (0,)))
     sweep(-9, 73, 90, st.smoothed(u, g, tmp, (0,), Q))
     sweep(-8, 72, 90, st.restricted(rs, tmp, u, lambda t, r: u[0, r] if t else before[r], s, (0,)))
@@ -421,34 +368,15 @@
     lax.fori_loop(0, ROWS // 8, copy, 0)
 
 
-def relay_late(is_odd, t2, near, far):
-    odd = is_odd[0]
-    for out, side in ((near, 1 - odd), (far, odd)):
-        for j in range(6):
-            out[j] = t2[58 * side + j]
-        for j in range(4):
-            out[6 + j] = t2[ROWS + 60 * side + j]
-
-
 def late(
-    is_odd, t2, near, far, s, co, u, rs, e0, e1_in, e2_in, sol7, sol_out, res_out, u2_out, sol2,
-    old, e1, u2, tmp, sol, sol_nat, res_nat, sems,
+    t2, s, co, u, rs, e0, e1_in, e2_in, sol7, sol_out, res_out, u2_out, sol2, e1, u2, tmp, sol, sol_nat, res_nat, sems
 ):
     beside = beside_maker()
     st = Stages(beside, co)
-    odd = is_odd[0]
-    for source, side in ((near, 1 - odd), (far, odd)):
-        for j in range(6):
-            old[0, 5 + 70 * side + j] = source[j]
-        for j in range(4):
-            old[1, 7 + 68 * side + j] = source[6 + j]
-
-    def earlier_step(n, r):
-        return t2[n * ROWS + r - HALO] if HALO <= r < HALO + ROWS else old[n, r]
 
     def first_defect(r):
         tmp[0, r] = (
-            rs[0, r] + earlier_step(0, r) - co[KD, r] * e0[0, r] + co[K, r] * around(beside, e0, 0, r)
+            rs[0, r] + t2[r - (HALO - 6)] - co[KD, r] * e0[0, r] + co[K, r] * around(beside, e0, 0, r)
         ) * co[KINV, r]
 
     sweep(-6, 70, 90, first_defect)
@@ -461,7 +389,7 @@
 
     def second_defect(r):
         k, kd, kinv = co[K, r], co[KD, r], co[KINV, r]
-        earlier = (earlier_step(1, r), e1[0, r])
+        earlier = (t2[76 + r - (HALO - 4)], e1[0, r])
         for m in (0, 1):
             tmp[m, r] = (rs[m, r] + earlier[m] - kd * e1[m, r] + k * around(beside, e1, m, r)) * kinv
 
@@ -518,8 +446,8 @@
         copy.wait()
 
 
-def finish(t3, s, co, before, u2_in, sol2, sol_in, sol_out, res, u2, tmp, sol, sol_nat, sem):
-    del sol_in
+def finish(t3, s, co, before, u2_in, sol2, sol_in, res_in, sol_out, res_out, base, u2, tmp, sol, sol_nat, res, sems):
+    del sol_in, res_in
     beside = beside_maker()
 
     def corrected(r):
@@ -546,28 +474,28 @@
 
     sweep(-1, 65, 90, final)
 
-    copy = pltpu.make_async_copy(sol_nat, sol_out.at[pl.ds(0, 2)], sem)
-    copy.start()
+    copies = [pltpu.make_async_copy(sol_nat, sol_out.at[pl.ds(0, 2)], sems.at[0])]
+    copies[0].start()
     for i in range(ROWS // 8):
         for j in range(8):
             r = HALO + 8 * i + j
             c, d = co[C, r], co[D, r]
             first, second = sol[0, r], sol[1, r]
             spot = tile_at(0, i, j)
-            res[0, spot, :] = s[0, r] + co[ST, r] - d * first + c * around(beside, sol, 0, r)
-            res[1, spot, :] = s[1, r] + first - d * second + c * around(beside, sol, 1, r)
-            res[2, spot, :] = s[2, r] + second - d * sol2[0, r] + c * around(beside, sol2, 0, r)
-    copy.wait()
-
-
-def tail(t4, res, res_in, res_out, total, sems):
+            base[spot, :] = s[0, r] + co[ST, r] - d * first + c * around(beside, sol, 0, r)
+            res[0, spot, :] = s[1, r] + first - d * second + c * around(beside, sol, 1, r)
+            res[1, spot, :] = s[2, r] + second - d * sol2[0, r] + c * around(beside, sol2, 0, r)
+    copies.append(pltpu.make_async_copy(res, res_out.at[pl.ds(1, 2)], sems.at[1]))
+    copies[1].start()
+    for copy in copies:
+        copy.wait()
+
+
+def tail(t4, base, res_in, res_out, total, sem):
     del res_in
-    ready = pltpu.make_async_copy(res.at[pl.ds(1, 2)], res_out.at[pl.ds(1, 2)], sems.at[0])
-    ready.start()
-    total[...] = res[pl.ds(0, 1)] + t4[...][None]
-    copy = pltpu.make_async_copy(total, res_out.at[pl.ds(0, 1)], sems.at[1])
+    total[0] = base[...] + t4[...]
+    copy = pltpu.make_async_copy(total, res_out.at[pl.ds(0, 1)], sem)
     copy.start()
-    ready.wait()
     copy.wait()
 
 
@@ -615,21 +543,15 @@
     near, far, near_late, far_late, guess_v, source_v, start_v, conduct_v = call(
         edge_pack,
         (is_first, is_odd, by_step(guess_v), by_step(source_v), by_step(start_v), by_step(conduct_v)),
-        [rows_of(66), rows_of(66), rows_of(122), rows_of(122), stepped(8), stepped(8), stepped(1), stepped(1)],
+        [rows_of(114), rows_of(114), rows_of(74), rows_of(74), stepped(8), stepped(8), stepped(1), stepped(1)],
         [dma((4, 3))],
         specs=[SMEM, SMEM] + [ANY] * 4,
         limit=1,
     )
     guess_v, source_v, start_v, conduct_v = (x.reshape(-1, 128) for x in (guess_v, source_v, start_v, conduct_v))
-    (send0,) = call(
-        last_step_pack,
-        (guess_v, source_v, conduct_v),
-        [rows_of(130)],
-        [pltpu.VMEM((2, ROWS, 8, 128), F32), pltpu.VMEM((ROWS, 8, 128), F32)],
-        limit=4,
-    )
+    far_in = along(far, "space", off_chip)
+    (send0,) = call(last_step_pack, (guess_v, source_v), [rows_of(128)], limit=1)
     t0 = along(send0, "tm", ahead)
-    far_in = along(far, "space", off_chip)
     near_in = along(near, "space", on_chip)
     far_late_in = along(far_late, "space", off_chip)
     near_late_in = along(near_late, "space", on_chip)
@@ -644,7 +566,7 @@
     g, s, co, u, rs, e0, e1, send2 = call(
         edges,
         (is_odd, near_in, far_in, g, s, co, u, rs, e0, e1),
-        [ext(8), ext(8), ext(9), ext(8), ext(4), ext(4), ext(4), rows_of(128)],
+        [ext(8), ext(8), ext(9), ext(8), ext(4), ext(4), ext(4), rows_of(148)],
         [vmem(8)],
         aliases={n + 3: n for n in range(7)},
         specs=[SMEM] + [FULL] * 9,
@@ -668,40 +590,36 @@
         middle,
         (is_odd, t0, near_in, far_in, g, s, co, u, rs, e0, e1, e2),
         [ext(8), ext(4), ext(4), ext(4), ext(4), rows_of(EXT), ext(1), one],
-        [vmem(1), pltpu.VMEM((EXT, 8, 128), F32), pltpu.VMEM((EXT, 8, 128), F32), vmem(4), vmem(2)],
+        [vmem(1), vmem(1), vmem(1), vmem(4), vmem(2)],
         aliases={n + 7: n for n in range(5)},
         specs=[SMEM] + [FULL] * 11,
         limit=6,
     )
     t4 = along(send4, "tm", ahead)
     nat3 = lambda steps: pltpu.VMEM((steps, ROWS * 8, 128), F32)
-    near, far = call(relay_late, (is_odd, t2), [rows_of(10), rows_of(10)], specs=[SMEM, FULL], limit=1)
-    far_in = along(far, "space", off_chip)
-    near_in = along(near, "space", on_chip)
     sol, res, u2, sol2 = call(
         late,
-        (is_odd, t2, near_in, far_in, s, co, u, rs, e0, e1, e2, sol7),
+        (t2, s, co, u, rs, e0, e1, e2, sol7),
         [stepped(8), stepped(8), ext(2), ext(1)],
-        [vmem(2), vmem(2), vmem(8), vmem(8), vmem(8), nat3(6), nat3(5), dma((3,))],
-        specs=[SMEM] + [FULL] * 11,
+        [vmem(2), vmem(8), vmem(8), vmem(8), nat3(6), nat3(5), dma((3,))],
         out_specs=[ANY, ANY, FULL, FULL],
         limit=16,
     )
-    sol, first_res = call(
+    sol, res, base = call(
         finish,
-        (t3, s, co, before, u2, sol2, sol),
-        [stepped(8), stepped(3)],
-        [vmem(2), vmem(2), vmem(2), nat3(2), dma],
-        aliases={6: 0},
-        specs=[FULL] * 6 + [ANY],
-        out_specs=[ANY, FULL],
+        (t3, s, co, before, u2, sol2, sol, res),
+        [stepped(8), stepped(8), jax.ShapeDtypeStruct((ROWS * 8, 128), F32)],
+        [vmem(2), vmem(2), vmem(2), nat3(2), nat3(2), dma((2,))],
+        aliases={6: 0, 7: 1},
+        specs=[FULL] * 6 + [ANY] * 2,
+        out_specs=[ANY, ANY, FULL],
         limit=6,
     )
     (res,) = call(
         tail,
-        (t4, first_res, res),
+        (t4, base, res),
         [stepped(8)],
-        [nat3(1), dma((2,))],
+        [nat3(1), dma],
         aliases={2: 0},
         specs=[FULL, FULL, ANY],
         out_specs=[ANY],

time: 54.3 us -> 50 us (0.921)
  the two profiles are of different devices: /device:TPU:96 before, /device:TPU:64 now
where the time goes in v7:
time: 50 us; the launch traced here: 49.7 us
  starting transfers between devices  26 us (52%)
  Pallas kernels  20.1 us (40%)
  waiting for transfers between devices  2.58 us (5%)
  between operations  1 us (2%)
    ppermute x10, starting transfers between devices, along(): lax.ppermute(block, axis, [(i, j) for i, j in pairs if 0 <= j < count])  26 us
    pallas_call x10, Pallas kernels, call(): pl.pallas_call(kernel, out_shape=outs, in_specs=specs or [FULL] * len(ins...  20.1 us
    ppermute x10, waiting for transfers between devices, along(): lax.ppermute(block, axis, [(i, j) for i, j in pairs if 0 <= j < count])  2.58 us
  transfers between devices with their start and end apart: 10, of which 2 were waited for; matrix products, arithmetic and copies ran while one was open for 0% of the time, Pallas kernels for 34%

profile of v7, /device:TPU:64, one launch (start us, length us, event | category | flops | bytes accessed | tf_op | source)
XLA Modules:
  0.0 49.7 jit_solution(8111875479936490900)
XLA Ops:
  0.6 2.4 %shard_map.59 = (f32[114,8,128]{2,1,0:T(8,128)S(1)}, f32[114,8,128]{2,1,0:T(8,128)S(1)}, f32[74,8,128]{2,1,0:T(8,128)S(1)}, f32[74,8,128]{2,1,0:T(8,128)S(1)}, f...) custom-call(f32[1]{0:T(128)} %bitcast.1.is_first, ...), custom_call_target="tpu_custom_call" | custom-call | tf_op jit(solution)/shard_map/pallas_call | solution.py:503
  3.0 0.1 collective-permute-start.2
  3.1 4.6 %collective-permute-start.3 = (f32[114,8,128]{2,1,0:T(8,128)S(1)}, f32[114,8,128]{2,1,0:T(8,128)S(1)}, u32[]{:S(2)}, u32[]{:S(2)}) collective-permute-start(f32[114,8,128]{2,1,0:T(8,128)S(1)} %get-tuple-element.54), channel_id=1, source_target_pairs={{1,2},{2,1},{3,4},{4,3},{5,6},{6,5},{7,8},{8,7},{9,10},{10,9},{11,... | collective-permute-start | bytes 1400840 | tf_op jit(solution)/shard_map/ppermute | solution.py:517
  7.7 0.1 shard_map.63
  7.8 3.4 %collective-permute-start.5 = (f32[128,8,128]{2,1,0:T(8,128)S(1)}, f32[128,8,128]{2,1,0:T(8,128)S(1)}, u32[]{:S(2)}, u32[]{:S(2)}) collective-permute-start(f32[128,8,128]{2,1,0:T(8,128)S(1)} %shard_map.63), channel_id=1, source_target_pairs={{0,32},{32,64},{64,96},{1,33},{33,65},{65,97},{2,34},{34,66},{66,9... | collective-permute-start | bytes 1572872 | tf_op jit(solution)/shard_map/ppermute | solution.py:517
  11.3 3.7 %shard_map.60 = (f32[8,86,8,128]{3,2,1,0:T(8,128)S(1)}, f32[8,86,8,128]{3,2,1,0:T(8,128)S(1)}, f32[9,86,8,128]{3,2,1,0:T(8,128)S(1)}, f32[8,86,8,128]{3,2,1,0:T(...) custom-call(f32[1]{0:T(128)} %bitcast.1.is_first, ...), custom_call_target="tpu_custom_call" | custom-call | tf_op jit(solution)/shard_map/pallas_call | solution.py:503
  15.0 0.0 collective-permute-done.2.near
  15.0 0.1 collective-permute-done.3.far
  15.1 1.0 %shard_map.61 = (f32[8,86,8,128]{3,2,1,0:T(8,128)S(1)}, f32[8,86,8,128]{3,2,1,0:T(8,128)S(1)}, f32[9,86,8,128]{3,2,1,0:T(8,128)S(1)}, f32[8,86,8,128]{3,2,1,0:T(...) custom-call(s32[1]{0:T(128)} %bitcast.is_odd, ...), custom_call_target="tpu_custom_call", output_to_operand_aliasing={{0}: (3, {}), {1}: (4, {}), {2}: (5, {}), {3}: (6, {}), {4}... | custom-call | tf_op jit(solution)/shard_map/pallas_call | solution.py:503
  16.2 3.4 %collective-permute-start.8 = (f32[148,8,128]{2,1,0:T(8,128)S(1)}, f32[148,8,128]{2,1,0:T(8,128)S(1)}, u32[]{:S(2)}, u32[]{:S(2)}) collective-permute-start(f32[148,8,128]{2,1,0:T(8,128)S(1)} %get-tuple-element.85), channel_id=1, source_target_pairs={{0,32},{32,64},{64,96},{1,33},{33,65},{65,97},{2,34},{34,66},{66,9... | collective-permute-start | bytes 1818632 | tf_op jit(solution)/shard_map/ppermute | solution.py:517
  19.6 0.1 collective-permute-start
  19.7 4.3 %collective-permute-start.1 = (f32[74,8,128]{2,1,0:T(8,128)S(1)}, f32[74,8,128]{2,1,0:T(8,128)S(1)}, u32[]{:S(2)}, u32[]{:S(2)}) collective-permute-start(f32[74,8,128]{2,1,0:T(8,128)S(1)} %get-tuple-element.52), channel_id=1, source_target_pairs={{1,2},{2,1},{3,4},{4,3},{5,6},{6,5},{7,8},{8,7},{9,10},{10,9},{11,... | collective-permute-start | bytes 909320 | tf_op jit(solution)/shard_map/ppermute | solution.py:517
  24.0 0.0 collective-permute-done.5.t0
  24.0 0.1 collective-permute-start.6
  24.1 3.4 %collective-permute-start.7 = (f32[19,8,128]{2,1,0:T(8,128)S(1)}, f32[19,8,128]{2,1,0:T(8,128)S(1)}, u32[]{:S(2)}, u32[]{:S(2)}) collective-permute-start(f32[19,8,128]{2,1,0:T(8,128)S(1)} %get-tuple-element.77), channel_id=1, source_target_pairs={{1,2},{2,1},{3,4},{4,3},{5,6},{6,5},{7,8},{8,7},{9,10},{10,9},{11,... | collective-permute-start | bytes 233480 | tf_op jit(solution)/shard_map/ppermute | solution.py:517
  27.5 0.0 collective-permute-done.near
  27.5 2.4 %collective-permute-done.1.far = f32[74,8,128]{2,1,0:T(8,128)S(1)} collective-permute-done((f32[74,8,128]{2,1,0:T(8,128)S(1)}, f32[74,8,128]{2,1,0:T(8,128)S(1)}, u32[]{:S(2)}, u32[]{:S(2)}) %collective-permute-start.1) | collective-permute-done | bytes 303136 | tf_op jit(solution)/shard_map/ppermute | solution.py:517
  30.0 2.5 %shard_map.62 = (f32[8,86,8,128]{3,2,1,0:T(8,128)S(1)}, f32[8,86,8,128]{3,2,1,0:T(8,128)S(1)}, f32[9,86,8,128]{3,2,1,0:T(8,128)S(1)}, f32[8,86,8,128]{3,2,1,0:T(...) custom-call(s32[1]{0:T(128)} %bitcast.is_odd, ...), custom_call_target="tpu_custom_call", output_to_operand_aliasing={{0}: (3, {}), {1}: (4, {}), {2}: (5, {}), {3}: (6, {}), {4}... | custom-call | tf_op jit(solution)/shard_map/pallas_call | solution.py:503
  32.5 3.4 %collective-permute-start.4 = (f32[70,8,128]{2,1,0:T(8,128)S(1)}, f32[70,8,128]{2,1,0:T(8,128)S(1)}, u32[]{:S(2)}, u32[]{:S(2)}) collective-permute-start(f32[70,8,128]{2,1,0:T(8,128)S(1)} %get-tuple-element.73), channel_id=1, source_target_pairs={{0,32},{32,64},{64,96},{1,33},{33,65},{65,97},{2,34},{34,66},{66,9... | collective-permute-start | bytes 860168 | tf_op jit(solution)/shard_map/ppermute | solution.py:517
  35.9 0.0 collective-permute-done.6.near
  35.9 0.0 collective-permute-done.7.far
  35.9 2.8 %shard_map.65 = (f32[8,86,8,128]{3,2,1,0:T(8,128)S(1)}, f32[4,86,8,128]{3,2,1,0:T(8,128)S(1)}, f32[4,86,8,128]{3,2,1,0:T(8,128)S(1)}, f32[4,86,8,128]{3,2,1,0:T(...) custom-call(s32[1]{0:T(128)} %bitcast.is_odd, ...), custom_call_target="tpu_custom_call", output_to_operand_aliasing={{0}: (7, {}), {1}: (8, {}), {2}: (9, {}), {3}: (10, {}), {4... | custom-call | tf_op jit(solution)/shard_map/pallas_call | solution.py:503
  38.7 3.3 %collective-permute-start.9 = (f32[512,128]{1,0:T(8,128)S(1)}, f32[512,128]{1,0:T(8,128)S(1)}, u32[]{:S(2)}, u32[]{:S(2)}) collective-permute-start(f32[512,128]{1,0:T(8,128)S(1)} %get-tuple-element.97), channel_id=1, source_target_pairs={{0,32},{32,64},{64,96},{1,33},{33,65},{65,97},{2,34},{34,66},{66,9... | collective-permute-start | bytes 786440 | tf_op jit(solution)/shard_map/ppermute | solution.py:517
  42.0 0.0 collective-permute-done.8.t2
  42.0 4.8 %shard_map.66 = (f32[8,512,128]{2,1,0:T(8,128)}, f32[8,512,128]{2,1,0:T(8,128)}, f32[2,86,8,128]{3,2,1,0:T(8,128)S(1)}, f32[1,86,8,128]{3,2,1,0:T(8,128)S(1)}) custom-call(f32[148,8,128]{2,1,0:T(8,128)S(1)} %collective-permute-done.8.t2, f32[8,86,8,128]{3,2,1,0:T(8,128)S(1)} %get-tuple-element.74.s, f32[9,86,8,128]{3,2,1,0:T(8,128)S(1)} %get-tuple-element.75.co, ...), custom_call_target="tpu_custom_call" | custom-call | tf_op jit(solution)/shard_map/pallas_call | solution.py:503
  46.8 0.0 collective-permute-done.4.t3
  46.8 2.0 %shard_map.67 = (f32[8,512,128]{2,1,0:T(8,128)}, f32[8,512,128]{2,1,0:T(8,128)}, f32[512,128]{1,0:T(8,128)S(1)}) custom-call(f32[70,8,128]{2,1,0:T(8,128)S(1)} %collective-permute-done.4.t3, f32[8,86,8,128]{3,2,1,0:T(8,128)S(1)} %get-tuple-element.74.s, f32[9,86,8,128]{3,2,1,0:T(8,128)S(1)} %get-tuple-element.75.co, ...), custom_call_target="tpu_custom_call", output_to_operand_aliasing={{0}: (6, {}), {1}: (7, {})} | custom-call | tf_op jit(solution)/shard_map/pallas_call | solution.py:503
  48.8 0.0 collective-permute-done.9.t4
  48.8 0.7 %shard_map.68 = f32[8,512,128]{2,1,0:T(8,128)} custom-call(f32[512,128]{1,0:T(8,128)S(1)} %collective-permute-done.9.t4, f32[512,128]{1,0:T(8,128)S(1)} %get-tuple-element.98.base, f32[8,512,128]{2,1,0:T(8,128)} %get-tuple-element.99.res_in), custom_call_target="tpu_custom_call", output_to_operand_aliasing={{}: (2, {})} | custom-call | tf_op jit(solution)/shard_map/pallas_call | solution.py:503
  (1 shorter events, 0.0 us)
Async XLA Ops:
  3.0 11.9 %collective-permute-start.2 = (f32[114,8,128]{2,1,0:T(8,128)S(1)}, f32[114,8,128]{2,1,0:T(8,128)S(1)}, u32[]{:S(2)}, u32[]{:S(2)}) collective-permute-start(f32[114,8,128]{2,1,0:T(8,128)S(1)} %get-tuple-element.53), channel_id=1, source_target_pairs={{0,1},{1,0},{2,3},{3,2},{4,5},{5,4},{6,7},{7,6},{8,9},{9,8},{10,11... | collective-permute-start | bytes 1400840 | tf_op jit(solution)/shard_map/ppermute | solution.py:517
  3.1 12.0 %collective-permute-start.3 = (f32[114,8,128]{2,1,0:T(8,128)S(1)}, f32[114,8,128]{2,1,0:T(8,128)S(1)}, u32[]{:S(2)}, u32[]{:S(2)}) collective-permute-start(f32[114,8,128]{2,1,0:T(8,128)S(1)} %get-tuple-element.54), channel_id=1, source_target_pairs={{1,2},{2,1},{3,4},{4,3},{5,6},{6,5},{7,8},{8,7},{9,10},{10,9},{11,... | collective-permute-start | bytes 1400840 | tf_op jit(solution)/shard_map/ppermute | solution.py:517
  7.8 16.2 %collective-permute-start.5 = (f32[128,8,128]{2,1,0:T(8,128)S(1)}, f32[128,8,128]{2,1,0:T(8,128)S(1)}, u32[]{:S(2)}, u32[]{:S(2)}) collective-permute-start(f32[128,8,128]{2,1,0:T(8,128)S(1)} %shard_map.63), channel_id=1, source_target_pairs={{0,32},{32,64},{64,96},{1,33},{33,65},{65,97},{2,34},{34,66},{66,9... | collective-permute-start | bytes 1572872 | tf_op jit(solution)/shard_map/ppermute | solution.py:517
  16.2 25.8 %collective-permute-start.8 = (f32[148,8,128]{2,1,0:T(8,128)S(1)}, f32[148,8,128]{2,1,0:T(8,128)S(1)}, u32[]{:S(2)}, u32[]{:S(2)}) collective-permute-start(f32[148,8,128]{2,1,0:T(8,128)S(1)} %get-tuple-element.85), channel_id=1, source_target_pairs={{0,32},{32,64},{64,96},{1,33},{33,65},{65,97},{2,34},{34,66},{66,9... | collective-permute-start | bytes 1818632 | tf_op jit(solution)/shard_map/ppermute | solution.py:517
  19.6 7.9 %collective-permute-start = (f32[74,8,128]{2,1,0:T(8,128)S(1)}, f32[74,8,128]{2,1,0:T(8,128)S(1)}, u32[]{:S(2)}, u32[]{:S(2)}) collective-permute-start(f32[74,8,128]{2,1,0:T(8,128)S(1)} %get-tuple-element.51), channel_id=1, source_target_pairs={{0,1},{1,0},{2,3},{3,2},{4,5},{5,4},{6,7},{7,6},{8,9},{9,8},{10,11... | collective-permute-start | bytes 909320 | tf_op jit(solution)/shard_map/ppermute | solution.py:517
  19.7 10.2 %collective-permute-start.1 = (f32[74,8,128]{2,1,0:T(8,128)S(1)}, f32[74,8,128]{2,1,0:T(8,128)S(1)}, u32[]{:S(2)}, u32[]{:S(2)}) collective-permute-start(f32[74,8,128]{2,1,0:T(8,128)S(1)} %get-tuple-element.52), channel_id=1, source_target_pairs={{1,2},{2,1},{3,4},{4,3},{5,6},{6,5},{7,8},{8,7},{9,10},{10,9},{11,... | collective-permute-start | bytes 909320 | tf_op jit(solution)/shard_map/ppermute | solution.py:517
  24.0 11.9 %collective-permute-start.6 = (f32[19,8,128]{2,1,0:T(8,128)S(1)}, f32[19,8,128]{2,1,0:T(8,128)S(1)}, u32[]{:S(2)}, u32[]{:S(2)}) collective-permute-start(f32[19,8,128]{2,1,0:T(8,128)S(1)} %get-tuple-element.76), channel_id=1, source_target_pairs={{0,1},{1,0},{2,3},{3,2},{4,5},{5,4},{6,7},{7,6},{8,9},{9,8},{10,11... | collective-permute-start | bytes 233480 | tf_op jit(solution)/shard_map/ppermute | solution.py:517
  24.1 11.8 %collective-permute-start.7 = (f32[19,8,128]{2,1,0:T(8,128)S(1)}, f32[19,8,128]{2,1,0:T(8,128)S(1)}, u32[]{:S(2)}, u32[]{:S(2)}) collective-permute-start(f32[19,8,128]{2,1,0:T(8,128)S(1)} %get-tuple-element.77), channel_id=1, source_target_pairs={{1,2},{2,1},{3,4},{4,3},{5,6},{6,5},{7,8},{8,7},{9,10},{10,9},{11,... | collective-permute-start | bytes 233480 | tf_op jit(solution)/shard_map/ppermute | solution.py:517
  32.5 14.3 %collective-permute-start.4 = (f32[70,8,128]{2,1,0:T(8,128)S(1)}, f32[70,8,128]{2,1,0:T(8,128)S(1)}, u32[]{:S(2)}, u32[]{:S(2)}) collective-permute-start(f32[70,8,128]{2,1,0:T(8,128)S(1)} %get-tuple-element.73), channel_id=1, source_target_pairs={{0,32},{32,64},{64,96},{1,33},{33,65},{65,97},{2,34},{34,66},{66,9... | collective-permute-start | bytes 860168 | tf_op jit(solution)/shard_map/ppermute | solution.py:517
  38.7 10.1 %collective-permute-start.9 = (f32[512,128]{1,0:T(8,128)S(1)}, f32[512,128]{1,0:T(8,128)S(1)}, u32[]{:S(2)}, u32[]{:S(2)}) collective-permute-start(f32[512,128]{1,0:T(8,128)S(1)} %get-tuple-element.97), channel_id=1, source_target_pairs={{0,32},{32,64},{64,96},{1,33},{33,65},{65,97},{2,34},{34,66},{66,9... | collective-permute-start | bytes 786440 | tf_op jit(solution)/shard_map/ppermute | solution.py:517

commit v8 on v7

--- a/solution.py
+++ b/solution.py
@@ -135,7 +135,7 @@
 
 
 def edge_pack(
-    is_first, is_odd, guess, source, start, conduct, near, far, near_late, far_late, gb, sb, tb, cb, sems
+    is_first, is_odd, guess, source, start, conduct, near, far, gb, sb, tb, cb, sems
 ):
     pairs = ((guess, gb), (source, sb), (start, tb), (conduct, cb))
 
@@ -162,22 +162,12 @@
 
         lax.fori_loop(0, count, body, 0, unroll=True)
 
-    for out, late_out, side in ((near, near_late, 1 - odd), (far, far_late, odd)):
-        for t in range(2, 8):
-            grab(out, (t - 2) * 10, gb, t, 54 * side, 10)
-        for t in range(3, 8):
-            grab(out, 60 + (t - 3) * 9, sb, t, 55 * side, 9)
-        grab(out, 105, cb, 0, 55 * side, 9)
-        for t in range(2):
-            grab(late_out, t * 11, gb, t, 53 * side, 11)
-        for t in range(2, 8):
-            grab(late_out, 20 + t, gb, t, 10 + 43 * side, 1)
-        for t in range(3):
-            grab(late_out, 28 + t * 10, sb, t, 54 * side, 10)
-        for t in range(3, 8):
-            grab(late_out, 55 + t, sb, t, 9 + 45 * side, 1)
-        grab(late_out, 63, cb, 0, 9 + 45 * side, 1)
-        grab(late_out, 64, tb, 0, 54 * side, 10, is_first[0])
+    for out, side in ((near, 1 - odd), (far, odd)):
+        for t in range(8):
+            grab(out, t * 11, gb, t, 53 * side, 11)
+            grab(out, 88 + t * 10, sb, t, 54 * side, 10)
+        grab(out, 168, cb, 0, 54 * side, 10)
+        grab(out, 178, tb, 0, 54 * side, 10, is_first[0])
     for copy in inner_tiles:
         copy.wait()
 
@@ -190,7 +180,7 @@
             out[ROWS + r] = source[tile_at(7, i, j), :] + guess[tile_at(6, i, j), :]
 
 
-def interior(is_first, guess, source, start, conduct, g, s, co, u, rs, e0, e1, tmp):
+def interior(is_first, guess, source, start, conduct, g, s, co, u, rs, e0, e1, send, tmp):
     beside = beside_maker()
 
     def fill(i, carry):
@@ -211,6 +201,10 @@
     sweep(4, 60, 90, st.smoothed(e0, None, tmp, (2, 3), KQ))
     sweep(5, 59, 90, st.coarse_defect(tmp, e0, lambda m, r: e0[m - 1, r], rs, (3,)))
     sweep(6, 58, 90, st.smoothed(e1, e0, tmp, (3,), KQ))
+    for r in range(4, 60):
+        send[r - 4] = e0[3, HALO + r]
+    for r in range(6, 58):
+        send[50 + r] = e1[3, HALO + r]
 
 
 def both(inner, depth, body):
@@ -231,54 +225,33 @@
     beside = beside_maker()
     odd = is_odd[0]
     for source, side in ((near, 1 - odd), (far, odd)):
+        for j in range(11):
+            for t in range(8):
+                g[t, 75 * side + j] = source[t * 11 + j]
         for j in range(10):
-            for t in range(2, 8):
-                g[t, 1 + 74 * side + j] = source[(t - 2) * 10 + j]
-        for j in range(9):
-            for t in range(3, 8):
-                s[t, 2 + 73 * side + j] = source[60 + (t - 3) * 9 + j]
-            coefficients(co, 2 + 73 * side + j, source[105 + j])
+            for t in range(8):
+                s[t, 1 + 74 * side + j] = source[88 + t * 10 + j]
+            coefficients(co, 1 + 74 * side + j, source[168 + j])
+            co[ST, 1 + 74 * side + j] = source[178 + j]
     st = Stages(beside, co)
-    both(3, 9, st.fine_defect(tmp, g, lambda t, r: g[t - 1, r], s, range(3, 8)))
-    both(2, 8, st.smoothed(u, g, tmp, range(3, 8), Q))
-    both(3, 7, st.restricted(rs, tmp, u, lambda t, r: u[t - 1, r], s, (2, 3)))
+    both(3, 10, st.fine_defect(tmp, g, lambda t, r: g[t - 1, r], s, range(3, 8)))
+    both(2, 9, st.smoothed(u, g, tmp, range(3, 8), Q))
+    both(3, 8, st.restricted(rs, tmp, u, lambda t, r: u[t - 1, r], s, (2, 3)))
     both(5, -3, scaled(co, rs, tmp))
-    both(4, 6, st.smoothed(e0, None, tmp, (2, 3), KQ))
-    both(7, 5, st.coarse_defect(tmp, e0, lambda m, r: e0[m - 1, r], rs, (3,)))
-    both(6, 4, st.smoothed(e1, e0, tmp, (3,), KQ))
-    for r in range(76):
-        out[r] = e0[3, HALO - 6 + r]
-    for r in range(72):
-        out[76 + r] = e1[3, HALO - 4 + r]
-
-
-def rest(
-    is_odd, near, far, g_in, s_in, co_in, u_in, rs_in, e0_in, e1_in, g, s, co, u, rs, e0, e1, e2, send, tmp
-):
-    del g_in, s_in, co_in, u_in, rs_in, e0_in, e1_in
+    both(4, 7, st.smoothed(e0, None, tmp, (2, 3), KQ))
+    both(7, 6, st.coarse_defect(tmp, e0, lambda m, r: e0[m - 1, r], rs, (3,)))
+    both(6, 5, st.smoothed(e1, e0, tmp, (3,), KQ))
+    for j in range(10):
+        out[j] = e0[3, HALO - 6 + j]
+        out[10 + j] = e0[3, HALO + 60 + j]
+        out[20 + j] = e1[3, HALO - 4 + j]
+        out[30 + j] = e1[3, HALO + 58 + j]
+
+
+def rest(g, s, co, u_in, rs_in, e0_in, e1_in, u, rs, e0, e1, e2, send, tmp):
+    del u_in, rs_in, e0_in, e1_in
     beside = beside_maker()
     st = Stages(beside, co)
-    odd = is_odd[0]
-    for source, side in ((near, 1 - odd), (far, odd)):
-        for j in range(11):
-            for t in range(2):
-                g[t, 75 * side + j] = source[t * 11 + j]
-        for t in range(2, 8):
-            g[t, 85 * side] = source[20 + t]
-        for t in range(3, 8):
-            s[t, 1 + 83 * side] = source[55 + t]
-        coefficients(co, 1 + 83 * side, source[63])
-        for j in range(10):
-            for t in range(3):
-                s[t, 1 + 74 * side + j] = source[28 + t * 10 + j]
-            co[ST, 1 + 74 * side + j] = source[64 + j]
-    both(-7, 10, st.fine_defect(tmp, g, lambda t, r: g[t - 1, r], s, range(3, 8)))
-    both(-8, 9, st.smoothed(u, g, tmp, range(3, 8), Q))
-    both(-7, 8, st.restricted(rs, tmp, u, lambda t, r: u[t - 1, r], s, (2, 3)))
-    both(-5, 7, scaled(co, rs, tmp))
-    both(-6, 7, st.smoothed(e0, None, tmp, (2, 3), KQ))
-    both(-3, 6, st.coarse_defect(tmp, e0, lambda m, r: e0[m - 1, r], rs, (3,)))
-    both(-4, 5, st.smoothed(e1, e0, tmp, (3,), KQ))
     sweep(-10, 74, 90, st.fine_defect(tmp, g, lambda t, r: g[t - 1, r], s, (1, 2)))
     sweep(-9, 73, 90, st.smoothed(u, g, tmp, (1, 2), Q))
     sweep(-8, 72, 90, st.restricted(rs, tmp, u, lambda t, r: u[t - 1, r], s, (1,)))
@@ -369,14 +342,22 @@
 
 
 def late(
-    t2, s, co, u, rs, e0, e1_in, e2_in, sol7, sol_out, res_out, u2_out, sol2, e1, u2, tmp, sol, sol_nat, res_nat, sems
+    t2, t2e, s, co, u, rs, e0, e1_in, e2_in, sol7, sol_out, res_out, u2_out, sol2, e1, u2, tmp, sol, sol_nat, res_nat, sems
 ):
     beside = beside_maker()
     st = Stages(beside, co)
 
+    def old0(r):
+        r -= HALO
+        return t2[r - 4] if 4 <= r < 60 else t2e[r + 6 if r < 4 else r - 50]
+
+    def old1(r):
+        r -= HALO
+        return t2[50 + r] if 6 <= r < 58 else t2e[r + 24 if r < 6 else r - 28]
+
     def first_defect(r):
         tmp[0, r] = (
-            rs[0, r] + t2[r - (HALO - 6)] - co[KD, r] * e0[0, r] + co[K, r] * around(beside, e0, 0, r)
+            rs[0, r] + old0(r) - co[KD, r] * e0[0, r] + co[K, r] * around(beside, e0, 0, r)
         ) * co[KINV, r]
 
     sweep(-6, 70, 90, first_defect)
@@ -389,7 +370,7 @@
 
     def second_defect(r):
         k, kd, kinv = co[K, r], co[KD, r], co[KINV, r]
-        earlier = (t2[76 + r - (HALO - 4)], e1[0, r])
+        earlier = (old1(r), e1[0, r])
         for m in (0, 1):
             tmp[m, r] = (rs[m, r] + earlier[m] - kd * e1[m, r] + k * around(beside, e1, m, r)) * kinv
 
@@ -540,55 +521,53 @@
 
     by_step = lambda x: pltpu.with_memory_space_constraint(x.reshape(-1, ROWS * 8, 128), pltpu.HBM)
     stepped = lambda steps: jax.ShapeDtypeStruct((steps, ROWS * 8, 128), F32)
-    near, far, near_late, far_late, guess_v, source_v, start_v, conduct_v = call(
+    near, far, guess_v, source_v, start_v, conduct_v = call(
         edge_pack,
         (is_first, is_odd, by_step(guess_v), by_step(source_v), by_step(start_v), by_step(conduct_v)),
-        [rows_of(114), rows_of(114), rows_of(74), rows_of(74), stepped(8), stepped(8), stepped(1), stepped(1)],
+        [rows_of(188), rows_of(188), stepped(8), stepped(8), stepped(1), stepped(1)],
         [dma((4, 3))],
         specs=[SMEM, SMEM] + [ANY] * 4,
         limit=1,
     )
     guess_v, source_v, start_v, conduct_v = (x.reshape(-1, 128) for x in (guess_v, source_v, start_v, conduct_v))
-    far_in = along(far, "space", off_chip)
     (send0,) = call(last_step_pack, (guess_v, source_v), [rows_of(128)], limit=1)
     t0 = along(send0, "tm", ahead)
+    far_in = along(far, "space", off_chip)
     near_in = along(near, "space", on_chip)
-    far_late_in = along(far_late, "space", off_chip)
-    near_late_in = along(near_late, "space", on_chip)
-    g, s, co, u, rs, e0, e1 = call(
+    g, s, co, u, rs, e0, e1, send2 = call(
         interior,
         (is_first, guess_v, source_v, start_v, conduct_v),
-        [ext(8), ext(8), ext(9), ext(8), ext(4), ext(4), ext(4)],
+        [ext(8), ext(8), ext(9), ext(8), ext(4), ext(4), ext(4), rows_of(108)],
         [vmem(8)],
         specs=[SMEM] + [FULL] * 4,
         limit=6,
     )
-    g, s, co, u, rs, e0, e1, send2 = call(
+    t2 = along(send2, "tm", ahead)
+    near, far = call(relay, (is_odd, t0), [rows_of(19), rows_of(19)], specs=[SMEM, FULL], limit=1)
+    far_relayed = along(far, "space", off_chip)
+    near_relayed = along(near, "space", on_chip)
+    g, s, co, u, rs, e0, e1, send2e = call(
         edges,
         (is_odd, near_in, far_in, g, s, co, u, rs, e0, e1),
-        [ext(8), ext(8), ext(9), ext(8), ext(4), ext(4), ext(4), rows_of(148)],
+        [ext(8), ext(8), ext(9), ext(8), ext(4), ext(4), ext(4), rows_of(40)],
         [vmem(8)],
         aliases={n + 3: n for n in range(7)},
         specs=[SMEM] + [FULL] * 9,
         limit=6,
     )
-    t2 = along(send2, "tm", ahead)
-    near, far = call(relay, (is_odd, t0), [rows_of(19), rows_of(19)], specs=[SMEM, FULL], limit=1)
-    far_in = along(far, "space", off_chip)
-    near_in = along(near, "space", on_chip)
-    g, s, co, u, rs, e0, e1, e2, send3 = call(
+    t2e = along(send2e, "tm", ahead)
+    u, rs, e0, e1, e2, send3 = call(
         rest,
-        (is_odd, near_late_in, far_late_in, g, s, co, u, rs, e0, e1),
-        [ext(8), ext(8), ext(9), ext(8), ext(4), ext(4), ext(4), ext(4), rows_of(70)],
-        [vmem(8)],
-        aliases={n + 3: n for n in range(7)},
-        specs=[SMEM] + [FULL] * 9,
+        (g, s, co, u, rs, e0, e1),
+        [ext(8), ext(4), ext(4), ext(4), ext(4), rows_of(70)],
+        [vmem(4)],
+        aliases={n + 3: n for n in range(4)},
         limit=6,
     )
     t3 = along(send3, "tm", ahead)
     u, rs, e0, e1, e2, before, sol7, send4 = call(
         middle,
-        (is_odd, t0, near_in, far_in, g, s, co, u, rs, e0, e1, e2),
+        (is_odd, t0, near_relayed, far_relayed, g, s, co, u, rs, e0, e1, e2),
         [ext(8), ext(4), ext(4), ext(4), ext(4), rows_of(EXT), ext(1), one],
         [vmem(1), vmem(1), vmem(1), vmem(4), vmem(2)],
         aliases={n + 7: n for n in range(5)},
@@ -599,7 +578,7 @@
     nat3 = lambda steps: pltpu.VMEM((steps, ROWS * 8, 128), F32)
     sol, res, u2, sol2 = call(
         late,
-        (t2, s, co, u, rs, e0, e1, e2, sol7),
+        (t2, t2e, s, co, u, rs, e0, e1, e2, sol7),
         [stepped(8), stepped(8), ext(2), ext(1)],
         [vmem(2), vmem(8), vmem(8), vmem(8), nat3(6), nat3(5), dma((3,))],
         out_specs=[ANY, ANY, FULL, FULL],

time: 50 us -> 58.6 us (1.17)
  the two profiles are of different devices: /device:TPU:64 before, /device:TPU:102 now
where the time goes in v8:
time: 58.6 us; the launch traced here: 58.3 us
  waiting for transfers between devices  22.9 us (39%)
  Pallas kernels  20 us (34%)
  starting transfers between devices  14.4 us (25%)
  between operations  0.98 us (2%)
    ppermute x9, waiting for transfers between devices, along(): lax.ppermute(block, axis, [(i, j) for i, j in pairs if 0 <= j < count])  22.9 us
    pallas_call x10, Pallas kernels, call(): pl.pallas_call(kernel, out_shape=outs, in_specs=specs or [FULL] * len(ins...  20 us
    ppermute x9, starting transfers between devices, along(): lax.ppermute(block, axis, [(i, j) for i, j in pairs if 0 <= j < count])  14.4 us
  transfers between devices with their start and end apart: 9, of which 3 were waited for; matrix products, arithmetic and copies ran while one was open for 0% of the time, Pallas kernels for 29%

profile of v8, /device:TPU:102, one launch (start us, length us, event | category | flops | bytes accessed | tf_op | source)
XLA Modules:
  0.0 58.3 jit_solution(3232246251801480098)
XLA Ops:
  0.6 2.4 %shard_map.59 = (f32[188,8,128]{2,1,0:T(8,128)S(1)}, f32[188,8,128]{2,1,0:T(8,128)S(1)}, f32[8,512,128]{2,1,0:T(8,128)S(1)}, f32[8,512,128]{2,1,0:T(8,128)S(1)},...) custom-call(f32[1]{0:T(128)} %bitcast.1.is_first, s32[1]{0:T(128)} %bitcast.is_odd, f32[8,512,128]{2,1,0:T(8,128)} %bitcast.43, ...), custom_call_target="tpu_custom_call" | custom-call | tf_op jit(solution)/shard_map/pallas_call | solution.py:484
  3.0 0.1 collective-permute-start
  3.1 4.9 %collective-permute-start.1 = (f32[188,8,128]{2,1,0:T(8,128)S(1)}, f32[188,8,128]{2,1,0:T(8,128)S(1)}, u32[]{:S(2)}, u32[]{:S(2)}) collective-permute-start(f32[188,8,128]{2,1,0:T(8,128)S(1)} %get-tuple-element.48), channel_id=1, source_target_pairs={{1,2},{2,1},{3,4},{4,3},{5,6},{6,5},{7,8},{8,7},{9,10},{10,9},{11,... | collective-permute-start | bytes 2310152 | tf_op jit(solution)/shard_map/ppermute | solution.py:498
  8.0 0.1 shard_map.63
  8.1 1.3 %collective-permute-start.3 = (f32[128,8,128]{2,1,0:T(8,128)S(1)}, f32[128,8,128]{2,1,0:T(8,128)S(1)}, u32[]{:S(2)}, u32[]{:S(2)}) collective-permute-start(f32[128,8,128]{2,1,0:T(8,128)S(1)} %shard_map.63), channel_id=1, source_target_pairs={{0,32},{32,64},{64,96},{1,33},{33,65},{65,97},{2,34},{34,66},{66,9... | collective-permute-start | bytes 1572872 | tf_op jit(solution)/shard_map/ppermute | solution.py:498
  9.4 3.7 %shard_map.60 = (f32[8,86,8,128]{3,2,1,0:T(8,128)S(1)}, f32[8,86,8,128]{3,2,1,0:T(8,128)S(1)}, f32[9,86,8,128]{3,2,1,0:T(8,128)S(1)}, f32[8,86,8,128]{3,2,1,0:T(...) custom-call(f32[1]{0:T(128)} %bitcast.1.is_first, ...), custom_call_target="tpu_custom_call" | custom-call | tf_op jit(solution)/shard_map/pallas_call | solution.py:484
  13.1 1.3 %collective-permute-start.6 = (f32[108,8,128]{2,1,0:T(8,128)S(1)}, f32[108,8,128]{2,1,0:T(8,128)S(1)}, u32[]{:S(2)}, u32[]{:S(2)}) collective-permute-start(f32[108,8,128]{2,1,0:T(8,128)S(1)} %get-tuple-element.76), channel_id=1, source_target_pairs={{0,32},{32,64},{64,96},{1,33},{33,65},{65,97},{2,34},{34,66},{66,9... | collective-permute-start | bytes 1327112 | tf_op jit(solution)/shard_map/ppermute | solution.py:498
  14.4 10.4 %collective-permute-done.3.t0 = f32[128,8,128]{2,1,0:T(8,128)S(1)} collective-permute-done((f32[128,8,128]{2,1,0:T(8,128)S(1)}, f32[128,8,128]{2,1,0:T(8,128)S(1)}, u32[]{:S(2)}, u32[]{:S(2)}) %collective-permute-start.3) | collective-permute-done | bytes 524320 | tf_op jit(solution)/shard_map/ppermute | solution.py:498
  24.8 0.1 collective-permute-start.4
  24.9 2.7 %collective-permute-start.5 = (f32[19,8,128]{2,1,0:T(8,128)S(1)}, f32[19,8,128]{2,1,0:T(8,128)S(1)}, u32[]{:S(2)}, u32[]{:S(2)}) collective-permute-start(f32[19,8,128]{2,1,0:T(8,128)S(1)} %get-tuple-element.69), channel_id=1, source_target_pairs={{1,2},{2,1},{3,4},{4,3},{5,6},{6,5},{7,8},{8,7},{9,10},{10,9},{11,... | collective-permute-start | bytes 233480 | tf_op jit(solution)/shard_map/ppermute | solution.py:498
  27.7 0.0 collective-permute-done.near
  27.7 0.0 collective-permute-done.1.far
  27.7 1.2 %shard_map.61 = (f32[8,86,8,128]{3,2,1,0:T(8,128)S(1)}, f32[8,86,8,128]{3,2,1,0:T(8,128)S(1)}, f32[9,86,8,128]{3,2,1,0:T(8,128)S(1)}, f32[8,86,8,128]{3,2,1,0:T(...) custom-call(s32[1]{0:T(128)} %bitcast.is_odd, ...), custom_call_target="tpu_custom_call", output_to_operand_aliasing={{0}: (3, {}), {1}: (4, {}), {2}: (5, {}), {3}: (6, {}), {4}... | custom-call | tf_op jit(solution)/shard_map/pallas_call | solution.py:484
  28.9 2.3 %shard_map.62 = (f32[8,86,8,128]{3,2,1,0:T(8,128)S(1)}, f32[4,86,8,128]{3,2,1,0:T(8,128)S(1)}, f32[4,86,8,128]{3,2,1,0:T(8,128)S(1)}, f32[4,86,8,128]{3,2,1,0:T(...) custom-call(f32[8,86,8,128]{3,2,1,0:T(8,128)S(1)} %get-tuple-element, ...), custom_call_target="tpu_custom_call", output_to_operand_aliasing={{0}: (3, {}), {1}: (4, {}), {2}: (5, {}), {3}: (6, {})} | custom-call | tf_op jit(solution)/shard_map/pallas_call | solution.py:484
  31.2 1.3 %collective-permute-start.2 = (f32[70,8,128]{2,1,0:T(8,128)S(1)}, f32[70,8,128]{2,1,0:T(8,128)S(1)}, u32[]{:S(2)}, u32[]{:S(2)}) collective-permute-start(f32[70,8,128]{2,1,0:T(8,128)S(1)} %get-tuple-element.67), channel_id=1, source_target_pairs={{0,32},{32,64},{64,96},{1,33},{33,65},{65,97},{2,34},{34,66},{66,9... | collective-permute-start | bytes 860168 | tf_op jit(solution)/shard_map/ppermute | solution.py:498
  32.5 0.0 collective-permute-done.4.near
  32.5 0.3 collective-permute-done.5.far
  32.8 2.8 %shard_map.65 = (f32[8,86,8,128]{3,2,1,0:T(8,128)S(1)}, f32[4,86,8,128]{3,2,1,0:T(8,128)S(1)}, f32[4,86,8,128]{3,2,1,0:T(8,128)S(1)}, f32[4,86,8,128]{3,2,1,0:T(...) custom-call(s32[1]{0:T(128)} %bitcast.is_odd, ...), custom_call_target="tpu_custom_call", output_to_operand_aliasing={{0}: (7, {}), {1}: (8, {}), {2}: (9, {}), {3}: (10, {}), {4... | custom-call | tf_op jit(solution)/shard_map/pallas_call | solution.py:484
  35.6 1.3 %collective-permute-start.8 = (f32[512,128]{1,0:T(8,128)S(1)}, f32[512,128]{1,0:T(8,128)S(1)}, u32[]{:S(2)}, u32[]{:S(2)}) collective-permute-start(f32[512,128]{1,0:T(8,128)S(1)} %get-tuple-element.89), channel_id=1, source_target_pairs={{0,32},{32,64},{64,96},{1,33},{33,65},{65,97},{2,34},{34,66},{66,9... | collective-permute-start | bytes 786440 | tf_op jit(solution)/shard_map/ppermute | solution.py:498
  36.9 1.5 %collective-permute-start.7 = (f32[40,8,128]{2,1,0:T(8,128)S(1)}, f32[40,8,128]{2,1,0:T(8,128)S(1)}, u32[]{:S(2)}, u32[]{:S(2)}) collective-permute-start(f32[40,8,128]{2,1,0:T(8,128)S(1)} %get-tuple-element.77), channel_id=1, source_target_pairs={{0,32},{32,64},{64,96},{1,33},{33,65},{65,97},{2,34},{34,66},{66,9... | collective-permute-start | bytes 491528 | tf_op jit(solution)/shard_map/ppermute | solution.py:498
  38.3 0.0 collective-permute-done.6.t2
  38.4 12.2 %collective-permute-done.7.t2e = f32[40,8,128]{2,1,0:T(8,128)S(1)} collective-permute-done((f32[40,8,128]{2,1,0:T(8,128)S(1)}, f32[40,8,128]{2,1,0:T(8,128)S(1)}, u32[]{:S(2)}, u32[]{:S(2)}) %collective-permute-start.7) | collective-permute-done | bytes 163872 | tf_op jit(solution)/shard_map/ppermute | solution.py:498
  50.6 4.7 %shard_map.66 = (f32[8,512,128]{2,1,0:T(8,128)}, f32[8,512,128]{2,1,0:T(8,128)}, f32[2,86,8,128]{3,2,1,0:T(8,128)S(1)}, f32[1,86,8,128]{3,2,1,0:T(8,128)S(1)}) custom-call(f32[108,8,128]{2,1,0:T(8,128)S(1)} %collective-permute-done.6.t2, f32[40,8,128]{2,1,0:T(8,128)S(1)} %collective-permute-done.7.t2e, f32[8,86,8,128]{3,2,1,0:T(8,128)S(1)} %get-tuple-element.61.s, ...), custom_call_target="tpu_custom_call" | custom-call | tf_op jit(solution)/shard_map/pallas_call | solution.py:484
  55.4 0.0 collective-permute-done.2.t3
  55.4 2.0 %shard_map.67 = (f32[8,512,128]{2,1,0:T(8,128)}, f32[8,512,128]{2,1,0:T(8,128)}, f32[512,128]{1,0:T(8,128)S(1)}) custom-call(f32[70,8,128]{2,1,0:T(8,128)S(1)} %collective-permute-done.2.t3, f32[8,86,8,128]{3,2,1,0:T(8,128)S(1)} %get-tuple-element.61.s, f32[9,86,8,128]{3,2,1,0:T(8,128)S(1)} %get-tuple-element.62.co, ...), custom_call_target="tpu_custom_call", output_to_operand_aliasing={{0}: (6, {}), {1}: (7, {})} | custom-call | tf_op jit(solution)/shard_map/pallas_call | solution.py:484
  57.4 0.0 collective-permute-done.8.t4
  57.4 0.7 %shard_map.68 = f32[8,512,128]{2,1,0:T(8,128)} custom-call(f32[512,128]{1,0:T(8,128)S(1)} %collective-permute-done.8.t4, f32[512,128]{1,0:T(8,128)S(1)} %get-tuple-element.90.base, f32[8,512,128]{2,1,0:T(8,128)} %get-tuple-element.91.res_in), custom_call_target="tpu_custom_call", output_to_operand_aliasing={{}: (2, {})} | custom-call | tf_op jit(solution)/shard_map/pallas_call | solution.py:484
  (1 shorter events, 0.0 us)
Async XLA Ops:
  3.0 24.6 %collective-permute-start = (f32[188,8,128]{2,1,0:T(8,128)S(1)}, f32[188,8,128]{2,1,0:T(8,128)S(1)}, u32[]{:S(2)}, u32[]{:S(2)}) collective-permute-start(f32[188,8,128]{2,1,0:T(8,128)S(1)} %get-tuple-element.47), channel_id=1, source_target_pairs={{0,1},{1,0},{2,3},{3,2},{4,5},{5,4},{6,7},{7,6},{8,9},{9,8},{10,11... | collective-permute-start | bytes 2310152 | tf_op jit(solution)/shard_map/ppermute | solution.py:498
  3.1 24.6 %collective-permute-start.1 = (f32[188,8,128]{2,1,0:T(8,128)S(1)}, f32[188,8,128]{2,1,0:T(8,128)S(1)}, u32[]{:S(2)}, u32[]{:S(2)}) collective-permute-start(f32[188,8,128]{2,1,0:T(8,128)S(1)} %get-tuple-element.48), channel_id=1, source_target_pairs={{1,2},{2,1},{3,4},{4,3},{5,6},{6,5},{7,8},{8,7},{9,10},{10,9},{11,... | collective-permute-start | bytes 2310152 | tf_op jit(solution)/shard_map/ppermute | solution.py:498
  8.1 16.7 %collective-permute-start.3 = (f32[128,8,128]{2,1,0:T(8,128)S(1)}, f32[128,8,128]{2,1,0:T(8,128)S(1)}, u32[]{:S(2)}, u32[]{:S(2)}) collective-permute-start(f32[128,8,128]{2,1,0:T(8,128)S(1)} %shard_map.63), channel_id=1, source_target_pairs={{0,32},{32,64},{64,96},{1,33},{33,65},{65,97},{2,34},{34,66},{66,9... | collective-permute-start | bytes 1572872 | tf_op jit(solution)/shard_map/ppermute | solution.py:498
  13.1 25.2 %collective-permute-start.6 = (f32[108,8,128]{2,1,0:T(8,128)S(1)}, f32[108,8,128]{2,1,0:T(8,128)S(1)}, u32[]{:S(2)}, u32[]{:S(2)}) collective-permute-start(f32[108,8,128]{2,1,0:T(8,128)S(1)} %get-tuple-element.76), channel_id=1, source_target_pairs={{0,32},{32,64},{64,96},{1,33},{33,65},{65,97},{2,34},{34,66},{66,9... | collective-permute-start | bytes 1327112 | tf_op jit(solution)/shard_map/ppermute | solution.py:498
  24.8 7.6 %collective-permute-start.4 = (f32[19,8,128]{2,1,0:T(8,128)S(1)}, f32[19,8,128]{2,1,0:T(8,128)S(1)}, u32[]{:S(2)}, u32[]{:S(2)}) collective-permute-start(f32[19,8,128]{2,1,0:T(8,128)S(1)} %get-tuple-element.68), channel_id=1, source_target_pairs={{0,1},{1,0},{2,3},{3,2},{4,5},{5,4},{6,7},{7,6},{8,9},{9,8},{10,11... | collective-permute-start | bytes 233480 | tf_op jit(solution)/shard_map/ppermute | solution.py:498
  24.9 7.8 %collective-permute-start.5 = (f32[19,8,128]{2,1,0:T(8,128)S(1)}, f32[19,8,128]{2,1,0:T(8,128)S(1)}, u32[]{:S(2)}, u32[]{:S(2)}) collective-permute-start(f32[19,8,128]{2,1,0:T(8,128)S(1)} %get-tuple-element.69), channel_id=1, source_target_pairs={{1,2},{2,1},{3,4},{4,3},{5,6},{6,5},{7,8},{8,7},{9,10},{10,9},{11,... | collective-permute-start | bytes 233480 | tf_op jit(solution)/shard_map/ppermute | solution.py:498
  31.2 24.2 %collective-permute-start.2 = (f32[70,8,128]{2,1,0:T(8,128)S(1)}, f32[70,8,128]{2,1,0:T(8,128)S(1)}, u32[]{:S(2)}, u32[]{:S(2)}) collective-permute-start(f32[70,8,128]{2,1,0:T(8,128)S(1)} %get-tuple-element.67), channel_id=1, source_target_pairs={{0,32},{32,64},{64,96},{1,33},{33,65},{65,97},{2,34},{34,66},{66,9... | collective-permute-start | bytes 860168 | tf_op jit(solution)/shard_map/ppermute | solution.py:498
  35.6 21.8 %collective-permute-start.8 = (f32[512,128]{1,0:T(8,128)S(1)}, f32[512,128]{1,0:T(8,128)S(1)}, u32[]{:S(2)}, u32[]{:S(2)}) collective-permute-start(f32[512,128]{1,0:T(8,128)S(1)} %get-tuple-element.89), channel_id=1, source_target_pairs={{0,32},{32,64},{64,96},{1,33},{33,65},{65,97},{2,34},{34,66},{66,9... | collective-permute-start | bytes 786440 | tf_op jit(solution)/shard_map/ppermute | solution.py:498
  36.9 13.7 %collective-permute-start.7 = (f32[40,8,128]{2,1,0:T(8,128)S(1)}, f32[40,8,128]{2,1,0:T(8,128)S(1)}, u32[]{:S(2)}, u32[]{:S(2)}) collective-permute-start(f32[40,8,128]{2,1,0:T(8,128)S(1)} %get-tuple-element.77), channel_id=1, source_target_pairs={{0,32},{32,64},{64,96},{1,33},{33,65},{65,97},{2,34},{34,66},{66,9... | collective-permute-start | bytes 491528 | tf_op jit(solution)/shard_map/ppermute | solution.py:498

commit v9 on v8

--- a/solution.py
+++ b/solution.py
@@ -212,9 +212,9 @@
     sweep(ROWS - inner, ROWS + depth, 99, body)
 
 
-def scaled(co, rs, tmp):
+def scaled(co, rs, tmp, pairs=(2, 3)):
     def body(r):
-        for m in (2, 3):
+        for m in pairs:
             tmp[m, r] = rs[m, r] * co[KINV, r]
 
     return body
@@ -248,14 +248,24 @@
         out[30 + j] = e1[3, HALO + 58 + j]
 
 
+def rest_inner(g, s, co, u_in, rs_in, e0_in, u, rs, e0, tmp):
+    del u_in, rs_in, e0_in
+    st = Stages(beside_maker(), co)
+    sweep(1, 63, 90, st.fine_defect(tmp, g, lambda t, r: g[t - 1, r], s, (1, 2)))
+    sweep(2, 62, 90, st.smoothed(u, g, tmp, (1, 2), Q))
+    sweep(3, 61, 90, st.restricted(rs, tmp, u, lambda t, r: u[t - 1, r], s, (1,)))
+    sweep(4, 60, 90, st.smoothed(e0, None, tmp, (1,), KQ))
+
+
 def rest(g, s, co, u_in, rs_in, e0_in, e1_in, u, rs, e0, e1, e2, send, tmp):
     del u_in, rs_in, e0_in, e1_in
     beside = beside_maker()
     st = Stages(beside, co)
-    sweep(-10, 74, 90, st.fine_defect(tmp, g, lambda t, r: g[t - 1, r], s, (1, 2)))
-    sweep(-9, 73, 90, st.smoothed(u, g, tmp, (1, 2), Q))
-    sweep(-8, 72, 90, st.restricted(rs, tmp, u, lambda t, r: u[t - 1, r], s, (1,)))
-    sweep(-7, 71, 90, st.smoothed(e0, None, tmp, (1,), KQ))
+    both(3, 10, st.fine_defect(tmp, g, lambda t, r: g[t - 1, r], s, (1, 2)))
+    both(2, 9, st.smoothed(u, g, tmp, (1, 2), Q))
+    both(3, 8, st.restricted(rs, tmp, u, lambda t, r: u[t - 1, r], s, (1,)))
+    both(5, -3, scaled(co, rs, tmp, (1,)))
+    both(4, 7, st.smoothed(e0, None, tmp, (1,), KQ))
     sweep(-6, 70, 90, st.coarse_defect(tmp, e0, lambda m, r: e0[m - 1, r], rs, (2,)))
     sweep(-5, 69, 90, st.smoothed(e1, e0, tmp, (2,), KQ))
     sweep(-4, 68, 90, st.coarse_defect(tmp, e1, lambda m, r: e1[m - 1, r], rs, (3,)))
@@ -543,6 +553,9 @@
         limit=6,
     )
     t2 = along(send2, "tm", ahead)
+    u, rs, e0 = call(
+        rest_inner, (g, s, co, u, rs, e0), [ext(8), ext(4), ext(4)], [vmem(4)], aliases={3: 0, 4: 1, 5: 2}, limit=3
+    )
     near, far = call(relay, (is_odd, t0), [rows_of(19), rows_of(19)], specs=[SMEM, FULL], limit=1)
     far_relayed = along(far, "space", off_chip)
     near_relayed = along(near, "space", on_chip)

time: 58.6 us -> 58.6 us (level)
  the two profiles are of different devices: /device:TPU:102 before, /device:TPU:98 now
where the time goes in v9:
time: 58.6 us; the launch traced here: 58.4 us
  starting transfers between devices  22.9 us (39%)
  Pallas kernels  20.1 us (34%)
  waiting for transfers between devices  14.4 us (25%)
  between operations  0.99 us (2%)
    ppermute x9, starting transfers between devices, along(): lax.ppermute(block, axis, [(i, j) for i, j in pairs if 0 <= j < count])  22.9 us
    pallas_call x11, Pallas kernels, call(): pl.pallas_call(kernel, out_shape=outs, in_specs=specs or [FULL] * len(ins...  20.1 us
    ppermute x9, waiting for transfers between devices, along(): lax.ppermute(block, axis, [(i, j) for i, j in pairs if 0 <= j < count])  14.4 us
  transfers between devices with their start and end apart: 9, of which 2 were waited for; matrix products, arithmetic and copies ran while one was open for 0% of the time, Pallas kernels for 29%

profile of v9, /device:TPU:98, one launch (start us, length us, event | category | flops | bytes accessed | tf_op | source)
XLA Modules:
  0.0 58.4 jit_solution(6302532233592362864)
XLA Ops:
  0.6 2.4 %shard_map.59 = (f32[188,8,128]{2,1,0:T(8,128)S(1)}, f32[188,8,128]{2,1,0:T(8,128)S(1)}, f32[8,512,128]{2,1,0:T(8,128)S(1)}, f32[8,512,128]{2,1,0:T(8,128)S(1)},...) custom-call(f32[1]{0:T(128)} %bitcast.1.is_first, s32[1]{0:T(128)} %bitcast.is_odd, f32[8,512,128]{2,1,0:T(8,128)} %bitcast.43, ...), custom_call_target="tpu_custom_call" | custom-call | tf_op jit(solution)/shard_map/pallas_call | solution.py:494
  3.0 0.1 collective-permute-start
  3.1 4.9 %collective-permute-start.1 = (f32[188,8,128]{2,1,0:T(8,128)S(1)}, f32[188,8,128]{2,1,0:T(8,128)S(1)}, u32[]{:S(2)}, u32[]{:S(2)}) collective-permute-start(f32[188,8,128]{2,1,0:T(8,128)S(1)} %get-tuple-element.51), channel_id=1, source_target_pairs={{1,2},{2,1},{3,4},{4,3},{5,6},{6,5},{7,8},{8,7},{9,10},{10,9},{11,... | collective-permute-start | bytes 2310152 | tf_op jit(solution)/shard_map/ppermute | solution.py:508
  8.0 0.1 shard_map.64
  8.1 3.4 %collective-permute-start.3 = (f32[128,8,128]{2,1,0:T(8,128)S(1)}, f32[128,8,128]{2,1,0:T(8,128)S(1)}, u32[]{:S(2)}, u32[]{:S(2)}) collective-permute-start(f32[128,8,128]{2,1,0:T(8,128)S(1)} %shard_map.64), channel_id=1, source_target_pairs={{0,32},{32,64},{64,96},{1,33},{33,65},{65,97},{2,34},{34,66},{66,9... | collective-permute-start | bytes 1572872 | tf_op jit(solution)/shard_map/ppermute | solution.py:508
  11.6 3.7 %shard_map.60 = (f32[8,86,8,128]{3,2,1,0:T(8,128)S(1)}, f32[8,86,8,128]{3,2,1,0:T(8,128)S(1)}, f32[9,86,8,128]{3,2,1,0:T(8,128)S(1)}, f32[8,86,8,128]{3,2,1,0:T(...) custom-call(f32[1]{0:T(128)} %bitcast.1.is_first, ...), custom_call_target="tpu_custom_call" | custom-call | tf_op jit(solution)/shard_map/pallas_call | solution.py:494
  15.2 3.1 %collective-permute-start.6 = (f32[108,8,128]{2,1,0:T(8,128)S(1)}, f32[108,8,128]{2,1,0:T(8,128)S(1)}, u32[]{:S(2)}, u32[]{:S(2)}) collective-permute-start(f32[108,8,128]{2,1,0:T(8,128)S(1)} %get-tuple-element.82), channel_id=1, source_target_pairs={{0,32},{32,64},{64,96},{1,33},{33,65},{65,97},{2,34},{34,66},{66,9... | collective-permute-start | bytes 1327112 | tf_op jit(solution)/shard_map/ppermute | solution.py:508
  18.4 6.5 %collective-permute-done.3.t0 = f32[128,8,128]{2,1,0:T(8,128)S(1)} collective-permute-done((f32[128,8,128]{2,1,0:T(8,128)S(1)}, f32[128,8,128]{2,1,0:T(8,128)S(1)}, u32[]{:S(2)}, u32[]{:S(2)}) %collective-permute-start.3) | collective-permute-done | bytes 524320 | tf_op jit(solution)/shard_map/ppermute | solution.py:508
  24.8 0.1 collective-permute-start.4
  24.9 2.7 %collective-permute-start.5 = (f32[19,8,128]{2,1,0:T(8,128)S(1)}, f32[19,8,128]{2,1,0:T(8,128)S(1)}, u32[]{:S(2)}, u32[]{:S(2)}) collective-permute-start(f32[19,8,128]{2,1,0:T(8,128)S(1)} %get-tuple-element.75), channel_id=1, source_target_pairs={{1,2},{2,1},{3,4},{4,3},{5,6},{6,5},{7,8},{8,7},{9,10},{10,9},{11,... | collective-permute-start | bytes 233480 | tf_op jit(solution)/shard_map/ppermute | solution.py:508
  27.7 1.1 %shard_map.61 = (f32[8,86,8,128]{3,2,1,0:T(8,128)S(1)}, f32[4,86,8,128]{3,2,1,0:T(8,128)S(1)}, f32[4,86,8,128]{3,2,1,0:T(8,128)S(1)}) custom-call(f32[8,86,8,128]{3,2,1,0:T(8,128)S(1)} %get-tuple-element.56.g.g_in, f32[8,86,8,128]{3,2,1,0:T(8,128)S(1)} %get-tuple-element.57.s.s_in, ...), custom_call_target="tpu_custom_call", output_to_operand_aliasing={{0}: (3, {}), {1}: (4, {}), {2}: (5, {})} | custom-call | tf_op jit(solution)/shard_map/pallas_call | solution.py:494
  28.8 0.0 collective-permute-done.near
  28.8 0.0 collective-permute-done.1.far
  28.8 1.2 %shard_map.62 = (f32[8,86,8,128]{3,2,1,0:T(8,128)S(1)}, f32[8,86,8,128]{3,2,1,0:T(8,128)S(1)}, f32[9,86,8,128]{3,2,1,0:T(8,128)S(1)}, f32[8,86,8,128]{3,2,1,0:T(...) custom-call(s32[1]{0:T(128)} %bitcast.is_odd, ...), custom_call_target="tpu_custom_call", output_to_operand_aliasing={{0}: (3, {}), {1}: (4, {}), {2}: (5, {}), {3}: (6, {}), {4}... | custom-call | tf_op jit(solution)/shard_map/pallas_call | solution.py:494
  30.0 1.2 %shard_map.63 = (f32[8,86,8,128]{3,2,1,0:T(8,128)S(1)}, f32[4,86,8,128]{3,2,1,0:T(8,128)S(1)}, f32[4,86,8,128]{3,2,1,0:T(8,128)S(1)}, f32[4,86,8,128]{3,2,1,0:T(...) custom-call(f32[8,86,8,128]{3,2,1,0:T(8,128)S(1)} %get-tuple-element, ...), custom_call_target="tpu_custom_call", output_to_operand_aliasing={{0}: (3, {}), {1}: (4, {}), {2}: (5, {}), {3}: (6, {})} | custom-call | tf_op jit(solution)/shard_map/pallas_call | solution.py:494
  31.2 3.4 %collective-permute-start.2 = (f32[70,8,128]{2,1,0:T(8,128)S(1)}, f32[70,8,128]{2,1,0:T(8,128)S(1)}, u32[]{:S(2)}, u32[]{:S(2)}) collective-permute-start(f32[70,8,128]{2,1,0:T(8,128)S(1)} %get-tuple-element.73), channel_id=1, source_target_pairs={{0,32},{32,64},{64,96},{1,33},{33,65},{65,97},{2,34},{34,66},{66,9... | collective-permute-start | bytes 860168 | tf_op jit(solution)/shard_map/ppermute | solution.py:508
  34.6 0.0 collective-permute-done.4.near
  34.7 0.0 collective-permute-done.5.far
  34.7 2.8 %shard_map.66 = (f32[8,86,8,128]{3,2,1,0:T(8,128)S(1)}, f32[4,86,8,128]{3,2,1,0:T(8,128)S(1)}, f32[4,86,8,128]{3,2,1,0:T(8,128)S(1)}, f32[4,86,8,128]{3,2,1,0:T(...) custom-call(s32[1]{0:T(128)} %bitcast.is_odd, ...), custom_call_target="tpu_custom_call", output_to_operand_aliasing={{0}: (7, {}), {1}: (8, {}), {2}: (9, {}), {3}: (10, {}), {4... | custom-call | tf_op jit(solution)/shard_map/pallas_call | solution.py:494
  37.5 3.1 %collective-permute-start.8 = (f32[512,128]{1,0:T(8,128)S(1)}, f32[512,128]{1,0:T(8,128)S(1)}, u32[]{:S(2)}, u32[]{:S(2)}) collective-permute-start(f32[512,128]{1,0:T(8,128)S(1)} %get-tuple-element.95), channel_id=1, source_target_pairs={{0,32},{32,64},{64,96},{1,33},{33,65},{65,97},{2,34},{34,66},{66,9... | collective-permute-start | bytes 786440 | tf_op jit(solution)/shard_map/ppermute | solution.py:508
  40.6 2.1 %collective-permute-start.7 = (f32[40,8,128]{2,1,0:T(8,128)S(1)}, f32[40,8,128]{2,1,0:T(8,128)S(1)}, u32[]{:S(2)}, u32[]{:S(2)}) collective-permute-start(f32[40,8,128]{2,1,0:T(8,128)S(1)} %get-tuple-element.83), channel_id=1, source_target_pairs={{0,32},{32,64},{64,96},{1,33},{33,65},{65,97},{2,34},{34,66},{66,9... | collective-permute-start | bytes 491528 | tf_op jit(solution)/shard_map/ppermute | solution.py:508
  42.7 0.0 collective-permute-done.6.t2
  42.7 7.9 %collective-permute-done.7.t2e = f32[40,8,128]{2,1,0:T(8,128)S(1)} collective-permute-done((f32[40,8,128]{2,1,0:T(8,128)S(1)}, f32[40,8,128]{2,1,0:T(8,128)S(1)}, u32[]{:S(2)}, u32[]{:S(2)}) %collective-permute-start.7) | collective-permute-done | bytes 163872 | tf_op jit(solution)/shard_map/ppermute | solution.py:508
  50.7 4.8 %shard_map.67 = (f32[8,512,128]{2,1,0:T(8,128)}, f32[8,512,128]{2,1,0:T(8,128)}, f32[2,86,8,128]{3,2,1,0:T(8,128)S(1)}, f32[1,86,8,128]{3,2,1,0:T(8,128)S(1)}) custom-call(f32[108,8,128]{2,1,0:T(8,128)S(1)} %collective-permute-done.6.t2, f32[40,8,128]{2,1,0:T(8,128)S(1)} %collective-permute-done.7.t2e, f32[8,86,8,128]{3,2,1,0:T(8,128)S(1)} %get-tuple-element.67.s, ...), custom_call_target="tpu_custom_call" | custom-call | tf_op jit(solution)/shard_map/pallas_call | solution.py:494
  55.4 0.0 collective-permute-done.2.t3
  55.5 2.0 %shard_map.68 = (f32[8,512,128]{2,1,0:T(8,128)}, f32[8,512,128]{2,1,0:T(8,128)}, f32[512,128]{1,0:T(8,128)S(1)}) custom-call(f32[70,8,128]{2,1,0:T(8,128)S(1)} %collective-permute-done.2.t3, f32[8,86,8,128]{3,2,1,0:T(8,128)S(1)} %get-tuple-element.67.s, f32[9,86,8,128]{3,2,1,0:T(8,128)S(1)} %get-tuple-element.68.co, ...), custom_call_target="tpu_custom_call", output_to_operand_aliasing={{0}: (6, {}), {1}: (7, {})} | custom-call | tf_op jit(solution)/shard_map/pallas_call | solution.py:494
  57.4 0.0 collective-permute-done.8.t4
  57.5 0.7 %shard_map.69 = f32[8,512,128]{2,1,0:T(8,128)} custom-call(f32[512,128]{1,0:T(8,128)S(1)} %collective-permute-done.8.t4, f32[512,128]{1,0:T(8,128)S(1)} %get-tuple-element.96.base, f32[8,512,128]{2,1,0:T(8,128)} %get-tuple-element.97.res_in), custom_call_target="tpu_custom_call", output_to_operand_aliasing={{}: (2, {})} | custom-call | tf_op jit(solution)/shard_map/pallas_call | solution.py:494
  (1 shorter events, 0.0 us)
Async XLA Ops:
  3.0 25.8 %collective-permute-start = (f32[188,8,128]{2,1,0:T(8,128)S(1)}, f32[188,8,128]{2,1,0:T(8,128)S(1)}, u32[]{:S(2)}, u32[]{:S(2)}) collective-permute-start(f32[188,8,128]{2,1,0:T(8,128)S(1)} %get-tuple-element.50), channel_id=1, source_target_pairs={{0,1},{1,0},{2,3},{3,2},{4,5},{5,4},{6,7},{7,6},{8,9},{9,8},{10,11... | collective-permute-start | bytes 2310152 | tf_op jit(solution)/shard_map/ppermute | solution.py:508
  3.1 25.7 %collective-permute-start.1 = (f32[188,8,128]{2,1,0:T(8,128)S(1)}, f32[188,8,128]{2,1,0:T(8,128)S(1)}, u32[]{:S(2)}, u32[]{:S(2)}) collective-permute-start(f32[188,8,128]{2,1,0:T(8,128)S(1)} %get-tuple-element.51), channel_id=1, source_target_pairs={{1,2},{2,1},{3,4},{4,3},{5,6},{6,5},{7,8},{8,7},{9,10},{10,9},{11,... | collective-permute-start | bytes 2310152 | tf_op jit(solution)/shard_map/ppermute | solution.py:508
  8.1 16.7 %collective-permute-start.3 = (f32[128,8,128]{2,1,0:T(8,128)S(1)}, f32[128,8,128]{2,1,0:T(8,128)S(1)}, u32[]{:S(2)}, u32[]{:S(2)}) collective-permute-start(f32[128,8,128]{2,1,0:T(8,128)S(1)} %shard_map.64), channel_id=1, source_target_pairs={{0,32},{32,64},{64,96},{1,33},{33,65},{65,97},{2,34},{34,66},{66,9... | collective-permute-start | bytes 1572872 | tf_op jit(solution)/shard_map/ppermute | solution.py:508
  15.2 27.5 %collective-permute-start.6 = (f32[108,8,128]{2,1,0:T(8,128)S(1)}, f32[108,8,128]{2,1,0:T(8,128)S(1)}, u32[]{:S(2)}, u32[]{:S(2)}) collective-permute-start(f32[108,8,128]{2,1,0:T(8,128)S(1)} %get-tuple-element.82), channel_id=1, source_target_pairs={{0,32},{32,64},{64,96},{1,33},{33,65},{65,97},{2,34},{34,66},{66,9... | collective-permute-start | bytes 1327112 | tf_op jit(solution)/shard_map/ppermute | solution.py:508
  24.8 9.8 %collective-permute-start.4 = (f32[19,8,128]{2,1,0:T(8,128)S(1)}, f32[19,8,128]{2,1,0:T(8,128)S(1)}, u32[]{:S(2)}, u32[]{:S(2)}) collective-permute-start(f32[19,8,128]{2,1,0:T(8,128)S(1)} %get-tuple-element.74), channel_id=1, source_target_pairs={{0,1},{1,0},{2,3},{3,2},{4,5},{5,4},{6,7},{7,6},{8,9},{9,8},{10,11... | collective-permute-start | bytes 233480 | tf_op jit(solution)/shard_map/ppermute | solution.py:508
  24.9 9.7 %collective-permute-start.5 = (f32[19,8,128]{2,1,0:T(8,128)S(1)}, f32[19,8,128]{2,1,0:T(8,128)S(1)}, u32[]{:S(2)}, u32[]{:S(2)}) collective-permute-start(f32[19,8,128]{2,1,0:T(8,128)S(1)} %get-tuple-element.75), channel_id=1, source_target_pairs={{1,2},{2,1},{3,4},{4,3},{5,6},{6,5},{7,8},{8,7},{9,10},{10,9},{11,... | collective-permute-start | bytes 233480 | tf_op jit(solution)/shard_map/ppermute | solution.py:508
  31.2 24.2 %collective-permute-start.2 = (f32[70,8,128]{2,1,0:T(8,128)S(1)}, f32[70,8,128]{2,1,0:T(8,128)S(1)}, u32[]{:S(2)}, u32[]{:S(2)}) collective-permute-start(f32[70,8,128]{2,1,0:T(8,128)S(1)} %get-tuple-element.73), channel_id=1, source_target_pairs={{0,32},{32,64},{64,96},{1,33},{33,65},{65,97},{2,34},{34,66},{66,9... | collective-permute-start | bytes 860168 | tf_op jit(solution)/shard_map/ppermute | solution.py:508
  37.5 20.0 %collective-permute-start.8 = (f32[512,128]{1,0:T(8,128)S(1)}, f32[512,128]{1,0:T(8,128)S(1)}, u32[]{:S(2)}, u32[]{:S(2)}) collective-permute-start(f32[512,128]{1,0:T(8,128)S(1)} %get-tuple-element.95), channel_id=1, source_target_pairs={{0,32},{32,64},{64,96},{1,33},{33,65},{65,97},{2,34},{34,66},{66,9... | collective-permute-start | bytes 786440 | tf_op jit(solution)/shard_map/ppermute | solution.py:508
  40.6 10.1 %collective-permute-start.7 = (f32[40,8,128]{2,1,0:T(8,128)S(1)}, f32[40,8,128]{2,1,0:T(8,128)S(1)}, u32[]{:S(2)}, u32[]{:S(2)}) collective-permute-start(f32[40,8,128]{2,1,0:T(8,128)S(1)} %get-tuple-element.83), channel_id=1, source_target_pairs={{0,32},{32,64},{64,96},{1,33},{33,65},{65,97},{2,34},{34,66},{66,9... | collective-permute-start | bytes 491528 | tf_op jit(solution)/shard_map/ppermute | solution.py:508
